TPU v7x, 16 devices: a whole 2x2x2 slice. The times are simulated.
16 devices in a mesh: fsdp: 2 (over z), ep: 8 (over y, x, core).
Axes of the slice: x: 2, y: 2, z: 2, core: 2. Of those that a mesh axis runs over, the one named last changes fastest.
Arguments:
- x_tok: bfloat16 [32768, 1024], P(('ep', 'fsdp'))
- dy_tok: bfloat16 [32768, 1024], P(('ep', 'fsdp'))
- expert_ids: int32 [32768, 8], P(('ep', 'fsdp'))
- expert_slot: int32 [32768, 8], P(('ep', 'fsdp'))
- w_router: bfloat16 [1024, 32], replicated
- w_gate: bfloat16 [32, 1024, 512], P('ep', 'fsdp')
- w_up: bfloat16 [32, 1024, 512], P('ep', 'fsdp')
- w_down: bfloat16 [32, 512, 1024], P('ep', None, 'fsdp')
Outputs:
- output 1: bfloat16 [32768, 1024], P(('ep', 'fsdp'))
- output 2: float32 [], replicated
- output 3: bfloat16 [32768, 1024], P(('ep', 'fsdp'))
- output 4: float32 [1024, 32], replicated
- output 5: bfloat16 [32, 1024, 512], P('ep', 'fsdp')
- output 6: bfloat16 [32, 1024, 512], P('ep', 'fsdp')
- output 7: bfloat16 [32, 512, 1024], P('ep', None, 'fsdp')
All inputs are finite; a program needn't handle non-finite values.
Results may differ from a plain program's by a relative error of at most 0.0106918.
Values are sent between devices in bfloat16 or wider.
A program may use at most 1 GiB of HBM per device.

v0:
```python
import jax
import jax.numpy as jnp
from jax import lax
from jax.sharding import PartitionSpec as P

AUX_COEF = 0.01


def solution(mesh):
    n_fsdp = mesh.shape['fsdp']
    n_ep = mesh.shape['ep']
    n_dev = n_fsdp * n_ep
    all_axes = ('fsdp', 'ep')
    tok_spec = P(('ep', 'fsdp'), None)
    up_spec = P('ep', 'fsdp', None)
    down_spec = P('ep', None, 'fsdp')

    def local_step(x_loc, dy_loc, ids_loc, slot_loc, w_router, wg_loc, wu_loc, wd_loc):
        tok_dev, d_model = x_loc.shape
        top_k = ids_loc.shape[1]
        experts = w_router.shape[1]
        local_exp = experts // n_ep
        capacity = 5 * tok_dev * top_k // (4 * experts)
        n_slots = experts * capacity
        tokens = tok_dev * n_dev
        logits = jnp.dot(x_loc, w_router, preferred_element_type=jnp.float32)
        prob_all = jax.nn.softmax(logits, axis=-1)
        gate = jnp.take_along_axis(prob_all, ids_loc, axis=1)
        flat_ids = ids_loc.reshape(-1)
        counts = jax.ops.segment_sum(jnp.ones(flat_ids.shape, jnp.float32), flat_ids, num_segments=experts)
        stat_sum = lax.psum(jnp.stack([counts, jnp.sum(prob_all, axis=0)]), all_axes)
        load_frac = stat_sum[0] / (tokens * top_k)
        aux_loss = AUX_COEF * experts * jnp.sum(load_frac * stat_sum[1] / tokens)
        flat_slot = slot_loc.reshape(-1)
        dest_row = jnp.where(flat_slot >= 0, flat_ids * capacity + flat_slot, n_slots)
        pair_ids = jnp.arange(1, tok_dev * top_k + 1, dtype=jnp.int32)
        pair_src = jax.ops.segment_sum(pair_ids, dest_row, num_segments=n_slots)
        filled = pair_src > 0
        pair_pos = jnp.where(filled, pair_src - 1, 0)
        tok_pos = jnp.where(filled, pair_pos // top_k, tok_dev)
        send_buf = jnp.take(x_loc, tok_pos, axis=0, mode='fill', fill_value=0).reshape(n_ep, local_exp, capacity, d_model)
        recv_buf = lax.all_to_all(send_buf, 'ep', 0, 0, tiled=True)
        wg_full = lax.all_gather(wg_loc, 'fsdp', axis=1, tiled=True)
        wu_full = lax.all_gather(wu_loc, 'fsdp', axis=1, tiled=True)
        wd_full = lax.all_gather(wd_loc, 'fsdp', axis=2, tiled=True)
        h_gate = jnp.einsum('slcd,ldf->slcf', recv_buf, wg_full, preferred_element_type=jnp.float32)
        h_up = jnp.einsum('slcd,ldf->slcf', recv_buf, wu_full, preferred_element_type=jnp.float32)
        sig_gate = jax.nn.sigmoid(h_gate)
        act_buf = (h_gate * sig_gate * h_up).astype(jnp.bfloat16)
        out_buf = jnp.einsum('slcf,lfd->slcd', act_buf, wd_full, preferred_element_type=jnp.float32).astype(jnp.bfloat16)
        back_buf = lax.all_to_all(out_buf, 'ep', 0, 0, tiled=True).reshape(n_slots, d_model)
        pair_out = jnp.take(back_buf, dest_row, axis=0, mode='fill', fill_value=0).reshape(tok_dev, top_k, d_model)
        y_loc = jnp.sum(gate[:, :, None] * pair_out, axis=1).astype(jnp.bfloat16)
        d_gate = jnp.einsum('td,tjd->tj', dy_loc, pair_out, preferred_element_type=jnp.float32)
        gate_slot = jnp.where(filled, jnp.take(gate.reshape(-1), pair_pos), 0.0)
        dy_slot = jnp.take(dy_loc, tok_pos, axis=0, mode='fill', fill_value=0)
        d_out = (gate_slot[:, None] * dy_slot).astype(jnp.bfloat16).reshape(n_ep, local_exp, capacity, d_model)
        d_out_recv = lax.all_to_all(d_out, 'ep', 0, 0, tiled=True)
        d_act = jnp.einsum('slcd,lfd->slcf', d_out_recv, wd_full, preferred_element_type=jnp.float32).astype(jnp.bfloat16)
        d_hgate = (d_act * h_up * sig_gate * (1.0 + h_gate * (1.0 - sig_gate))).astype(jnp.bfloat16)
        d_hup = (d_act * h_gate * sig_gate).astype(jnp.bfloat16)
        dwd_part = jnp.einsum('slcf,slcd->lfd', act_buf, d_out_recv, preferred_element_type=jnp.float32)
        dwg_part = jnp.einsum('slcd,slcf->ldf', recv_buf, d_hgate, preferred_element_type=jnp.float32)
        dwu_part = jnp.einsum('slcd,slcf->ldf', recv_buf, d_hup, preferred_element_type=jnp.float32)
        d_in = (jnp.einsum('slcf,ldf->slcd', d_hgate, wg_full, preferred_element_type=jnp.float32)
                + jnp.einsum('slcf,ldf->slcd', d_hup, wu_full, preferred_element_type=jnp.float32)).astype(jnp.bfloat16)
        d_back = lax.all_to_all(d_in, 'ep', 0, 0, tiled=True).reshape(n_slots, d_model)
        pair_dx = jnp.take(d_back, dest_row, axis=0, mode='fill', fill_value=0).reshape(tok_dev, top_k, d_model)
        match = ids_loc[:, :, None] == jnp.arange(experts)[None, None, :]
        d_prob = jnp.sum(jnp.where(match, d_gate[:, :, None], 0.0), axis=1) + AUX_COEF * experts * load_frac[None, :]
        d_logit = prob_all * (d_prob - jnp.sum(prob_all * d_prob, axis=-1, keepdims=True))
        d_logit_b = d_logit.astype(jnp.bfloat16)
        dx_router = lax.dot_general(d_logit_b, w_router, (((1,), (1,)), ((), ())), preferred_element_type=jnp.float32)
        dx_loc = (jnp.sum(pair_dx, axis=1, dtype=jnp.float32) + dx_router).astype(jnp.bfloat16)
        dw_router = lax.psum(lax.dot_general(x_loc, d_logit_b, (((0,), (0,)), ((), ())), preferred_element_type=jnp.float32), all_axes)
        dwg_loc = lax.psum_scatter(dwg_part, 'fsdp', scatter_dimension=1, tiled=True).astype(jnp.bfloat16)
        dwu_loc = lax.psum_scatter(dwu_part, 'fsdp', scatter_dimension=1, tiled=True).astype(jnp.bfloat16)
        dwd_loc = lax.psum_scatter(dwd_part, 'fsdp', scatter_dimension=2, tiled=True).astype(jnp.bfloat16)
        return y_loc, aux_loss, dx_loc, dw_router, dwg_loc, dwu_loc, dwd_loc

    return jax.shard_map(local_step, mesh=mesh,
                         in_specs=(tok_spec, tok_spec, tok_spec, tok_spec, P(), up_spec, up_spec, down_spec),
                         out_specs=(tok_spec, P(), tok_spec, P(), up_spec, up_spec, down_spec),
                         check_vma=False)
```

profile of v0, /device:TPU:0, one launch (start us, length us, event | category | flops | bytes accessed | tf_op | source)
XLA Modules:
  0.0 3041.9 jit_solution(18168570725030691611)
XLA Ops:
  7.2 0.9 add_select_fusion.3
  9.0 85.8 %scatter_custom_fusion = s32[20480]{0:T(1024)S(1)} fusion(s32[16384]{0:T(1024)S(1)} %reshape.178, s32[16384]{0:T(1024)S(1)} %iota_add_fusion, s32[]{:T(128)} %constant.40.clone.1), kind=kCustom, calls=%fused_computation.90 | custom fusion | flops 16384 | bytes 81924 | tf_op jit(solution)/shard_map/scatter-add | solution.py:37
  94.9 0.7 fusion.50
  95.6 102.6 %gather_fusion.2 = bf16[20480,1024]{1,0:T(8,128)(2,1)} fusion(bf16[2048,1024]{1,0:T(8,128)(2,1)} %param.12, s32[20480]{0:T(1024)S(1)} %get-tuple-element.17), kind=kCustom, calls=%fused_computation.clone | custom fusion | bytes 83968000 | tf_op jit(solution)/shard_map/jit(_take)/gather | solution.py:41
  198.3 28.0 broadcast_select_fusion
  226.3 8.0 all-to-all-start
  235.2 3.5 fusion.59
  238.8 0.7 fusion.57
  239.4 130.5 %gather_fusion.1 = f32[16384]{0:T(1024)S(1)} fusion(f32[2048,32]{0,1:T(8,128)S(1)} %get-tuple-element.12, s32[16384]{0:T(1024)S(1)} %reshape.170), kind=kCustom, calls=%fused_computation.5 | custom fusion | bytes 262144 | tf_op jit(solution)/shard_map/jit(take_along_axis)/gather | solution.py:28
  370.0 0.6 reshape.173
  371.3 0.5 select_n.80
  371.8 102.8 %gather_fusion.4 = bf16[20480,1024]{1,0:T(8,128)(2,1)} fusion(bf16[2048,1024]{1,0:T(8,128)(2,1)} %param.13, s32[20480]{0:T(1024)S(1)} %copy-done.11), kind=kCustom, calls=%fused_computation.2.clone | custom fusion | bytes 83968000 | tf_op jit(solution)/shard_map/jit(_take)/gather | solution.py:56
  474.6 113.0 %gather_fusion = f32[20480]{0:T(1024)S(1)} fusion(f32[16384]{0:T(1024)S(1)} %select_n.80, s32[20480]{0:T(1024)S(1)} %copy-done.14), kind=kCustom, calls=%fused_computation.4 | custom fusion | bytes 245760 | tf_op jit(solution)/shard_map/jit(_take)/gather | solution.py:55
  587.7 28.0 multiply_convert_fusion
  615.7 73.4 %all-to-all-done = bf16[8,4,640,1024]{3,2,1,0:T(8,128)(2,1)} async-done(((bf16[8,4,640,1024]{3,2,1,0:T(8,128)(2,1)}), bf16[8,4,640,1024]{3,2,1,0:T(8,128)(2,1)}, u32[]{:S(2)}, u32[]{:S(2)}) %all-to-all-start) | async-done | bytes 41943072 | tf_op jit(solution)/shard_map/all_to_all | solution.py:42
  689.1 7.8 all-to-all-start.2
  697.0 0.7 all-gather.4.cloned.1.call-update
  697.7 0.7 all-gather.8.cloned.1.call-update
  699.2 57.4 %all-gather.4.cloned.1.call-done = bf16[4,1024,512]{2,1,0:T(8,128)(2,1)} async-done(((bf16[4,512,512]{2,1,0:T(8,128)(2,1)}), bf16[4,1024,512]{2,1,0:T(8,128)(2,1)}) %all-gather.4.cloned.1.call-update) | async-done | bytes 4194320 | tf_op jit(solution)/shard_map/all_gather | solution.py:43
  756.6 36.9 %fusion.17 = f32[4,8,640,512]{3,2,1,0:T(8,128)} fusion(bf16[8,4,640,1024]{3,2,1,0:T(8,128)(2,1)} %all-to-all-done, bf16[4,1024,512]{2,1,0:T(8,128)(2,1)} %all-gather.4.cloned.1.call-done), kind=kOutput, calls=%fused_computation.37 | convolution fusion | flops 21474836480 | bytes 88080384 | tf_op jit(solution)/shard_map/slcd,ldf->slcf/dot_general | solution.py:46
  793.5 19.7 all-gather.8.cloned.1.call-done
  813.2 337.6 %all-to-all-done.2 = bf16[8,4,640,1024]{3,2,1,0:T(8,128)(2,1)} async-done(((bf16[8,4,640,1024]{3,2,1,0:T(8,128)(2,1)}), bf16[8,4,640,1024]{3,2,1,0:T(8,128)(2,1)}, u32[]{:S(2)}, u32[]{:S(2)}) %all-to-all-start.2) | async-done | bytes 41943072 | tf_op jit(solution)/shard_map/all_to_all | solution.py:58
  1150.8 30.4 fusion.25
  1181.2 66.0 %fusion.6 = (bf16[8,4,640,512]{3,2,0,1:T(8,128)(2,1)}, bf16[8,4,640,512]{3,2,0,1:T(8,128)(2,1)}, bf16[8,4,640,512]{3,2,0,1:T(8,128)(2,1)}) fusion(f32[4,8,640,512]{3,2,1,0:T(8,128)} %fusion.17, bf16[4,8,640,512]{3,2,1,0:T(8,128)(2,1)} %fusion.25, bf16[4,1024,512]{2,1,0:T(8,128)(2,1)} %all-gather.6.cloned.1.call-done, bf16[8,4,640,1024]{3,2,1,0:T(8,128)(2,1)} %all-to-all-done), kind=kOutput, calls=%fused_computation.21 | convolution fusion | flops 21653094400 | bytes 171966464 | tf_op jit(solution)/shard_map/slcd,ldf->slcf/dot_general | solution.py:47
  1247.2 31.1 %convert_bitcast_fusion = bf16[8,4,640,1024]{3,2,0,1:T(8,128)(2,1)} fusion(bf16[8,4,640,512]{3,2,0,1:T(8,128)(2,1)} %get-tuple-element.13, bf16[4,512,1024]{2,1,0:T(8,128)(2,1)} %all-gather.8.cloned.1.call-done), kind=kOutput, calls=%fused_computation.29 | convolution fusion | flops 21495808000 | bytes 67108864 | tf_op jit(solution)/shard_map/slcf,lfd->slcd/dot_general | solution.py:50
  1278.4 28.2 copy.88
  1306.6 7.8 all-to-all-start.1
  1314.4 31.6 %fusion.42 = f32[4,512,1024]{2,1,0:T(8,128)} fusion(bf16[8,4,640,512]{3,2,0,1:T(8,128)(2,1)} %get-tuple-element.13, bf16[8,4,640,1024]{3,2,1,0:T(8,128)(2,1)} %all-to-all-done.2), kind=kOutput, calls=%fused_computation.58 | convolution fusion | flops 21474836480 | bytes 71303168 | tf_op jit(solution)/shard_map/slcf,slcd->lfd/dot_general | solution.py:62
  1346.1 31.0 %fusion.39 = f32[4,1024,512]{2,1,0:T(8,128)} fusion(bf16[8,4,640,1024]{3,2,1,0:T(8,128)(2,1)} %all-to-all-done, bf16[8,4,640,512]{3,2,0,1:T(8,128)(2,1)} %get-tuple-element.15), kind=kOutput, calls=%fused_computation.57 | convolution fusion | flops 21474836480 | bytes 71303168 | tf_op jit(solution)/shard_map/slcd,slcf->ldf/dot_general | solution.py:64
  1377.1 40.4 %fusion.31 = f32[4,8,640,1024]{3,2,1,0:T(8,128)} fusion(bf16[8,4,640,512]{3,2,0,1:T(8,128)(2,1)} %get-tuple-element.14, bf16[4,1024,512]{2,1,0:T(8,128)(2,1)} %all-gather.4.cloned.1.call-done), kind=kOutput, calls=%fused_computation.51 | convolution fusion | flops 21474836480 | bytes 109051904 | tf_op jit(solution)/shard_map/slcf,ldf->slcd/dot_general | solution.py:65
  1417.5 49.8 %fusion = bf16[8,4,640,1024]{3,2,0,1:T(8,128)(2,1)} fusion(f32[4,8,640,1024]{3,2,1,0:T(8,128)} %fusion.31, bf16[8,4,640,512]{3,2,0,1:T(8,128)(2,1)} %get-tuple-element.15, bf16[4,1024,512]{2,1,0:T(8,128)(2,1)} %all-gather.6.cloned.1.call-done), kind=kOutput, calls=%fused_computation.12 | convolution fusion | flops 21516779520 | bytes 150994944 | tf_op jit(solution)/shard_map/slcf,ldf->slcd/dot_general | solution.py:66
  1467.3 28.4 copy.92
  1495.7 272.6 %all-to-all-done.1 = bf16[8,4,640,1024]{3,2,1,0:T(8,128)(2,1)} async-done(((bf16[8,4,640,1024]{3,2,1,0:T(8,128)(2,1)}), bf16[8,4,640,1024]{3,2,1,0:T(8,128)(2,1)}, u32[]{:S(2)}, u32[]{:S(2)}) %all-to-all-start.1) | async-done | bytes 41943072 | tf_op jit(solution)/shard_map/all_to_all | solution.py:51
  1768.3 7.8 all-to-all-start.3
  1776.2 31.0 %fusion.36 = f32[4,1024,512]{2,1,0:T(8,128)} fusion(bf16[8,4,640,1024]{3,2,1,0:T(8,128)(2,1)} %all-to-all-done, bf16[8,4,640,512]{3,2,0,1:T(8,128)(2,1)} %get-tuple-element.14), kind=kOutput, calls=%fused_computation.56 | convolution fusion | flops 21474836480 | bytes 71303168 | tf_op jit(solution)/shard_map/slcd,slcf->ldf/dot_general | solution.py:63
  1808.2 113.4 %scatter_custom_fusion.1 = f32[32]{0:T(128)S(1)} fusion(s32[16384]{0:T(1024)S(1)} %reshape.186, f32[16384]{0:T(1024)S(1)} %broadcast.89, f32[]{:T(128)} %constant.50.clone.1), kind=kCustom, calls=%fused_computation.95 | custom fusion | flops 16384 | bytes 132 | tf_op jit(solution)/shard_map/scatter-add | solution.py:30
  1921.6 333.8 %psum.14 = f32[2,32]{1,0:T(2,128)S(1)} all-reduce(f32[2,32]{1,0:T(2,128)S(1)} %pad_maximum_fusion), channel_id=1, replica_groups=mesh['fsdp'=2,'ep'=8] {'fsdp','ep'}, use_global_device_ids=true, to_apply=%region_6.9 | all-reduce | flops 64 | bytes 512 | tf_op jit(solution)/shard_map/psum | solution.py:31
  2255.4 0.6 multiply_bitcast_fusion
  2256.7 3.8 convert_element_type.85
  2260.5 3.8 convert_element_type.84
  2264.3 3.8 convert_element_type.83
  2268.1 340.2 %gather_fusion.3 = bf16[16384,1024]{1,0:T(8,128)(2,1)} fusion(bf16[20480,1024]{1,0:T(8,128)(2,1)} %bitcast.11, s32[16384]{0:T(1024)S(1)} %fusion.51), kind=kCustom, calls=%fused_computation.1.clone | custom fusion | bytes 67174400 | tf_op jit(solution)/shard_map/jit(_take)/gather | solution.py:52
  2608.3 25.3 fusion.19
  2634.6 3.7 convolution_bitcast_fusion
  2638.3 340.5 %gather_fusion.5 = bf16[16384,1024]{1,0:T(8,128)(2,1)} fusion(bf16[20480,1024]{1,0:T(8,128)(2,1)} %bitcast.21, s32[16384]{0:T(1024)S(1)} %fusion.51), kind=kCustom, calls=%fused_computation.3.clone | custom fusion | bytes 67174400 | tf_op jit(solution)/shard_map/jit(_take)/gather | solution.py:68
  2978.8 49.8 %convert_reduce_fusion = (f32[2048,1024]{1,0:T(8,128)S(1)}, bf16[2048,1024]{1,0:T(8,128)(2,1)}) fusion(bf16[16384,1024]{1,0:T(8,128)(2,1)} %gather_fusion.5, pred[16384]{0:T(1024)(128)(4,1)S(1)} %compare_and_fusion.1, bf16[16384,1024]{1,0:T(8,128)(2,1)} %gather_fusion.3, f32[2048,8]{1,0:T(8,128)S(1)} %copy-done.4), kind=kLoop, calls=%fused_computation.10 | loop fusion | flops 113246208 | bytes 79773696 | tf_op jit(solution)/shard_map/reduce_sum | solution.py:74
  3028.6 3.3 add_convert_fusion.1
  3031.9 1.6 copy.133
  (76 shorter events, 5.5 us)
Async XLA Ops:
  7.2 228.0 %copy-start = (bf16[1024,32]{0,1:T(8,128)(2,1)S(1)}, bf16[1024,32]{0,1:T(8,128)(2,1)}, u32[]{:S(2)}) copy-start(bf16[1024,32]{0,1:T(8,128)(2,1)} %param.16) | copy-start | bytes 196612
  9.0 189.3 %copy-start.12 = (s32[16384]{0:T(1024)}, s32[16384]{0:T(1024)S(1)}, u32[]{:S(2)}) copy-start(s32[16384]{0:T(1024)S(1)} %reshape.178) | copy-start | bytes 196612
  94.8 103.5 %copy-start.8 = (s32[20480]{0:T(1024)}, s32[20480]{0:T(1024)S(1)}, u32[]{:S(2)}) copy-start(s32[20480]{0:T(1024)S(1)} %scatter_custom_fusion) | copy-start | bytes 245764
  94.9 103.4 %copy-start.15 = (pred[20480]{0:T(1024)(128)(4,1)}, pred[20480]{0:T(1024)(128)(4,1)S(1)}, u32[]{:S(2)}) copy-start(pred[20480]{0:T(1024)(128)(4,1)S(1)} %compare_and_fusion) | copy-start | bytes 61444
  95.6 102.6 %copy-start.10 = (s32[20480]{0:T(1024)}, s32[20480]{0:T(1024)S(1)}, u32[]{:S(2)}) copy-start(s32[20480]{0:T(1024)S(1)} %get-tuple-element.17) | copy-start | bytes 245764
  226.3 8.0 copy-start.5
  226.3 462.8 %all-to-all-start = ((bf16[8,4,640,1024]{3,2,1,0:T(8,128)(2,1)}), bf16[8,4,640,1024]{3,2,1,0:T(8,128)(2,1)}, u32[]{:S(2)}, u32[]{:S(2)}) async-start(bf16[8,4,640,1024]{3,2,1,0:T(8,128)(2,1)} %bitcast.111), calls=%async_computation | async-start | bytes 83886080 | tf_op jit(solution)/shard_map/all_to_all | solution.py:42
  239.4 130.6 %copy-start.1 = (f32[2048,32]{0,1:T(8,128)}, f32[2048,32]{0,1:T(8,128)S(1)}, u32[]{:S(2)}) copy-start(f32[2048,32]{0,1:T(8,128)S(1)} %get-tuple-element.12) | copy-start | bytes 786436
  239.4 131.4 %copy-start.6 = (s32[2048,8]{0,1:T(8,128)S(1)}, s32[2048,8]{0,1:T(8,128)}, u32[]{:S(2)}) copy-start(s32[2048,8]{0,1:T(8,128)} %param.14) | copy-start | bytes 196612
  239.4 132.3 %copy-start.11 = (s32[20480]{0:T(1024)S(1)}, s32[20480]{0:T(1024)}, u32[]{:S(2)}) copy-start(s32[20480]{0:T(1024)} %copy-done.10) | copy-start | bytes 245764
  371.3 103.4 %copy-start.3 = (f32[2048,8]{1,0:T(8,128)}, f32[2048,8]{1,0:T(8,128)S(1)}, u32[]{:S(2)}) copy-start(f32[2048,8]{1,0:T(8,128)S(1)} %copy.84) | copy-start | bytes 196612
  371.8 102.8 %copy-start.14 = (s32[20480]{0:T(1024)S(1)}, s32[20480]{0:T(1024)}, u32[]{:S(2)}) copy-start(s32[20480]{0:T(1024)} %get-tuple-element.16) | copy-start | bytes 245764
  474.6 113.1 %copy-start.9 = (s32[20480]{0:T(1024)S(1)}, s32[20480]{0:T(1024)}, u32[]{:S(2)}) copy-start(s32[20480]{0:T(1024)} %copy-done.8) | copy-start | bytes 245764
  474.6 113.1 %copy-start.16 = (pred[20480]{0:T(1024)(128)(4,1)S(1)}, pred[20480]{0:T(1024)(128)(4,1)}, u32[]{:S(2)}) copy-start(pred[20480]{0:T(1024)(128)(4,1)} %copy-done.15) | copy-start | bytes 61444
  689.1 461.7 %all-to-all-start.2 = ((bf16[8,4,640,1024]{3,2,1,0:T(8,128)(2,1)}), bf16[8,4,640,1024]{3,2,1,0:T(8,128)(2,1)}, u32[]{:S(2)}, u32[]{:S(2)}) async-start(bf16[8,4,640,1024]{3,2,1,0:T(8,128)(2,1)} %bitcast.112), calls=%async_computation.2 | async-start | bytes 83886080 | tf_op jit(solution)/shard_map/all_to_all | solution.py:58
  696.9 59.7 %all-gather.4.cloned.1.call-start = ((), (), s32[]{:S(2)}) async-start(), calls=%async_computation.7 | async-start | bytes 6291456 | tf_op jit(solution)/shard_map/all_gather | solution.py:43
  697.7 115.6 %all-gather.8.cloned.1.call-start = ((), (), s32[]{:S(2)}) async-start(), calls=%async_computation.9 | async-start | bytes 6291456 | tf_op jit(solution)/shard_map/all_gather | solution.py:45
  698.4 482.8 %all-gather.6.cloned.1.call-start = ((), (), s32[]{:S(2)}) async-start(), calls=%async_computation.8 | async-start | bytes 6291456 | tf_op jit(solution)/shard_map/all_gather | solution.py:44
  1306.6 461.7 %all-to-all-start.1 = ((bf16[8,4,640,1024]{3,2,1,0:T(8,128)(2,1)}), bf16[8,4,640,1024]{3,2,1,0:T(8,128)(2,1)}, u32[]{:S(2)}, u32[]{:S(2)}) async-start(bf16[8,4,640,1024]{3,2,1,0:T(8,128)(2,1)} %copy.88), calls=%async_computation.1 | async-start | bytes 83886080 | tf_op jit(solution)/shard_map/all_to_all | solution.py:51
  1314.4 942.4 %reduce-scatter.8.cloned.1.call-start = ((), (), s32[]{:S(2)}) async-start(), calls=%async_computation.13 | async-start | bytes 12582912 | tf_op jit(solution)/shard_map/reduce_scatter | solution.py:78
  1346.0 914.5 %reduce-scatter.6.cloned.1.call-start = ((), (), s32[]{:S(2)}) async-start(), calls=%async_computation.12 | async-start | bytes 12582912 | tf_op jit(solution)/shard_map/reduce_scatter | solution.py:77
  1768.3 870.1 %all-to-all-start.3 = ((bf16[8,4,640,1024]{3,2,1,0:T(8,128)(2,1)}), bf16[8,4,640,1024]{3,2,1,0:T(8,128)(2,1)}, u32[]{:S(2)}, u32[]{:S(2)}) async-start(bf16[8,4,640,1024]{3,2,1,0:T(8,128)(2,1)} %copy.92), calls=%async_computation.3 | async-start | bytes 83886080 | tf_op jit(solution)/shard_map/all_to_all | solution.py:67
  1776.1 31.2 %copy-start.7 = (s32[2048,8]{0,1:T(8,128)S(1)}, s32[2048,8]{0,1:T(8,128)}, u32[]{:S(2)}) copy-start(s32[2048,8]{0,1:T(8,128)} %param.14) | copy-start | bytes 196612
  1776.1 145.5 %copy-start.17 = (f32[32]{0:T(128)S(1)}, f32[32]{0:T(128)}, u32[]{:S(2)}) copy-start(f32[32]{0:T(128)} %get-tuple-element.11) | copy-start | bytes 388
  1776.1 480.5 %copy-start.13 = (s32[16384]{0:T(1024)S(1)}, s32[16384]{0:T(1024)}, u32[]{:S(2)}) copy-start(s32[16384]{0:T(1024)} %copy-done.12) | copy-start | bytes 196612
  1776.1 488.2 %reduce-scatter.4.cloned.1.call-start = ((), (), s32[]{:S(2)}) async-start(), calls=%async_computation.11 | async-start | bytes 12582912 | tf_op jit(solution)/shard_map/reduce_scatter | solution.py:76
  1807.3 1224.6 %all-reduce.2.cloned.1.call-start = ((), (), s32[]{:S(2)}) async-start(), calls=%async_computation.10 | async-start | bytes 262144 | tf_op jit(solution)/shard_map/psum | solution.py:75
  2608.3 26.1 copy-start.2
  2638.3 340.5 %copy-start.4 = (f32[2048,8]{1,0:T(8,128)S(1)}, f32[2048,8]{1,0:T(8,128)}, u32[]{:S(2)}) copy-start(f32[2048,8]{1,0:T(8,128)} %copy-done.3) | copy-start | bytes 196612
Sparse Core Ops, SparseCore 0:
  699.3 57.2 all-gather.3
  758.1 55.0 all-gather.7
  814.8 55.0 all-gather.5
  1346.1 99.4 reduce-scatter.7
  1447.8 97.3 reduce-scatter.5
  1807.4 99.5 reduce-scatter.3
  2638.4 66.5 all-reduce.1
where the time goes:
time: 3060 us; the launch traced here: 3040 us
  local copies, waits for them, and re-layouts  1190 us (39%)
  waiting for transfers between devices  763 us (25%)
  matrix products  384 us (13%)
  blocking collectives  334 us (11%)
  other arithmetic  320 us (10%)
  starting transfers between devices  31.9 us (1%)
    gather x1, local copies, waits for them, and re-layouts, local_step(): jnp.take(d_back, dest_row, axis=0, mode='fill', fill_value=0)  340 us
    gather x1, local copies, waits for them, and re-layouts, local_step(): jnp.take(back_buf, dest_row, axis=0, mode='fill', fill_value=0)  340 us
    all_to_all x1, waiting for transfers between devices, local_step(): d_out_recv = lax.all_to_all(d_out, 'ep', 0, 0, tiled=True)  338 us
    psum x1, blocking collectives, local_step(): lax.psum(jnp.stack([counts, jnp.sum(prob_all, axis=0)]), all_axes)  334 us
    all_to_all x1, waiting for transfers between devices, local_step(): lax.all_to_all(out_buf, 'ep', 0, 0, tiled=True).reshape(n_slots, d_model)  273 us
    gather x5, local copies, waits for them, and re-layouts, local_step(): gate = jnp.take_along_axis(prob_all, ids_loc, axis=1)  132 us
    scatter-add x1, other arithmetic, local_step(): jax.ops.segment_sum(jnp.ones(flat_ids.shape, jnp.float32), flat_ids, num_...  113 us
    gather x1, local copies, waits for them, and re-layouts, local_step(): gate_slot = jnp.where(filled, jnp.take(gate.reshape(-1), pair_pos), 0.0)  113 us
  transfers between devices with their start and end apart: 11, of which 5 were waited for; matrix products, arithmetic and copies ran while one was open for 51% of the time, Pallas kernels for 0%

commit v1 on v0

v1 whole, which is shorter than its diff:
```python
import functools

import jax
import jax.numpy as jnp
from jax import lax
from jax.experimental import pallas as pl
from jax.experimental.pallas import tpu as pltpu
from jax.sharding import PartitionSpec as P


AUX_COEF = 0.01
BLK = 1024
TILE = 256
X, Y = 2, 4
KERNEL_FLOPS = 100_000_000
F32 = jnp.float32
BF16 = jnp.bfloat16


def dot(a, b, ca, cb):
    return lax.dot_general(a, b, (((ca,), (cb,)), ((), ())), preferred_element_type=F32)


def expert_kernel(has_init, nt_ref, xd0_ref, xd1_ref, pos_ref, gate_ref, wg_ref, wu_ref, wd_ref, *rest):
    if has_init:
        ig_ref, iu_ref, id_ref = rest[:3]
        rest = rest[3:]
    (yd0_ref, yd1_ref, dgate_ref, og_ref, ou_ref, od_ref,
     xd_ref, yd_ref, ag_ref, au_ref, ad_ref, tok_sem, in_sem, out_sem) = rest
    b = pl.program_id(0)
    e = pl.program_id(1)
    last = pl.num_programs(0) - 1
    n_exp = og_ref.shape[0]
    d_model = xd_ref.shape[3]
    tok_in = [pltpu.make_async_copy(src, xd_ref.at[k], tok_sem.at[k]) for k, src in enumerate((xd0_ref, xd1_ref))]
    tok_out = [pltpu.make_async_copy(yd_ref.at[k], dst, tok_sem.at[2 + k]) for k, dst in enumerate((yd0_ref, yd1_ref))]

    def in_copies(k):
        return [pltpu.make_async_copy(src.at[k], dst.at[k], in_sem.at[k, i])
                for i, (src, dst) in enumerate(((ig_ref, ag_ref), (iu_ref, au_ref), (id_ref, ad_ref)))]

    def out_copies(k):
        return [pltpu.make_async_copy(src.at[k], dst.at[k], out_sem.at[k, i])
                for i, (src, dst) in enumerate(((ag_ref, og_ref), (au_ref, ou_ref), (ad_ref, od_ref)))]

    @pl.when((b == 0) & (e == 0))
    def _():
        tok_in[0].start()
        if has_init:
            for c in in_copies(0):
                c.start()
        tok_in[1].start()
        if has_init:
            for k in range(1, n_exp):
                for c in in_copies(k):
                    c.start()

    for k in range(2):
        @pl.when((b == k) & (e == 0))
        def _():
            tok_in[k].wait()

    @pl.when(e == 0)
    def _():
        yd_ref[b] = jnp.zeros(yd_ref.shape[1:], F32)

    @pl.when(b == 0)
    def _():
        if has_init:
            for c in in_copies(e):
                c.wait()
        else:
            ag_ref[e] = jnp.zeros(ag_ref.shape[1:], F32)
            au_ref[e] = jnp.zeros(au_ref.shape[1:], F32)
            ad_ref[e] = jnp.zeros(ad_ref.shape[1:], F32)

    dgate_ref[...] = jnp.zeros(dgate_ref.shape, F32)
    gate_row = gate_ref[0, 0]

    def tile(i, carry):
        pos = pos_ref[0, 0]
        rows = (lax.broadcasted_iota(jnp.int32, (TILE, BLK), 0) + i * TILE).astype(F32)
        hit = rows == pos
        pick = jnp.where(hit, 1.0, 0.0).astype(BF16)
        gate_c = jnp.sum(jnp.where(hit, gate_row, 0.0), axis=1, keepdims=True)
        xc = dot(pick, xd_ref[b, 0], 1, 0).astype(BF16)
        dyc = dot(pick, xd_ref[b, 1], 1, 0)
        hg = dot(xc, wg_ref[0], 1, 0)
        hu = dot(xc, wu_ref[0], 1, 0)
        sig = jax.nn.sigmoid(hg)
        act = (hg * sig * hu).astype(BF16)
        do = (gate_c * dyc).astype(BF16)
        da = dot(do, wd_ref[0], 1, 1).astype(BF16).astype(F32)
        dhg = (da * hu * sig * (1.0 + hg * (1.0 - sig))).astype(BF16)
        dhu = (da * hg * sig).astype(BF16)
        o = dot(act, wd_ref[0], 1, 0).astype(BF16)
        dgate_c = jnp.sum(dyc * o.astype(F32), axis=1, keepdims=True)
        dgate_ref[0, 0] += jnp.sum(jnp.where(hit, dgate_c, 0.0), axis=0, keepdims=True)
        db = (dot(dhg, wg_ref[0], 1, 1) + dot(dhu, wu_ref[0], 1, 1)).astype(BF16)
        ag_ref[e] += dot(xc, dhg, 0, 0)
        au_ref[e] += dot(xc, dhu, 0, 0)
        ad_ref[e] += dot(act, do, 0, 0)
        gate_t = jnp.transpose(jnp.broadcast_to(gate_row, (8, BLK)))[:, :1]
        width = 256
        for c in range(d_model // width):
            cols = slice(c * width, (c + 1) * width)
            yd_ref[b, 0, :, cols] += gate_t * dot(pick, o[:, cols], 0, 0)
            yd_ref[b, 1, :, cols] += dot(pick, db[:, cols], 0, 0)
        return carry

    lax.fori_loop(0, nt_ref[b, e], tile, 0)

    for k in range(2):
        @pl.when((b == k) & (e == n_exp - 1))
        def _():
            tok_out[k].start()

    @pl.when(b == last)
    def _():
        for c in out_copies(e):
            c.start()

        @pl.when(e == n_exp - 1)
        def _():
            for k in range(2):
                tok_out[k].wait()
            for k in range(n_exp):
                for c in out_copies(k):
                    c.wait()


def experts(nt, xd0, xd1, pos, gate, wg, wu, wd, init):
    n_exp, d_model, d_ff = wg.shape
    row = pl.BlockSpec((1, 1, 1, BLK), lambda b, e, nt: (b, e, 0, 0))
    up = pl.BlockSpec((1, d_model, d_ff), lambda b, e, nt: (e, 0, 0))
    down = pl.BlockSpec((1, d_ff, d_model), lambda b, e, nt: (e, 0, 0))
    hbm = pl.BlockSpec(memory_space=pl.ANY)
    acc_up = jax.ShapeDtypeStruct((n_exp, d_model, d_ff), F32)
    acc_down = jax.ShapeDtypeStruct((n_exp, d_ff, d_model), F32)
    out_tok = jax.ShapeDtypeStruct((2, BLK, d_model), F32)
    return pl.pallas_call(
        functools.partial(expert_kernel, init is not None),
        grid_spec=pltpu.PrefetchScalarGridSpec(
            num_scalar_prefetch=1,
            grid=(2, n_exp),
            in_specs=[hbm, hbm, row, row, up, up, down] + ([hbm] * 3 if init is not None else []),
            out_specs=[hbm, hbm, row, hbm, hbm, hbm],
            scratch_shapes=[
                pltpu.VMEM((2, 2, BLK, d_model), BF16),
                pltpu.VMEM((2, 2, BLK, d_model), F32),
                pltpu.VMEM((n_exp, d_model, d_ff), F32),
                pltpu.VMEM((n_exp, d_model, d_ff), F32),
                pltpu.VMEM((n_exp, d_ff, d_model), F32),
                pltpu.SemaphoreType.DMA((4,)),
                pltpu.SemaphoreType.DMA((n_exp, 3)),
                pltpu.SemaphoreType.DMA((n_exp, 3)),
            ],
        ),
        out_shape=[out_tok, out_tok, jax.ShapeDtypeStruct((2, n_exp, 1, BLK), F32), acc_up, acc_up, acc_down],
        input_output_aliases={8: 3, 9: 4, 10: 5} if init is not None else {},
        compiler_params=pltpu.CompilerParams(
            dimension_semantics=("arbitrary", "arbitrary"), vmem_limit_bytes=67_000_000),
        cost_estimate=pl.CostEstimate(flops=KERNEL_FLOPS, bytes_accessed=80_000_000, transcendentals=1_000_000),
    )(nt, xd0, xd1, pos, gate, wg, wu, wd, *(init or ()))


def whole(mine, axis, f_idx):
    other = lax.ppermute(mine, 'fsdp', [(0, 1), (1, 0)])
    return jnp.where(f_idx == 0, jnp.concatenate([mine, other], axis), jnp.concatenate([other, mine], axis))


def swap_halves(part, axis, f_idx):
    size = part.shape[axis] // 2
    mine = lax.dynamic_slice_in_dim(part, f_idx * size, size, axis)
    theirs = lax.dynamic_slice_in_dim(part, (1 - f_idx) * size, size, axis)
    other = lax.ppermute(theirs, 'fsdp', [(0, 1), (1, 0)])
    return (mine + other).astype(BF16)


def by_distance(a, bits):
    rest = a.shape[1:]
    a = a.reshape(2, 2, 2, *rest)
    for axis, bit in enumerate(bits):
        a = jnp.where(bit, jnp.flip(a, axis), a)
    return a.reshape(8, *rest)


def hop(a, bit):
    return lax.ppermute(a, 'ep', [(i, i ^ bit) for i in range(8)])


def solution(mesh):
    n_fsdp = mesh.shape['fsdp']
    n_ep = mesh.shape['ep']
    n_dev = n_fsdp * n_ep
    all_axes = ('fsdp', 'ep')
    tok_spec = P(('ep', 'fsdp'), None)
    up_spec = P('ep', 'fsdp', None)
    down_spec = P('ep', None, 'fsdp')

    def local_step(x_loc, dy_loc, ids_loc, slot_loc, w_router, wg_loc, wu_loc, wd_loc):
        tok_dev, _ = x_loc.shape
        top_k = ids_loc.shape[1]
        n_exp = w_router.shape[1]
        local_exp = n_exp // n_ep
        tokens = tok_dev * n_dev
        halves = tok_dev // BLK
        f_idx = lax.axis_index('fsdp')

        logits = dot(w_router, x_loc, 0, 1)
        prob = jax.nn.softmax(logits, axis=0)
        expert = jnp.arange(n_exp, dtype=jnp.int32)[None, :, None]
        match = ids_loc.T[:, None, :] == expert
        chosen = jnp.any(match, axis=0)
        kept = jnp.any(match & (slot_loc.T[:, None, :] >= 0), axis=0)
        stat = jnp.stack([jnp.sum(chosen.astype(F32), axis=1), jnp.sum(prob, axis=1)])
        stat = lax.psum(stat, all_axes)
        load_frac = stat[0] / (tokens * top_k)
        aux_loss = AUX_COEF * n_exp * jnp.sum(load_frac * stat[1] / tokens)

        upto = jnp.arange(BLK)[:, None] <= jnp.arange(BLK)[None, :]
        kept_b = kept.astype(BF16).reshape(n_exp * halves, BLK)
        place = dot(kept_b, upto.astype(BF16), 1, 0).reshape(n_exp, tok_dev) - 1.0
        pos = jnp.where(kept, place, -1.0)
        gate = jnp.where(kept, prob, 0.0)
        meta = jnp.stack([pos, gate], axis=1).reshape(n_ep, local_exp, 2, tok_dev)
        meta = lax.all_to_all(meta, 'ep', 0, 0, tiled=True)
        ep_idx = lax.axis_index('ep')
        bits = [(ep_idx // d) % 2 == 1 for d in (4, 2, 1)]
        meta = by_distance(meta, bits)
        meta = meta.reshape(n_ep, local_exp, 2, halves, BLK).transpose(3, 0, 1, 2, 4)
        pos_b = meta[:, :, :, 0:1]
        gate_b = meta[:, :, :, 1:2]
        nt = ((jnp.max(pos_b[..., 0, :], axis=-1) + TILE) / TILE).astype(jnp.int32)

        xd = {(0, h): jnp.stack([x_loc[h * BLK:(h + 1) * BLK], dy_loc[h * BLK:(h + 1) * BLK]]) for h in range(2)}
        xd[X, 0] = hop(xd[0, 0], X)
        xd[Y, 1] = hop(xd[0, 1], Y)
        xd[X, 1] = hop(xd[0, 1], X)
        xd[Y, 0] = hop(xd[0, 0], Y)
        xd[X + Y, 1] = hop(xd[Y, 1], X)
        xd[X + Y, 0] = hop(xd[X, 0], Y)
        wg, wu, wd = (whole(w, axis, f_idx) for w, axis in ((wg_loc, 1), (wu_loc, 1), (wd_loc, 2)))

        acc = None
        part, dgate, sent = {}, {}, {}
        order = ((X, 0), (Y, 1), (0, 0), (0, 1), (X + Y, 0), (X + Y, 1), (Y, 0), (X, 1))
        for k, h in order[:4]:
            xd[k + 1, h] = hop(xd[k, h], 1)
        for n, (k, h) in enumerate(order):
            nt_k = nt[h, k:k + 2]
            if n >= 2:
                nt_k, done = lax.optimization_barrier((nt_k, sent[order[n - 2]]))
                part[order[n - 2]] = done
            yd0, yd1, dgate[k, h], *acc = experts(
                nt_k, xd[k, h], xd[k + 1, h], pos_b[h, k:k + 2], gate_b[h, k:k + 2], wg, wu, wd, acc)
            other = hop(yd1, 1)
            sent[k, h] = [yd0[i] + other[i] for i in range(2)]
            if n == 2:
                for late in order[4:]:
                    xd[late], dgate[k, h] = lax.optimization_barrier((xd[late], dgate[k, h]))
                    xd[late[0] + 1, late[1]] = hop(xd[late], 1)
        for last in order[-2:]:
            part[last] = sent[last]
        direct = [[hop(part[X, 0][i], X), hop(part[Y, 1][i], Y)] for i in range(2)]
        relay = [[hop(part[X + Y, 0][i], X), hop(part[X + Y, 1][i], Y)] for i in range(2)]
        relay = [[hop(part[Y, 0][i] + relay[i][0], Y), hop(part[X, 1][i] + relay[i][1], X)]
                 for i in range(2)]
        total = [[part[0, h][i] + direct[i][h] + relay[i][h] for h in range(2)] for i in range(2)]
        y = jnp.concatenate(total[0], axis=0).astype(BF16)
        dx_exp = jnp.concatenate(total[1], axis=0)
        dgate = jnp.stack([jnp.concatenate([dgate[k, h] for k in (0, X, Y, X + Y)], axis=0) for h in range(2)], axis=3)
        dgate = by_distance(dgate.reshape(n_ep, local_exp, tok_dev), bits)
        dgate = lax.all_to_all(dgate, 'ep', 0, 0, tiled=True).reshape(n_exp, tok_dev)
        d_prob = dgate + AUX_COEF * n_exp * load_frac[:, None]
        d_logit = (prob * (d_prob - jnp.sum(prob * d_prob, axis=0, keepdims=True))).astype(BF16)
        dx = (dx_exp + dot(d_logit, w_router, 0, 1)).astype(BF16)
        dw_router = lax.psum(dot(x_loc, d_logit, 0, 1), all_axes)
        dwg, dwu, dwd = acc
        return (y, aux_loss, dx, dw_router, swap_halves(dwg, 1, f_idx), swap_halves(dwu, 1, f_idx),
                swap_halves(dwd, 2, f_idx))

    return jax.shard_map(local_step, mesh=mesh,
                         in_specs=(tok_spec, tok_spec, tok_spec, tok_spec, P(), up_spec, up_spec, down_spec),
                         out_specs=(tok_spec, P(), tok_spec, P(), up_spec, up_spec, down_spec),
                         check_vma=False)
```

time: 3060 us -> 1800 us (0.59)
  local copies, waits for them, and re-layouts: 1190 us -> 22.9 us
  Pallas kernels: 0 us -> 485 us
  matrix products: 384 us -> 10.4 us
  starting transfers between devices: 31.9 us -> 235 us
  blocking collectives: 334 us -> 169 us
  other arithmetic: 320 us -> 160 us
  waiting for transfers between devices: 763 us -> 697 us
    gather x10 -> x0, local copies, waits for them, and re-layouts: 1130 us -> none  [the longest x1 340 us: local_step(): jnp.take(d_back, dest_row, axis=0, mode='fill', fill_value=0)]
    ppermute x0 -> x40, waiting for transfers between devices: none -> 691 us  [the longest x34 530 us: hop(): return lax.ppermute(a, 'ep', [(i, i ^ bit) for i in range(8)])]
    all_to_all x4 -> x2, waiting for transfers between devices: 684 us -> 6.03 us  [the longest x1 6.03 us: local_step(): meta = lax.all_to_all(meta, 'ep', 0, 0, tiled=True)]
    pallas_call x0 -> x8, Pallas kernels: none -> 485 us  [experts(): pl.pallas_call(functools.partial(expert_kernel, init is not None), grid_s...]
    dot_general x13 -> x4, matrix products: 384 us -> 10.4 us  [dot(): lax.dot_general(a, b, (((ca,), (cb,)), ((), ())), preferred_element_type=...]
    ppermute x0 -> x40, starting transfers between devices: none -> 228 us  [the longest x34 197 us: hop(): return lax.ppermute(a, 'ep', [(i, i ^ bit) for i in range(8)])]
    scatter-add x2 -> x0, other arithmetic: 199 us -> none  [the longest x1 113 us: local_step(): jax.ops.segment_sum(jnp.ones(flat_ids.shape, jnp.float32), flat_ids, num_...]
    psum x1, blocking collectives: 334 us -> 169 us  [local_step(): stat = lax.psum(stat, all_axes)]
  transfers between devices with their start and end apart: 11 -> 43, of which waited for: 5 -> 16; matrix products, arithmetic and copies ran while one was open for 51% -> 10% of each run, Pallas kernels for 0% -> 27%
where the time goes in v1:
time: 1800 us
  waiting for transfers between devices  697 us (39%)
  Pallas kernels  485 us (27%)
  starting transfers between devices  235 us (13%)
  blocking collectives  169 us (9%)
  other arithmetic  160 us (9%)
  local copies, waits for them, and re-layouts  22.9 us (1%)
    ppermute x34, waiting for transfers between devices, hop(): return lax.ppermute(a, 'ep', [(i, i ^ bit) for i in range(8)])  530 us
    pallas_call x8, Pallas kernels, experts(): pl.pallas_call(functools.partial(expert_kernel, init is not None), grid_s...  485 us
    ppermute x34, starting transfers between devices, hop(): return lax.ppermute(a, 'ep', [(i, i ^ bit) for i in range(8)])  197 us
    psum x1, blocking collectives, local_step(): stat = lax.psum(stat, all_axes)  169 us
    ppermute x3, waiting for transfers between devices, whole(): other = lax.ppermute(mine, 'fsdp', [(0, 1), (1, 0)])  115 us
    add x6, other arithmetic, local_step(): sent[k, h] = [yd0[i] + other[i] for i in range(2)]  72.8 us
    ppermute x3, waiting for transfers between devices, swap_halves(): other = lax.ppermute(theirs, 'fsdp', [(0, 1), (1, 0)])  46 us
  transfers between devices with their start and end apart: 43, of which 16 were waited for; matrix products, arithmetic and copies ran while one was open for 10% of the time, Pallas kernels for 27%

profile of v1, /device:TPU:0, one launch (start us, length us, event | category | flops | bytes accessed | tf_op | source)
XLA Modules:
  0.0 1796.3 jit_solution(2232727168458272604)
XLA Ops:
  26.8 80.6 %collective-permute-done.xd0_ref = bf16[2,1024,1024]{2,1,0:T(8,128)(2,1)} collective-permute-done((bf16[2,1024,1024]{2,1,0:T(8,128)(2,1)}, bf16[2,1024,1024]{2,1,0:T(8,128)(2,1)}, u32[]{:S(2)}, u32[]{:S(2)}) %collective-permute-start) | collective-permute-done | bytes 4194336 | tf_op jit(solution)/shard_map/ppermute | solution.py:189
  116.3 6.0 all-to-all-done
  126.6 34.8 %collective-permute-done.2 = bf16[4,512,512]{2,1,0:T(8,128)(2,1)} collective-permute-done((bf16[4,512,512]{2,1,0:T(8,128)(2,1)S(1)}, bf16[4,512,512]{2,1,0:T(8,128)(2,1)}, u32[]{:S(2)}, u32[]{:S(2)}) %collective-permute-start.2) | collective-permute-done | bytes 2097184 | tf_op jit(solution)/shard_map/ppermute | solution.py:168
  165.9 40.4 %collective-permute-done.3 = bf16[4,512,512]{2,1,0:T(8,128)(2,1)} collective-permute-done((bf16[4,512,512]{2,1,0:T(8,128)(2,1)}, bf16[4,512,512]{2,1,0:T(8,128)(2,1)}, u32[]{:S(2)}, u32[]{:S(2)}) %collective-permute-start.3) | collective-permute-done | bytes 2097184 | tf_op jit(solution)/shard_map/ppermute | solution.py:168
  211.3 39.5 %collective-permute-done.4 = bf16[4,512,512]{2,1,0:T(8,128)(2,1)} collective-permute-done((bf16[4,512,512]{2,1,0:T(8,128)(2,1)}, bf16[4,512,512]{2,1,0:T(8,128)(2,1)}, u32[]{:S(2)}, u32[]{:S(2)}) %collective-permute-start.4) | collective-permute-done | bytes 2097184 | tf_op jit(solution)/shard_map/ppermute | solution.py:168
  255.8 55.6 %shard_map.135 = (f32[2,1024,1024]{2,1,0:T(8,128)}, f32[2,1024,1024]{2,1,0:T(8,128)}, f32[2,4,1,1024]{3,2,1,0:T(1,128)}, f32[4,1024,512]{2,1,0:T(8,128)}, f32[4,...) custom-call(s32[2,4]{1,0:T(2,128)} %get-tuple-element.200.nt_ref, bf16[2,1024,1024]{2,1,0:T(8,128)(2,1)} %collective-permute-done.xd0_ref, ...), custom_call_target="tpu_custom_call" | custom-call | flops 100000000 | bytes 80000000 | tf_op jit(solution)/shard_map/pallas_call | solution.py:141
  311.3 15.0 collective-permute-start.5
  326.4 61.3 %shard_map.136 = (f32[2,1024,1024]{2,1,0:T(8,128)}, f32[2,1024,1024]{2,1,0:T(8,128)}, f32[2,4,1,1024]{3,2,1,0:T(1,128)}, f32[4,1024,512]{2,1,0:T(8,128)}, f32[4,...) custom-call(s32[2,4]{1,0:T(2,128)} %get-tuple-element.199.nt_ref, ...), custom_call_target="tpu_custom_call", output_to_operand_aliasing={{3}: (8, {}), {4}: (9, {}), {5}: (10, {})} | custom-call | flops 100000000 | bytes 80000000 | tf_op jit(solution)/shard_map/pallas_call | solution.py:141
  388.3 12.1 fusion.19
  400.5 6.8 collective-permute-done.6.xd1_ref
  407.3 61.4 %shard_map.137 = (f32[2,1024,1024]{2,1,0:T(8,128)}, f32[2,1024,1024]{2,1,0:T(8,128)}, f32[2,4,1,1024]{3,2,1,0:T(1,128)}, f32[4,1024,512]{2,1,0:T(8,128)}, f32[4,...) custom-call(s32[2,4]{1,0:T(2,128)} %get-tuple-element.83.nt_ref, ...), custom_call_target="tpu_custom_call", output_to_operand_aliasing={{3}: (8, {}), {4}: (9, {}), {5}: (10, {})} | custom-call | flops 100000000 | bytes 80000000 | tf_op jit(solution)/shard_map/pallas_call | solution.py:141
  468.7 10.4 collective-permute-start.9
  479.1 32.8 %collective-permute-start.11 = (bf16[2,1024,1024]{2,1,0:T(8,128)(2,1)}, bf16[2,1024,1024]{2,1,0:T(8,128)(2,1)}, u32[]{:S(2)}, u32[]{:S(2)}) collective-permute-start(bf16[2,1024,1024]{2,1,0:T(8,128)(2,1)} %collective-permute-done.xd0_ref), channel_id=1, source_target_pairs={{0,4},{1,5},{2,6},{3,7},{4,0},{5,1},{6,2},{7,3},{8,12},{9,13},{10,... | collective-permute-start | bytes 12582920 | tf_op jit(solution)/shard_map/ppermute | solution.py:189
  511.9 12.1 fusion.15
  524.0 61.6 %shard_map.138 = (f32[2,1024,1024]{2,1,0:T(8,128)}, f32[2,1024,1024]{2,1,0:T(8,128)}, f32[2,4,1,1024]{3,2,1,0:T(1,128)}, f32[4,1024,512]{2,1,0:T(8,128)}, f32[4,...) custom-call(s32[2,4]{1,0:T(2,128)} %get-tuple-element.99.nt_ref, ...), custom_call_target="tpu_custom_call", output_to_operand_aliasing={{3}: (8, {}), {4}: (9, {}), {5}: (10, {})} | custom-call | flops 100000000 | bytes 80000000 | tf_op jit(solution)/shard_map/pallas_call | solution.py:141
  585.8 31.0 %collective-permute-start.17 = (bf16[2,1024,1024]{2,1,0:T(8,128)(2,1)}, bf16[2,1024,1024]{2,1,0:T(8,128)(2,1)}, u32[]{:S(2)}, u32[]{:S(2)}) collective-permute-start(bf16[2,1024,1024]{2,1,0:T(8,128)(2,1)} %collective-permute-done.7.xd0_ref), channel_id=1, source_target_pairs={{0,2},{1,3},{2,0},{3,1},{4,6},{5,7},{6,4},{7,5},{8,10},{9,11},{10,... | collective-permute-start | bytes 12582920 | tf_op jit(solution)/shard_map/ppermute | solution.py:189
  616.9 91.1 %collective-permute-done.17.xd0_ref = bf16[2,1024,1024]{2,1,0:T(8,128)(2,1)} collective-permute-done((bf16[2,1024,1024]{2,1,0:T(8,128)(2,1)}, bf16[2,1024,1024]{2,1,0:T(8,128)(2,1)}, u32[]{:S(2)}, u32[]{:S(2)}) %collective-permute-start.17) | collective-permute-done | bytes 4194336 | tf_op jit(solution)/shard_map/ppermute | solution.py:189
  708.0 12.1 fusion.17
  720.1 61.4 %shard_map.139 = (f32[2,1024,1024]{2,1,0:T(8,128)}, f32[2,1024,1024]{2,1,0:T(8,128)}, f32[2,4,1,1024]{3,2,1,0:T(1,128)}, f32[4,1024,512]{2,1,0:T(8,128)}, f32[4,...) custom-call(s32[2,4]{1,0:T(2,128)} %get-tuple-element.94.nt_ref, ...), custom_call_target="tpu_custom_call", output_to_operand_aliasing={{3}: (8, {}), {4}: (9, {}), {5}: (10, {})} | custom-call | flops 100000000 | bytes 80000000 | tf_op jit(solution)/shard_map/pallas_call | solution.py:141
  781.5 10.8 collective-permute-start.15
  792.3 27.2 %collective-permute-start.16 = (bf16[2,1024,1024]{2,1,0:T(8,128)(2,1)}, bf16[2,1024,1024]{2,1,0:T(8,128)(2,1)}, u32[]{:S(2)}, u32[]{:S(2)}) collective-permute-start(bf16[2,1024,1024]{2,1,0:T(8,128)(2,1)} %pad_maximum_fusion.xd0_ref), channel_id=1, source_target_pairs={{0,4},{1,5},{2,6},{3,7},{4,0},{5,1},{6,2},{7,3},{8,12},{9,13},{10,... | collective-permute-start | bytes 12582920 | tf_op jit(solution)/shard_map/ppermute | solution.py:189
  819.4 12.1 fusion.11
  831.6 61.3 %shard_map.140 = (f32[2,1024,1024]{2,1,0:T(8,128)}, f32[2,1024,1024]{2,1,0:T(8,128)}, f32[2,4,1,1024]{3,2,1,0:T(1,128)}, f32[4,1024,512]{2,1,0:T(8,128)}, f32[4,...) custom-call(s32[2,4]{1,0:T(2,128)} %get-tuple-element.114.nt_ref, ...), custom_call_target="tpu_custom_call", output_to_operand_aliasing={{3}: (8, {}), {4}: (9, {}), {5}: (10, {})} | custom-call | flops 100000000 | bytes 80000000 | tf_op jit(solution)/shard_map/pallas_call | solution.py:141
  893.1 10.3 collective-permute-start.26
  903.4 7.6 collective-permute-done.16.xd0_ref
  910.9 83.5 %collective-permute-done.26.xd0_ref = bf16[2,1024,1024]{2,1,0:T(8,128)(2,1)} collective-permute-done((bf16[2,1024,1024]{2,1,0:T(8,128)(2,1)}, bf16[2,1024,1024]{2,1,0:T(8,128)(2,1)}, u32[]{:S(2)}, u32[]{:S(2)}) %collective-permute-start.26) | collective-permute-done | bytes 4194336 | tf_op jit(solution)/shard_map/ppermute | solution.py:189
  996.2 12.1 fusion.13
  1008.3 61.6 %shard_map.141 = (f32[2,1024,1024]{2,1,0:T(8,128)}, f32[2,1024,1024]{2,1,0:T(8,128)}, f32[2,4,1,1024]{3,2,1,0:T(1,128)}, f32[4,1024,512]{2,1,0:T(8,128)}, f32[4,...) custom-call(s32[2,4]{1,0:T(2,128)} %get-tuple-element.108.nt_ref, ...), custom_call_target="tpu_custom_call", output_to_operand_aliasing={{3}: (8, {}), {4}: (9, {}), {5}: (10, {})} | custom-call | flops 100000000 | bytes 80000000 | tf_op jit(solution)/shard_map/pallas_call | solution.py:141
  1069.9 10.5 collective-permute-start.21
  1080.4 12.2 fusion.7
  1092.6 30.8 %collective-permute-start.22 = (f32[1024,1024]{1,0:T(8,128)}, f32[1024,1024]{1,0:T(8,128)}, u32[]{:S(2)}, u32[]{:S(2)}) collective-permute-start(f32[1024,1024]{1,0:T(8,128)} %get-tuple-element.124), channel_id=1, source_target_pairs={{0,2},{1,3},{2,0},{3,1},{4,6},{5,7},{6,4},{7,5},{8,10},{9,11},{10,... | collective-permute-start | bytes 12582920 | tf_op jit(solution)/shard_map/ppermute | solution.py:189
  1123.5 61.3 %shard_map.142 = (f32[2,1024,1024]{2,1,0:T(8,128)}, f32[2,1024,1024]{2,1,0:T(8,128)}, f32[2,4,1,1024]{3,2,1,0:T(1,128)}, f32[4,1024,512]{2,1,0:T(8,128)}, f32[4,...) custom-call(s32[2,4]{1,0:T(2,128)} %get-tuple-element.129.nt_ref, ...), custom_call_target="tpu_custom_call", output_to_operand_aliasing={{3}: (8, {}), {4}: (9, {}), {5}: (10, {})} | custom-call | flops 100000000 | bytes 80000000 | tf_op jit(solution)/shard_map/pallas_call | solution.py:141
  1188.6 26.6 %collective-permute-done.22 = f32[1024,1024]{1,0:T(8,128)} collective-permute-done((f32[1024,1024]{1,0:T(8,128)}, f32[1024,1024]{1,0:T(8,128)}, u32[]{:S(2)}, u32[]{:S(2)}) %collective-permute-start.22) | collective-permute-done | bytes 4194336 | tf_op jit(solution)/shard_map/ppermute | solution.py:189
  1215.2 89.7 %collective-permute-done.32 = f32[1024,1024]{1,0:T(8,128)} collective-permute-done((f32[1024,1024]{1,0:T(8,128)}, f32[1024,1024]{1,0:T(8,128)}, u32[]{:S(2)}, u32[]{:S(2)}) %collective-permute-start.32) | collective-permute-done | bytes 4194336 | tf_op jit(solution)/shard_map/ppermute | solution.py:189
  1309.8 5.1 constant_dynamic-slice_fusion.1
  1314.9 11.8 collective-permute-start.39
  1329.2 9.7 fusion.4
  1338.9 31.3 %collective-permute-done.35 = f32[1024,1024]{1,0:T(8,128)} collective-permute-done((f32[1024,1024]{1,0:T(8,128)}, f32[1024,1024]{1,0:T(8,128)}, u32[]{:S(2)}, u32[]{:S(2)}) %collective-permute-start.35) | collective-permute-done | bytes 4194336 | tf_op jit(solution)/shard_map/ppermute | solution.py:189
  1370.2 15.2 collective-permute-start.37
  1387.0 13.8 fusion.2
  1400.7 59.4 %collective-permute-done.34 = f32[1024,1024]{1,0:T(8,128)} collective-permute-done((f32[1024,1024]{1,0:T(8,128)}, f32[1024,1024]{1,0:T(8,128)}, u32[]{:S(2)}, u32[]{:S(2)}) %collective-permute-start.34) | collective-permute-done | bytes 4194336 | tf_op jit(solution)/shard_map/ppermute | solution.py:189
  1462.3 46.0 %collective-permute-done.38 = f32[4,512,512]{2,1,0:T(8,128)} collective-permute-done((f32[4,512,512]{2,1,0:T(8,128)}, f32[4,512,512]{2,1,0:T(8,128)}, u32[]{:S(2)}, u32[]{:S(2)}) %collective-permute-start.38) | collective-permute-done | bytes 4194336 | tf_op jit(solution)/shard_map/ppermute | solution.py:176
  1514.6 169.0 %psum.14 = f32[2,32]{1,0:T(2,128)S(1)} all-reduce(f32[2,32]{1,0:T(2,128)S(1)} %pad_maximum_fusion.4), channel_id=1, replica_groups=mesh['fsdp'=2,'ep'=8] {'fsdp','ep'}, use_global_device_ids=true, to_apply=%region_7.0 | all-reduce | flops 64 | bytes 512 | tf_op jit(solution)/shard_map/psum | solution.py:217
  1691.6 5.7 add_convert_fusion
  1697.3 5.7 add_convert_fusion.1
  1707.4 5.2 add_add_fusion.1
  1712.6 5.0 add_add_fusion
  1726.0 52.3 %collective-permute-done.24 = f32[1024,1024]{1,0:T(8,128)} collective-permute-done((f32[1024,1024]{1,0:T(8,128)}, f32[1024,1024]{1,0:T(8,128)}, u32[]{:S(2)}, u32[]{:S(2)}) %collective-permute-start.24) | collective-permute-done | bytes 4194336 | tf_op jit(solution)/shard_map/ppermute | solution.py:189
  (179 shorter events, 100.7 us)
Async XLA Ops:
  13.4 94.1 %collective-permute-start = (bf16[2,1024,1024]{2,1,0:T(8,128)(2,1)}, bf16[2,1024,1024]{2,1,0:T(8,128)(2,1)}, u32[]{:S(2)}, u32[]{:S(2)}) collective-permute-start(bf16[2,1024,1024]{2,1,0:T(8,128)(2,1)} %pad_maximum_fusion.xd0_ref), channel_id=1, source_target_pairs={{0,2},{1,3},{2,0},{3,1},{4,6},{5,7},{6,4},{7,5},{8,10},{9,11},{10,... | collective-permute-start | bytes 12582920 | tf_op jit(solution)/shard_map/ppermute | solution.py:189
  19.0 103.8 %collective-permute-start.7 = (bf16[2,1024,1024]{2,1,0:T(8,128)(2,1)}, bf16[2,1024,1024]{2,1,0:T(8,128)(2,1)}, u32[]{:S(2)}, u32[]{:S(2)}) collective-permute-start(bf16[2,1024,1024]{2,1,0:T(8,128)(2,1)} %pad_maximum_fusion.1.xd0_ref), channel_id=1, source_target_pairs={{0,4},{1,5},{2,6},{3,7},{4,0},{5,1},{6,2},{7,3},{8,12},{9,13},{10,... | collective-permute-start | bytes 12582920 | tf_op jit(solution)/shard_map/ppermute | solution.py:189
  107.5 148.3 %collective-permute-start.1 = (bf16[2,1024,1024]{2,1,0:T(8,128)(2,1)}, bf16[2,1024,1024]{2,1,0:T(8,128)(2,1)}, u32[]{:S(2)}, u32[]{:S(2)}) collective-permute-start(bf16[2,1024,1024]{2,1,0:T(8,128)(2,1)} %collective-permute-done.xd0_ref), channel_id=1, source_target_pairs={{0,1},{1,0},{2,3},{3,2},{4,5},{5,4},{6,7},{7,6},{8,9},{9,8},{10,11... | collective-permute-start | bytes 12582920 | tf_op jit(solution)/shard_map/ppermute | solution.py:189
  108.4 14.0 all-to-all-start
  112.7 48.6 %collective-permute-start.2 = (bf16[4,512,512]{2,1,0:T(8,128)(2,1)S(1)}, bf16[4,512,512]{2,1,0:T(8,128)(2,1)}, u32[]{:S(2)}, u32[]{:S(2)}) collective-permute-start(bf16[4,512,512]{2,1,0:T(8,128)(2,1)S(1)} %copy-done.6), channel_id=1, source_target_pairs={{0,8},{8,0},{1,9},{9,1},{2,10},{10,2},{3,11},{11,3},{4,12},{12,4},... | collective-permute-start | bytes 6291464 | tf_op jit(solution)/shard_map/ppermute | solution.py:168
  114.3 92.0 %collective-permute-start.3 = (bf16[4,512,512]{2,1,0:T(8,128)(2,1)}, bf16[4,512,512]{2,1,0:T(8,128)(2,1)}, u32[]{:S(2)}, u32[]{:S(2)}) collective-permute-start(bf16[4,512,512]{2,1,0:T(8,128)(2,1)} %param.14), channel_id=1, source_target_pairs={{0,8},{8,0},{1,9},{9,1},{2,10},{10,2},{3,11},{11,3},{4,12},{12,4},... | collective-permute-start | bytes 6291464 | tf_op jit(solution)/shard_map/ppermute | solution.py:168
  114.8 136.0 %collective-permute-start.4 = (bf16[4,512,512]{2,1,0:T(8,128)(2,1)}, bf16[4,512,512]{2,1,0:T(8,128)(2,1)}, u32[]{:S(2)}, u32[]{:S(2)}) collective-permute-start(bf16[4,512,512]{2,1,0:T(8,128)(2,1)} %param.15), channel_id=1, source_target_pairs={{0,8},{8,0},{1,9},{9,1},{2,10},{10,2},{3,11},{11,3},{4,12},{12,4},... | collective-permute-start | bytes 6291464 | tf_op jit(solution)/shard_map/ppermute | solution.py:168
  122.8 203.6 %collective-permute-start.8 = (bf16[2,1024,1024]{2,1,0:T(8,128)(2,1)}, bf16[2,1024,1024]{2,1,0:T(8,128)(2,1)}, u32[]{:S(2)}, u32[]{:S(2)}) collective-permute-start(bf16[2,1024,1024]{2,1,0:T(8,128)(2,1)} %collective-permute-done.7.xd0_ref), channel_id=1, source_target_pairs={{0,1},{1,0},{2,3},{3,2},{4,5},{5,4},{6,7},{7,6},{8,9},{9,8},{10,11... | collective-permute-start | bytes 12582920 | tf_op jit(solution)/shard_map/ppermute | solution.py:189
  311.3 77.0 %collective-permute-start.5 = (f32[2,1024,1024]{2,1,0:T(8,128)}, f32[2,1024,1024]{2,1,0:T(8,128)}, u32[]{:S(2)}, u32[]{:S(2)}) collective-permute-start(f32[2,1024,1024]{2,1,0:T(8,128)} %get-tuple-element.82), channel_id=1, source_target_pairs={{0,1},{1,0},{2,3},{3,2},{4,5},{5,4},{6,7},{7,6},{8,9},{9,8},{10,11... | collective-permute-start | bytes 25165832 | tf_op jit(solution)/shard_map/ppermute | solution.py:189
  387.7 124.2 %collective-permute-start.13 = (f32[2,1024,1024]{2,1,0:T(8,128)}, f32[2,1024,1024]{2,1,0:T(8,128)}, u32[]{:S(2)}, u32[]{:S(2)}) collective-permute-start(f32[2,1024,1024]{2,1,0:T(8,128)} %get-tuple-element.98), channel_id=1, source_target_pairs={{0,1},{1,0},{2,3},{3,2},{4,5},{5,4},{6,7},{7,6},{8,9},{9,8},{10,11... | collective-permute-start | bytes 25165832 | tf_op jit(solution)/shard_map/ppermute | solution.py:189
  387.8 19.5 %collective-permute-start.6 = (bf16[2,1024,1024]{2,1,0:T(8,128)(2,1)}, bf16[2,1024,1024]{2,1,0:T(8,128)(2,1)}, u32[]{:S(2)}, u32[]{:S(2)}) collective-permute-start(bf16[2,1024,1024]{2,1,0:T(8,128)(2,1)} %pad_maximum_fusion.xd0_ref), channel_id=1, source_target_pairs={{0,1},{1,0},{2,3},{3,2},{4,5},{5,4},{6,7},{7,6},{8,9},{9,8},{10,11... | collective-permute-start | bytes 12582920 | tf_op jit(solution)/shard_map/ppermute | solution.py:189
  388.3 135.7 %collective-permute-start.14 = (bf16[2,1024,1024]{2,1,0:T(8,128)(2,1)}, bf16[2,1024,1024]{2,1,0:T(8,128)(2,1)}, u32[]{:S(2)}, u32[]{:S(2)}) collective-permute-start(bf16[2,1024,1024]{2,1,0:T(8,128)(2,1)} %pad_maximum_fusion.1.xd0_ref), channel_id=1, source_target_pairs={{0,1},{1,0},{2,3},{3,2},{4,5},{5,4},{6,7},{7,6},{8,9},{9,8},{10,11... | collective-permute-start | bytes 12582920 | tf_op jit(solution)/shard_map/ppermute | solution.py:189
  468.7 239.3 %collective-permute-start.9 = (f32[2,1024,1024]{2,1,0:T(8,128)}, f32[2,1024,1024]{2,1,0:T(8,128)}, u32[]{:S(2)}, u32[]{:S(2)}) collective-permute-start(f32[2,1024,1024]{2,1,0:T(8,128)} %get-tuple-element.91), channel_id=1, source_target_pairs={{0,1},{1,0},{2,3},{3,2},{4,5},{5,4},{6,7},{7,6},{8,9},{9,8},{10,11... | collective-permute-start | bytes 25165832 | tf_op jit(solution)/shard_map/ppermute | solution.py:189
  479.1 137.7 %collective-permute-start.11 = (bf16[2,1024,1024]{2,1,0:T(8,128)(2,1)}, bf16[2,1024,1024]{2,1,0:T(8,128)(2,1)}, u32[]{:S(2)}, u32[]{:S(2)}) collective-permute-start(bf16[2,1024,1024]{2,1,0:T(8,128)(2,1)} %collective-permute-done.xd0_ref), channel_id=1, source_target_pairs={{0,4},{1,5},{2,6},{3,7},{4,0},{5,1},{6,2},{7,3},{8,12},{9,13},{10,... | collective-permute-start | bytes 12582920 | tf_op jit(solution)/shard_map/ppermute | solution.py:189
  585.6 233.8 %collective-permute-start.19 = (f32[2,1024,1024]{2,1,0:T(8,128)}, f32[2,1024,1024]{2,1,0:T(8,128)}, u32[]{:S(2)}, u32[]{:S(2)}) collective-permute-start(f32[2,1024,1024]{2,1,0:T(8,128)} %get-tuple-element.113), channel_id=1, source_target_pairs={{0,1},{1,0},{2,3},{3,2},{4,5},{5,4},{6,7},{7,6},{8,9},{9,8},{10,11... | collective-permute-start | bytes 25165832 | tf_op jit(solution)/shard_map/ppermute | solution.py:189
  585.8 122.2 %collective-permute-start.17 = (bf16[2,1024,1024]{2,1,0:T(8,128)(2,1)}, bf16[2,1024,1024]{2,1,0:T(8,128)(2,1)}, u32[]{:S(2)}, u32[]{:S(2)}) collective-permute-start(bf16[2,1024,1024]{2,1,0:T(8,128)(2,1)} %collective-permute-done.7.xd0_ref), channel_id=1, source_target_pairs={{0,2},{1,3},{2,0},{3,1},{4,6},{5,7},{6,4},{7,5},{8,10},{9,11},{10,... | collective-permute-start | bytes 12582920 | tf_op jit(solution)/shard_map/ppermute | solution.py:189
  616.9 103.3 %collective-permute-start.12 = (bf16[2,1024,1024]{2,1,0:T(8,128)(2,1)}, bf16[2,1024,1024]{2,1,0:T(8,128)(2,1)}, u32[]{:S(2)}, u32[]{:S(2)}) collective-permute-start(bf16[2,1024,1024]{2,1,0:T(8,128)(2,1)} %collective-permute-done.11.xd0_ref), channel_id=1, source_target_pairs={{0,1},{1,0},{2,3},{3,2},{4,5},{5,4},{6,7},{7,6},{8,9},{9,8},{10,11... | collective-permute-start | bytes 12582920 | tf_op jit(solution)/shard_map/ppermute | solution.py:189
  708.0 123.6 %collective-permute-start.20 = (bf16[2,1024,1024]{2,1,0:T(8,128)(2,1)}, bf16[2,1024,1024]{2,1,0:T(8,128)(2,1)}, u32[]{:S(2)}, u32[]{:S(2)}) collective-permute-start(bf16[2,1024,1024]{2,1,0:T(8,128)(2,1)} %collective-permute-done.17.xd0_ref), channel_id=1, source_target_pairs={{0,1},{1,0},{2,3},{3,2},{4,5},{5,4},{6,7},{7,6},{8,9},{9,8},{10,11... | collective-permute-start | bytes 12582920 | tf_op jit(solution)/shard_map/ppermute | solution.py:189
  781.5 214.7 %collective-permute-start.15 = (f32[2,1024,1024]{2,1,0:T(8,128)}, f32[2,1024,1024]{2,1,0:T(8,128)}, u32[]{:S(2)}, u32[]{:S(2)}) collective-permute-start(f32[2,1024,1024]{2,1,0:T(8,128)} %get-tuple-element.107), channel_id=1, source_target_pairs={{0,1},{1,0},{2,3},{3,2},{4,5},{5,4},{6,7},{7,6},{8,9},{9,8},{10,11... | collective-permute-start | bytes 25165832 | tf_op jit(solution)/shard_map/ppermute | solution.py:189
  792.3 118.7 %collective-permute-start.16 = (bf16[2,1024,1024]{2,1,0:T(8,128)(2,1)}, bf16[2,1024,1024]{2,1,0:T(8,128)(2,1)}, u32[]{:S(2)}, u32[]{:S(2)}) collective-permute-start(bf16[2,1024,1024]{2,1,0:T(8,128)(2,1)} %pad_maximum_fusion.xd0_ref), channel_id=1, source_target_pairs={{0,4},{1,5},{2,6},{3,7},{4,0},{5,1},{6,2},{7,3},{8,12},{9,13},{10,... | collective-permute-start | bytes 12582920 | tf_op jit(solution)/shard_map/ppermute | solution.py:189
  892.9 187.5 %collective-permute-start.25 = (f32[2,1024,1024]{2,1,0:T(8,128)}, f32[2,1024,1024]{2,1,0:T(8,128)}, u32[]{:S(2)}, u32[]{:S(2)}) collective-permute-start(f32[2,1024,1024]{2,1,0:T(8,128)} %get-tuple-element.128), channel_id=1, source_target_pairs={{0,1},{1,0},{2,3},{3,2},{4,5},{5,4},{6,7},{7,6},{8,9},{9,8},{10,11... | collective-permute-start | bytes 25165832 | tf_op jit(solution)/shard_map/ppermute | solution.py:189
  893.1 101.4 %collective-permute-start.26 = (bf16[2,1024,1024]{2,1,0:T(8,128)(2,1)}, bf16[2,1024,1024]{2,1,0:T(8,128)(2,1)}, u32[]{:S(2)}, u32[]{:S(2)}) collective-permute-start(bf16[2,1024,1024]{2,1,0:T(8,128)(2,1)} %pad_maximum_fusion.1.xd0_ref), channel_id=1, source_target_pairs={{0,2},{1,3},{2,0},{3,1},{4,6},{5,7},{6,4},{7,5},{8,10},{9,11},{10,... | collective-permute-start | bytes 12582920 | tf_op jit(solution)/shard_map/ppermute | solution.py:189
  910.9 97.4 %collective-permute-start.18 = (bf16[2,1024,1024]{2,1,0:T(8,128)(2,1)}, bf16[2,1024,1024]{2,1,0:T(8,128)(2,1)}, u32[]{:S(2)}, u32[]{:S(2)}) collective-permute-start(bf16[2,1024,1024]{2,1,0:T(8,128)(2,1)} %collective-permute-done.16.xd0_ref), channel_id=1, source_target_pairs={{0,1},{1,0},{2,3},{3,2},{4,5},{5,4},{6,7},{7,6},{8,9},{9,8},{10,11... | collective-permute-start | bytes 12582920 | tf_op jit(solution)/shard_map/ppermute | solution.py:189
  994.5 129.0 %collective-permute-start.27 = (bf16[2,1024,1024]{2,1,0:T(8,128)(2,1)}, bf16[2,1024,1024]{2,1,0:T(8,128)(2,1)}, u32[]{:S(2)}, u32[]{:S(2)}) collective-permute-start(bf16[2,1024,1024]{2,1,0:T(8,128)(2,1)} %collective-permute-done.26.xd0_ref), channel_id=1, source_target_pairs={{0,1},{1,0},{2,3},{3,2},{4,5},{5,4},{6,7},{7,6},{8,9},{9,8},{10,11... | collective-permute-start | bytes 12582920 | tf_op jit(solution)/shard_map/ppermute | solution.py:189
  994.5 190.8 %collective-permute-start.31 = (f32[1024,1024]{1,0:T(8,128)}, f32[1024,1024]{1,0:T(8,128)}, u32[]{:S(2)}, u32[]{:S(2)}) collective-permute-start(f32[1024,1024]{1,0:T(8,128)} %get-tuple-element.139), channel_id=1, source_target_pairs={{0,2},{1,3},{2,0},{3,1},{4,6},{5,7},{6,4},{7,5},{8,10},{9,11},{10,... | collective-permute-start | bytes 12582920 | tf_op jit(solution)/shard_map/ppermute | solution.py:189
  1069.9 256.8 %collective-permute-start.21 = (f32[2,1024,1024]{2,1,0:T(8,128)}, f32[2,1024,1024]{2,1,0:T(8,128)}, u32[]{:S(2)}, u32[]{:S(2)}) collective-permute-start(f32[2,1024,1024]{2,1,0:T(8,128)} %get-tuple-element.123), channel_id=1, source_target_pairs={{0,1},{1,0},{2,3},{3,2},{4,5},{5,4},{6,7},{7,6},{8,9},{9,8},{10,11... | collective-permute-start | bytes 25165832 | tf_op jit(solution)/shard_map/ppermute | solution.py:189
  1092.6 122.6 %collective-permute-start.22 = (f32[1024,1024]{1,0:T(8,128)}, f32[1024,1024]{1,0:T(8,128)}, u32[]{:S(2)}, u32[]{:S(2)}) collective-permute-start(f32[1024,1024]{1,0:T(8,128)} %get-tuple-element.124), channel_id=1, source_target_pairs={{0,2},{1,3},{2,0},{3,1},{4,6},{5,7},{6,4},{7,5},{8,10},{9,11},{10,... | collective-permute-start | bytes 12582920 | tf_op jit(solution)/shard_map/ppermute | solution.py:189
  1184.8 200.7 %collective-permute-start.28 = (f32[2,1024,1024]{2,1,0:T(8,128)}, f32[2,1024,1024]{2,1,0:T(8,128)}, u32[]{:S(2)}, u32[]{:S(2)}) collective-permute-start(f32[2,1024,1024]{2,1,0:T(8,128)} %get-tuple-element.136), channel_id=1, source_target_pairs={{0,1},{1,0},{2,3},{3,2},{4,5},{5,4},{6,7},{7,6},{8,9},{9,8},{10,11... | collective-permute-start | bytes 25165832 | tf_op jit(solution)/shard_map/ppermute | solution.py:189
  1185.0 119.9 %collective-permute-start.32 = (f32[1024,1024]{1,0:T(8,128)}, f32[1024,1024]{1,0:T(8,128)}, u32[]{:S(2)}, u32[]{:S(2)}) collective-permute-start(f32[1024,1024]{1,0:T(8,128)} %get-tuple-element.140), channel_id=1, source_target_pairs={{0,2},{1,3},{2,0},{3,1},{4,6},{5,7},{6,4},{7,5},{8,10},{9,11},{10,... | collective-permute-start | bytes 12582920 | tf_op jit(solution)/shard_map/ppermute | solution.py:189
  1185.3 129.6 %collective-permute-start.29 = (f32[1024,1024]{1,0:T(8,128)}, f32[1024,1024]{1,0:T(8,128)}, u32[]{:S(2)}, u32[]{:S(2)}) collective-permute-start(f32[1024,1024]{1,0:T(8,128)} %get-tuple-element.137), channel_id=1, source_target_pairs={{0,4},{1,5},{2,6},{3,7},{4,0},{5,1},{6,2},{7,3},{8,12},{9,13},{10,... | collective-permute-start | bytes 12582920 | tf_op jit(solution)/shard_map/ppermute | solution.py:189
  1215.2 155.0 %collective-permute-start.35 = (f32[1024,1024]{1,0:T(8,128)}, f32[1024,1024]{1,0:T(8,128)}, u32[]{:S(2)}, u32[]{:S(2)}) collective-permute-start(f32[1024,1024]{1,0:T(8,128)} %get-tuple-element.143), channel_id=1, source_target_pairs={{0,4},{1,5},{2,6},{3,7},{4,0},{5,1},{6,2},{7,3},{8,12},{9,13},{10,... | collective-permute-start | bytes 12582920 | tf_op jit(solution)/shard_map/ppermute | solution.py:189
  1304.9 155.3 %collective-permute-start.34 = (f32[1024,1024]{1,0:T(8,128)}, f32[1024,1024]{1,0:T(8,128)}, u32[]{:S(2)}, u32[]{:S(2)}) collective-permute-start(f32[1024,1024]{1,0:T(8,128)} %get-tuple-element.142), channel_id=1, source_target_pairs={{0,4},{1,5},{2,6},{3,7},{4,0},{5,1},{6,2},{7,3},{8,12},{9,13},{10,... | collective-permute-start | bytes 12582920 | tf_op jit(solution)/shard_map/ppermute | solution.py:189
  1314.9 145.8 %collective-permute-start.39 = (f32[4,512,512]{2,1,0:T(8,128)}, f32[4,512,512]{2,1,0:T(8,128)}, u32[]{:S(2)}, u32[]{:S(2)}) collective-permute-start(f32[4,512,512]{2,1,0:T(8,128)} %constant_dynamic-slice_fusion), channel_id=1, source_target_pairs={{0,8},{8,0},{1,9},{9,1},{2,10},{10,2},{3,11},{11,3},{4,12},{12,4},... | collective-permute-start | bytes 12582920 | tf_op jit(solution)/shard_map/ppermute | solution.py:176
  1326.7 181.6 %collective-permute-start.38 = (f32[4,512,512]{2,1,0:T(8,128)}, f32[4,512,512]{2,1,0:T(8,128)}, u32[]{:S(2)}, u32[]{:S(2)}) collective-permute-start(f32[4,512,512]{2,1,0:T(8,128)} %constant_dynamic-slice_fusion.1), channel_id=1, source_target_pairs={{0,8},{8,0},{1,9},{9,1},{2,10},{10,2},{3,11},{11,3},{4,12},{12,4},... | collective-permute-start | bytes 12582920 | tf_op jit(solution)/shard_map/ppermute | solution.py:176
  1370.2 314.9 %collective-permute-start.37 = (f32[4,512,512]{2,1,0:T(8,128)}, f32[4,512,512]{2,1,0:T(8,128)}, u32[]{:S(2)}, u32[]{:S(2)}) collective-permute-start(f32[4,512,512]{2,1,0:T(8,128)} %constant_dynamic-slice_fusion.2), channel_id=1, source_target_pairs={{0,8},{8,0},{1,9},{9,1},{2,10},{10,2},{3,11},{11,3},{4,12},{12,4},... | collective-permute-start | bytes 12582920 | tf_op jit(solution)/shard_map/ppermute | solution.py:176
  1385.5 301.9 %collective-permute-start.33 = (f32[1024,1024]{1,0:T(8,128)}, f32[1024,1024]{1,0:T(8,128)}, u32[]{:S(2)}, u32[]{:S(2)}) collective-permute-start(f32[1024,1024]{1,0:T(8,128)} %get-tuple-element.157), channel_id=1, source_target_pairs={{0,4},{1,5},{2,6},{3,7},{4,0},{5,1},{6,2},{7,3},{8,12},{9,13},{10,... | collective-permute-start | bytes 12582920 | tf_op jit(solution)/shard_map/ppermute | solution.py:189
  1386.9 127.6 %copy-start.25 = (f32[32]{0:T(128)S(1)}, f32[32]{0:T(128)}, u32[]{:S(2)}) copy-start(f32[32]{0:T(128)} %get-tuple-element.193) | copy-start | bytes 388
  1386.9 127.6 %copy-start.26 = (f32[32]{0:T(128)S(1)}, f32[32]{0:T(128)}, u32[]{:S(2)}) copy-start(f32[32]{0:T(128)} %get-tuple-element.207) | copy-start | bytes 388
  1386.9 298.0 %copy-start.5 = (f32[32,2048]{1,0:T(8,128)S(1)}, f32[32,2048]{1,0:T(8,128)}, u32[]{:S(2)}) copy-start(f32[32,2048]{1,0:T(8,128)} %copy-done.4) | copy-start | bytes 786436
  1387.0 298.0 %copy-start.12 = (f32[2048]{0:T(1024)S(1)}, f32[2048]{0:T(1024)}, u32[]{:S(2)}) copy-start(f32[2048]{0:T(1024)} %copy-done.11) | copy-start | bytes 24580
  1387.0 298.0 %copy-start.14 = (f32[2048]{0:T(1024)S(1)}, f32[2048]{0:T(1024)}, u32[]{:S(2)}) copy-start(f32[2048]{0:T(1024)} %copy-done.13) | copy-start | bytes 24580
  1460.1 252.5 %collective-permute-start.36 = (f32[1024,1024]{1,0:T(8,128)}, f32[1024,1024]{1,0:T(8,128)}, u32[]{:S(2)}, u32[]{:S(2)}) collective-permute-start(f32[1024,1024]{1,0:T(8,128)} %get-tuple-element.159), channel_id=1, source_target_pairs={{0,2},{1,3},{2,0},{3,1},{4,6},{5,7},{6,4},{7,5},{8,10},{9,11},{10,... | collective-permute-start | bytes 12582920 | tf_op jit(solution)/shard_map/ppermute | solution.py:189
  1460.7 259.8 %collective-permute-start.10 = (f32[1024,1024]{1,0:T(8,128)}, f32[1024,1024]{1,0:T(8,128)}, u32[]{:S(2)}, u32[]{:S(2)}) collective-permute-start(f32[1024,1024]{1,0:T(8,128)} %get-tuple-element.93), channel_id=1, source_target_pairs={{0,2},{1,3},{2,0},{3,1},{4,6},{5,7},{6,4},{7,5},{8,10},{9,11},{10,... | collective-permute-start | bytes 12582920 | tf_op jit(solution)/shard_map/ppermute | solution.py:189
  1508.3 212.1 %collective-permute-start.23 = (f32[1024,1024]{1,0:T(8,128)}, f32[1024,1024]{1,0:T(8,128)}, u32[]{:S(2)}, u32[]{:S(2)}) collective-permute-start(f32[1024,1024]{1,0:T(8,128)} %get-tuple-element.158), channel_id=1, source_target_pairs={{0,4},{1,5},{2,6},{3,7},{4,0},{5,1},{6,2},{7,3},{8,12},{9,13},{10,... | collective-permute-start | bytes 12582920 | tf_op jit(solution)/shard_map/ppermute | solution.py:189
  1511.1 173.7 %all-to-all-start.1 = ((f32[8,4,2048]{2,1,0:T(4,128)}), f32[8,4,2048]{2,1,0:T(4,128)S(1)}, u32[]{:S(2)}, u32[]{:S(2)}) async-start(f32[8,4,2048]{2,1,0:T(4,128)} %bitcast.55), calls=%async_computation.1 | async-start | bytes 524288 | tf_op jit(solution)/shard_map/all_to_all | solution.py:274
  1514.5 272.0 %all-reduce.2.cloned.1.call-start = ((), (), s32[]{:S(2)}) async-start(), calls=%async_computation.2 | async-start | bytes 262144 | tf_op jit(solution)/shard_map/psum | solution.py:278
  1685.1 93.3 %collective-permute-start.24 = (f32[1024,1024]{1,0:T(8,128)}, f32[1024,1024]{1,0:T(8,128)}, u32[]{:S(2)}, u32[]{:S(2)}) collective-permute-start(f32[1024,1024]{1,0:T(8,128)} %get-tuple-element.126), channel_id=1, source_target_pairs={{0,4},{1,5},{2,6},{3,7},{4,0},{5,1},{6,2},{7,3},{8,12},{9,13},{10,... | collective-permute-start | bytes 12582920 | tf_op jit(solution)/shard_map/ppermute | solution.py:189
  1687.4 91.9 %collective-permute-start.30 = (f32[1024,1024]{1,0:T(8,128)}, f32[1024,1024]{1,0:T(8,128)}, u32[]{:S(2)}, u32[]{:S(2)}) collective-permute-start(f32[1024,1024]{1,0:T(8,128)} %get-tuple-element.160), channel_id=1, source_target_pairs={{0,2},{1,3},{2,0},{3,1},{4,6},{5,7},{6,4},{7,5},{8,10},{9,11},{10,... | collective-permute-start | bytes 12582920 | tf_op jit(solution)/shard_map/ppermute | solution.py:189
  (28 other events, 1090.1 us)
Sparse Core Ops, SparseCore 0:
  1691.7 63.0 all-reduce.1

commit v2 on v0

v2 whole, which is shorter than its diff:
```python
import functools

import jax
import jax.numpy as jnp
from jax import lax
from jax.experimental import pallas as pl
from jax.experimental.pallas import tpu as pltpu
from jax.sharding import PartitionSpec as P


AUX_COEF = 0.01
BLK = 1024
TILE = 256
X, Y = 2, 4
F32 = jnp.float32
BF16 = jnp.bfloat16


def dot(a, b, ca, cb):
    return lax.dot_general(a, b, (((ca,), (cb,)), ((), ())), preferred_element_type=F32)


def expert_kernel(n_blk, n_exp, fresh, nt_ref, pos_ref, gate_ref, wg0_ref, wg1_ref, wu0_ref, wu1_ref, wd0_ref, wd1_ref, *rest):
    n_pair = n_exp // 2
    rest = list(rest)
    take = lambda n: [rest.pop(0) for _ in range(n)]
    tok_in_refs = take(n_blk)
    acc_in_refs = [None if fresh[p] else take(2) for p in range(n_pair)]
    tok_out_refs = take(n_blk)
    dgate_ref, = take(1)
    acc_out_refs = [take(2) for _ in range(n_pair)]
    xd_ref, yd_ref, acc_ref, in_sem, out_sem, acc_in_sem, acc_out_sem = rest
    b = pl.program_id(0)
    e = pl.program_id(1)
    half = xd_ref.shape[3] // 2
    tok_in = [pltpu.make_async_copy(src, xd_ref.at[k % 2], in_sem.at[k]) for k, src in enumerate(tok_in_refs)]
    tok_out = [pltpu.make_async_copy(yd_ref.at[k % 2], dst, out_sem.at[k]) for k, dst in enumerate(tok_out_refs)]

    def acc_in(k):
        return [pltpu.make_async_copy(acc_in_refs[k // 2][s].at[k % 2], acc_ref.at[k, s], acc_in_sem.at[k, s]) for s in range(2)]

    def acc_out(k):
        return [pltpu.make_async_copy(acc_ref.at[k, s], acc_out_refs[k // 2][s].at[k % 2], acc_out_sem.at[k, s]) for s in range(2)]

    @pl.when((b == 0) & (e == 0))
    def _():
        tok_in[0].start()
        if not fresh[0]:
            for c in acc_in(0):
                c.start()

    for k in range(n_exp):
        @pl.when((b == 0) & (e == k))
        def _():
            if k + 1 < n_exp and not fresh[(k + 1) // 2]:
                for c in acc_in(k + 1):
                    c.start()
            if k == n_exp // 2 - 1:
                tok_in[1].start()

    for k in range(n_blk):
        @pl.when((b == k) & (e == 0))
        def _():
            tok_in[k].wait()
            if 1 <= k < n_blk - 1:
                tok_in[k + 1].start()
            if k >= 2:
                tok_out[k - 2].wait()

    slot = b % 2

    @pl.when(e == 0)
    def _():
        yd_ref[slot] = jnp.zeros(yd_ref.shape[1:], F32)

    def acc_ready():
        for k in range(n_exp):
            @pl.when((b == 0) & (e == k))
            def _():
                if fresh[k // 2]:
                    acc_ref[k] = jnp.zeros(acc_ref.shape[1:], F32)
                else:
                    for c in acc_in(k):
                        c.wait()

    dgate_ref[...] = jnp.zeros(dgate_ref.shape, F32)
    wg, wu, wd = (wg0_ref, wg1_ref), (wu0_ref, wu1_ref), (wd0_ref, wd1_ref)
    cols = (slice(0, half), slice(half, 2 * half))

    gate_row = gate_ref[0, 0]

    def tile(base, size, first):
        pos = pos_ref[0, 0]
        rows = (lax.broadcasted_iota(jnp.int32, (size, BLK), 0) + base).astype(F32)
        hit = rows == pos
        pick = jnp.where(hit, 1.0, 0.0).astype(BF16)
        gate_c = jnp.sum(jnp.where(hit, gate_row, 0.0), axis=1, keepdims=True)
        xc = [dot(pick, xd_ref[slot, 0, :, c], 1, 0).astype(BF16) for c in cols]
        dyc = [dot(pick, xd_ref[slot, 1, :, c], 1, 0) for c in cols]
        hg = dot(xc[0], wg[0][0], 1, 0) + dot(xc[1], wg[1][0], 1, 0)
        hu = dot(xc[0], wu[0][0], 1, 0) + dot(xc[1], wu[1][0], 1, 0)
        sig = jax.nn.sigmoid(hg)
        act = (hg * sig * hu).astype(BF16)
        do = [(gate_c * d).astype(BF16) for d in dyc]
        da = (dot(do[0], wd[0][0], 1, 1) + dot(do[1], wd[1][0], 1, 1)).astype(BF16).astype(F32)
        dhg = (da * hu * sig * (1.0 + hg * (1.0 - sig))).astype(BF16)
        dhu = (da * hg * sig).astype(BF16)
        o = [dot(act, w[0], 1, 0).astype(BF16) for w in wd]
        dgate_c = sum(jnp.sum(dyc[s] * o[s].astype(F32), axis=1, keepdims=True) for s in range(2))
        dgate_ref[0, 0] += jnp.sum(jnp.where(hit, dgate_c, 0.0), axis=0, keepdims=True)
        db = [(dot(dhg, wg[s][0], 1, 1) + dot(dhu, wu[s][0], 1, 1)).astype(BF16) for s in range(2)]
        pl.when(first)(acc_ready)
        for s in range(2):
            acc_ref[e, s, 0] += dot(xc[s], dhg, 0, 0)
            acc_ref[e, s, 1] += dot(xc[s], dhu, 0, 0)
            acc_ref[e, s, 2] += dot(act, do[s], 0, 0)
        gate_t = jnp.transpose(jnp.broadcast_to(gate_row, (8, BLK)))[:, :1]
        width = 256
        for s in range(2):
            for c in range(half // width):
                part = slice(c * width, (c + 1) * width)
                out = slice(s * half + c * width, s * half + (c + 1) * width)
                yd_ref[slot, 0, :, out] += gate_t * dot(pick, o[s][:, part], 0, 0)
                yd_ref[slot, 1, :, out] += dot(pick, db[s][:, part], 0, 0)

    def full_tile(i, carry):
        tile(i * TILE, TILE, i == 0)
        return carry

    tiles = nt_ref[b, e]
    full = jnp.right_shift(tiles, 1)
    lax.fori_loop(0, full, full_tile, 0)
    pl.when((tiles & 1) == 1)(lambda: tile(full * TILE, TILE // 2, full == 0))
    pl.when(tiles == 0)(acc_ready)

    for k in range(n_blk):
        @pl.when((b == k) & (e == n_exp - 1))
        def _():
            tok_out[k].start()

    for k in range(n_exp):
        @pl.when((b == n_blk - 1) & (e == k))
        def _():
            for c in acc_out(k):
                c.start()

    @pl.when((b == n_blk - 1) & (e == n_exp - 1))
    def _():
        for k in range(max(0, n_blk - 2), n_blk):
            tok_out[k].wait()
        for k in range(n_exp):
            for c in acc_out(k):
                c.wait()


def experts(nt, pos, gate, toks, weights, e0, acc):
    n_blk, n_exp = nt.shape
    d_model = toks[0].shape[2]
    half, d_ff = weights[0].shape[1:]
    row = pl.BlockSpec((1, 1, 1, BLK), lambda b, e, nt: (b, e, 0, 0))
    up = pl.BlockSpec((1, half, d_ff), lambda b, e, nt: (e + e0, 0, 0))
    down = pl.BlockSpec((1, d_ff, half), lambda b, e, nt: (e + e0, 0, 0))
    hbm = pl.BlockSpec(memory_space=pl.ANY)
    fresh = tuple(a is None for a in acc)
    acc_args = [r for a in acc if a is not None for r in a]
    acc_shape = jax.ShapeDtypeStruct((2, 3, half, d_ff), F32)
    first_in = 1 + 8 + n_blk
    first_out = n_blk + 1
    aliases = {}
    for p, a in enumerate(acc):
        if a is not None:
            for s in range(2):
                aliases[first_in] = first_out + 2 * p + s
                first_in += 1
    res = pl.pallas_call(
        functools.partial(expert_kernel, n_blk, n_exp, fresh),
        grid_spec=pltpu.PrefetchScalarGridSpec(
            num_scalar_prefetch=1,
            grid=(n_blk, n_exp),
            in_specs=[row, row, up, up, up, up, down, down] + [hbm] * (n_blk + len(acc_args)),
            out_specs=[hbm] * n_blk + [row] + [hbm] * (2 * len(acc)),
            scratch_shapes=[
                pltpu.VMEM((2, 2, BLK, d_model), BF16),
                pltpu.VMEM((2, 2, BLK, d_model), F32),
                pltpu.VMEM((n_exp, 2, 3, half, d_ff), F32),
                pltpu.SemaphoreType.DMA((n_blk,)),
                pltpu.SemaphoreType.DMA((n_blk,)),
                pltpu.SemaphoreType.DMA((n_exp, 2)),
                pltpu.SemaphoreType.DMA((n_exp, 2)),
            ],
        ),
        out_shape=[jax.ShapeDtypeStruct((2, BLK, d_model), F32)] * n_blk
        + [jax.ShapeDtypeStruct((n_blk, n_exp, 1, BLK), F32)] + [acc_shape] * (2 * len(acc)),
        input_output_aliases=aliases,
        compiler_params=pltpu.CompilerParams(
            dimension_semantics=("arbitrary", "arbitrary"), vmem_limit_bytes=67_000_000),
        cost_estimate=pl.CostEstimate(flops=100_000_000, bytes_accessed=80_000_000, transcendentals=1_000_000),
    )(nt, pos, gate, *weights, *toks, *acc_args)
    toks_out, dgate, acc = res[:n_blk], res[n_blk], res[n_blk + 1:]
    return toks_out, dgate, [acc[2 * p:2 * p + 2] for p in range(len(acc) // 2)]


def by_distance(a, bits):
    rest = a.shape[1:]
    a = a.reshape(2, 2, 2, *rest)
    for axis, bit in enumerate(bits):
        a = jnp.where(bit, jnp.flip(a, axis), a)
    return a.reshape(8, *rest)


def hop(a, bit):
    return lax.ppermute(a, 'ep', [(i, i ^ bit) for i in range(8)])


def hop_z(a):
    return lax.ppermute(a, 'fsdp', [(0, 1), (1, 0)])


def turn(a, f_idx):
    half = a.shape[-1] // 2
    return jnp.where(f_idx == 1, jnp.concatenate([a[..., half:], a[..., :half]], axis=-1), a)


def solution(mesh):
    n_fsdp = mesh.shape['fsdp']
    n_ep = mesh.shape['ep']
    n_dev = n_fsdp * n_ep
    all_axes = ('fsdp', 'ep')
    tok_spec = P(('ep', 'fsdp'), None)
    up_spec = P('ep', 'fsdp', None)
    down_spec = P('ep', None, 'fsdp')

    def local_step(x_loc, dy_loc, ids_loc, slot_loc, w_router, wg_loc, wu_loc, wd_loc):
        tok_dev, _ = x_loc.shape
        top_k = ids_loc.shape[1]
        n_exp = w_router.shape[1]
        local_exp = n_exp // n_ep
        tokens = tok_dev * n_dev
        halves = tok_dev // BLK
        f_idx = lax.axis_index('fsdp')
        ep_idx = lax.axis_index('ep')
        bits = [(ep_idx // d) % 2 == 1 for d in (4, 2, 1)]

        loc = (wg_loc, wu_loc, wd_loc)
        n2 = local_exp // 2
        other_w = [[hop_z(w[p * n2:(p + 1) * n2]) for w in loc] for p in range(2)]

        xd = {(0, h): turn(jnp.stack([x_loc[h * BLK:(h + 1) * BLK], dy_loc[h * BLK:(h + 1) * BLK]]), f_idx) for h in range(2)}
        xd[X, 0] = hop(xd[0, 0], X)
        xd[Y, 1] = hop(xd[0, 1], Y)
        xd[X, 1] = hop(xd[0, 1], X)
        xd[Y, 0] = hop(xd[0, 0], Y)
        xd[X + Y, 1] = hop(xd[Y, 1], X)
        xd[X + Y, 0] = hop(xd[X, 0], Y)

        logits = dot(w_router, x_loc, 0, 1)
        prob = jax.nn.softmax(logits, axis=0)
        expert = jnp.arange(n_exp, dtype=jnp.int32)[None, :, None]
        match = ids_loc.T[:, None, :] == expert
        chosen = jnp.any(match, axis=0)
        kept = jnp.any(match & (slot_loc.T[:, None, :] >= 0), axis=0)
        stat = jnp.stack([jnp.sum(chosen.astype(F32), axis=1), jnp.sum(prob, axis=1)])

        upto = jnp.arange(BLK)[:, None] <= jnp.arange(BLK)[None, :]
        kept_b = kept.astype(BF16).reshape(n_exp * halves, BLK)
        place = dot(kept_b, upto.astype(BF16), 1, 0).reshape(n_exp, tok_dev) - 1.0
        pos = jnp.where(kept, place, -1.0)
        gate = jnp.where(kept, prob, 0.0)
        meta = jnp.stack([pos, gate], axis=1).reshape(n_ep, local_exp, 2, tok_dev)
        own_meta = lax.dynamic_index_in_dim(meta, ep_idx, 0, keepdims=False)
        peer_meta = hop(lax.dynamic_index_in_dim(meta, ep_idx ^ 1, 0, keepdims=False), 1)
        far_meta = lax.all_to_all(meta, 'ep', 0, 0, tiled=True)

        def blocked(m):
            m = m.reshape(-1, local_exp, 2, halves, BLK).transpose(3, 0, 1, 2, 4)
            nt = ((jnp.max(m[..., 0, :], axis=-1) + TILE // 2) / (TILE // 2)).astype(jnp.int32)
            return nt, m[..., 0:1, :], m[..., 1:2, :]

        metas = [blocked(jnp.stack([own_meta, peer_meta])), None]

        def meta_of(sets, e_lo, e_hi):
            out = []
            for j in range(3):
                rows = [metas[k != 0][j][h, k:k + 2, e_lo:e_hi] for k, h in sets]
                out.append(jnp.concatenate(rows, axis=0))
            return out

        own_sets = ((0, 0), (0, 1))
        near = ((X, 0), (Y, 1))
        diag = ((X + Y, 0), (X + Y, 1))
        last = ((Y, 0), (X, 1))
        calls = [(own_sets[:1], 0, 2), (own_sets[1:], 0, 2), (near, 0, 4), (diag, 0, 4), (last, 0, 2), (last, 2, 4), (own_sets, 2, 4)]
        acc = [None, None]
        part, dgate, raw = {}, {}, {}
        first_weights = [w for i, m in enumerate(loc) for w in (m, other_w[0][i])]

        def core_hop(k, h):
            xd[k + 1, h] = hop(xd[k, h], 1)

        for k, h in own_sets:
            core_hop(k, h)

        def reduce_core(n, sets):
            for k, h in sets:
                mine, theirs = raw[n, k, h]
                other = hop(theirs, 1)
                part[n, k, h] = [mine[i] + other[i] for i in range(2)]

        stat_bits = [1, X, Y]
        for n, (sets, e_lo, e_hi) in enumerate(calls):
            nt, pos_k, gate_k = meta_of(sets, e_lo, e_hi)
            if n in (3, 4):
                ready = calls[n - 1][0]
                nt, done = lax.optimization_barrier((nt, [part[n - 1, k, h] for k, h in ready]))
                for (k, h), d in zip(ready, done):
                    part[n - 1, k, h] = d
            toks = [xd[k + c, h] for k, h in sets for c in range(2)]
            pairs = slice(e_lo // 2, e_hi // 2)
            outs, dgate[n], acc[pairs] = experts(
                nt, pos_k, gate_k, toks, first_weights if n < 2 else weights, e_lo, acc[pairs])
            for j, (k, h) in enumerate(sets):
                raw[n, k, h] = outs[2 * j:2 * j + 2]
            if n not in (4, 5):
                reduce_core(n, sets)
            if n == 0:
                xd[X, 0], xd[Y, 1], dgate[n] = lax.optimization_barrier((xd[X, 0], xd[Y, 1], dgate[n]))
                for k, h in near:
                    core_hop(k, h)
            if n == 1:
                far_meta, other_w[1], dgate[n] = lax.optimization_barrier((far_meta, other_w[1], dgate[n]))
                metas[1] = blocked(by_distance(far_meta, bits))
                weights = [w for i, m in enumerate(loc) for w in (m, jnp.concatenate([other_w[0][i], other_w[1][i]], axis=0))]
            if n == 2:
                for k, h in diag + last:
                    xd[k, h], dgate[n] = lax.optimization_barrier((xd[k, h], dgate[n]))
                    core_hop(k, h)
            if n < 4:
                stat, dgate[n] = lax.optimization_barrier((stat, dgate[n]))
                stat = stat + (hop(stat, stat_bits[n]) if n < 3 else hop_z(stat))

        direct = [[hop(part[2, X, 0][i], X), hop(part[2, Y, 1][i], Y)] for i in range(2)]
        diagonal = [[hop(part[3, X + Y, 0][i], X), hop(part[3, X + Y, 1][i], Y)] for i in range(2)]
        ends = [[raw[n, k, h][0] for n in (4, 5)] + [hop(raw[n, k, h][1], 1) for n in (4, 5)] for k, h in last]
        relay = []
        for i in range(2):
            sums = [(m0[i] + o0[i]) + (m1[i] + o1[i]) + d for (m0, m1, o0, o1), d in zip(ends, diagonal[i])]
            ends, sums = lax.optimization_barrier((ends, sums))
            relay.append([hop(sums[0], Y), hop(sums[1], X)])

        grads = []
        for p in range(2):
            got = hop_z(acc[p][1])
            grads.append((acc[p][0] + got).astype(BF16))
        dwg, dwu, dwd = (jnp.concatenate([g[:, i] for g in grads], axis=0) for i in range(3))

        def dgate_of(n):
            d = dgate[n]
            return d.reshape(-1, 2, d.shape[1], BLK)

        far = {}
        for n, sets in ((2, near), (3, diag), (4, last), (5, last)):
            d = dgate_of(n)
            for j, (k, h) in enumerate(sets):
                for c in range(2):
                    far.setdefault((k + c, h), []).append(d[j, c])
        zero = jnp.zeros((local_exp, BLK), F32)
        far = jnp.stack([jnp.concatenate([jnp.concatenate(far.get((k, h), [zero]), axis=0) for h in range(halves)], axis=1) for k in range(n_ep)])
        far = by_distance(far, bits)
        far = lax.all_to_all(far, 'ep', 0, 0, tiled=True)
        own = jnp.concatenate([jnp.concatenate([dgate_of(0), dgate_of(1)], axis=0), dgate_of(6)], axis=2)
        own = own.transpose(1, 2, 0, 3).reshape(2, local_exp, tok_dev)
        peer = hop(own[1], 1)
        far = by_distance(far, bits)
        d_gate = by_distance(jnp.concatenate([own[:1], peer[None], far[2:]], axis=0), bits).reshape(n_exp, tok_dev)

        load_frac = stat[0] / (tokens * top_k)
        aux_loss = AUX_COEF * n_exp * jnp.sum(load_frac * stat[1] / tokens)
        d_prob = d_gate + AUX_COEF * n_exp * load_frac[:, None]
        d_logit = (prob * (d_prob - jnp.sum(prob * d_prob, axis=0, keepdims=True))).astype(BF16)
        dw_router = lax.psum(dot(x_loc, d_logit, 0, 1), all_axes)

        pre = [[part[h, 0, h][i] + part[6, 0, h][i] + direct[i][h] for h in range(2)] for i in range(2)]
        pre = lax.optimization_barrier(pre)
        y = turn(jnp.concatenate([pre[0][h] + relay[0][h] for h in range(2)], axis=0).astype(BF16), f_idx)
        y, pre = lax.optimization_barrier((y, pre))
        dx_exp = jnp.concatenate([pre[1][h] + relay[1][h] for h in range(2)], axis=0)
        dx = (turn(dx_exp, f_idx) + dot(d_logit, w_router, 0, 1)).astype(BF16)
        return y, aux_loss, dx, dw_router, dwg, dwu, dwd

    return jax.shard_map(local_step, mesh=mesh,
                         in_specs=(tok_spec, tok_spec, tok_spec, tok_spec, P(), up_spec, up_spec, down_spec),
                         out_specs=(tok_spec, P(), tok_spec, P(), up_spec, up_spec, down_spec),
                         check_vma=False)
```

time: 3060 us -> 1480 us (0.48)
  local copies, waits for them, and re-layouts: 1190 us -> 49.9 us
  Pallas kernels: 0 us -> 456 us
  matrix products: 384 us -> 12.3 us
  blocking collectives: 334 us -> 0 us
  waiting for transfers between devices: 763 us -> 499 us
  starting transfers between devices: 31.9 us -> 241 us
  other arithmetic: 320 us -> 192 us
    gather x10 -> x0, local copies, waits for them, and re-layouts: 1130 us -> none  [the longest x1 340 us: local_step(): jnp.take(d_back, dest_row, axis=0, mode='fill', fill_value=0)]
    all_to_all x4 -> x2, waiting for transfers between devices: 684 us -> 88.7 us  [the longest x1 48.8 us: local_step(): far = lax.all_to_all(far, 'ep', 0, 0, tiled=True)]
    pallas_call x0 -> x7, Pallas kernels: none -> 456 us  [experts(): pl.pallas_call(functools.partial(expert_kernel, n_blk, n_exp, fresh), gri...]
    ppermute x0 -> x52, waiting for transfers between devices: none -> 410 us  [the longest x43 347 us: hop(): return lax.ppermute(a, 'ep', [(i, i ^ bit) for i in range(8)])]
    dot_general x13 -> x4, matrix products: 384 us -> 12.3 us  [dot(): lax.dot_general(a, b, (((ca,), (cb,)), ((), ())), preferred_element_type=...]
    psum x1 -> x0, blocking collectives: 334 us -> none  [local_step(): lax.psum(jnp.stack([counts, jnp.sum(prob_all, axis=0)]), all_axes)]
    ppermute x0 -> x52, starting transfers between devices: none -> 231 us  [the longest x43 209 us: hop(): return lax.ppermute(a, 'ep', [(i, i ^ bit) for i in range(8)])]
    scatter-add x2 -> x0, other arithmetic: 199 us -> none  [the longest x1 113 us: local_step(): jax.ops.segment_sum(jnp.ones(flat_ids.shape, jnp.float32), flat_ids, num_...]
  transfers between devices with their start and end apart: 11 -> 55, of which waited for: 5 -> 21; matrix products, arithmetic and copies ran while one was open for 51% -> 17% of each run, Pallas kernels for 0% -> 31%
where the time goes in v2:
time: 1480 us; the launch traced here: 1470 us
  waiting for transfers between devices  499 us (34%)
  Pallas kernels  456 us (31%)
  starting transfers between devices  241 us (16%)
  other arithmetic  192 us (13%)
  local copies, waits for them, and re-layouts  49.9 us (3%)
  between operations  17.2 us (1%)
    pallas_call x7, Pallas kernels, experts(): pl.pallas_call(functools.partial(expert_kernel, n_blk, n_exp, fresh), gri...  456 us
    ppermute x43, waiting for transfers between devices, hop(): return lax.ppermute(a, 'ep', [(i, i ^ bit) for i in range(8)])  347 us
    ppermute x43, starting transfers between devices, hop(): return lax.ppermute(a, 'ep', [(i, i ^ bit) for i in range(8)])  209 us
    ppermute x9, waiting for transfers between devices, hop_z(): return lax.ppermute(a, 'fsdp', [(0, 1), (1, 0)])  62.5 us
    all_to_all x1, waiting for transfers between devices, local_step(): far = lax.all_to_all(far, 'ep', 0, 0, tiled=True)  48.8 us
    add x4, other arithmetic, reduce_core(): part[n, k, h] = [mine[i] + other[i] for i in range(2)]  48.5 us
    all_to_all x1, waiting for transfers between devices, local_step(): far_meta = lax.all_to_all(meta, 'ep', 0, 0, tiled=True)  39.9 us
    add x2, other arithmetic, local_step(): part[h, 0, h][i] + part[6, 0, h][i] + direct[i][h]  39.4 us
  transfers between devices with their start and end apart: 55, of which 21 were waited for; matrix products, arithmetic and copies ran while one was open for 17% of the time, Pallas kernels for 31%

profile of v2, /device:TPU:0, one launch (start us, length us, event | category | flops | bytes accessed | tf_op | source)
XLA Modules:
  0.0 1467.5 jit_solution(6705524201563645328)
XLA Ops:
  7.2 3.9 slice_bitcast_fusion.2
  47.6 22.1 %collective-permute-done.2.wu1_ref = bf16[2,512,512]{2,1,0:T(8,128)(2,1)S(1)} collective-permute-done((bf16[2,512,512]{2,1,0:T(8,128)(2,1)S(1)}, bf16[2,512,512]{2,1,0:T(8,128)(2,1)S(1)}, u32[]{:S(2)}, u32[]{:S(2)}) %collective-permute-start.2) | collective-permute-done | bytes 1048608 | tf_op jit(solution)/shard_map/ppermute | solution.py:216
  72.4 22.5 %collective-permute-done.3.wd1_ref = bf16[2,512,512]{2,1,0:T(8,128)(2,1)} collective-permute-done((bf16[2,512,512]{2,1,0:T(8,128)(2,1)S(1)}, bf16[2,512,512]{2,1,0:T(8,128)(2,1)}, u32[]{:S(2)}, u32[]{:S(2)}) %collective-permute-start.3) | collective-permute-done | bytes 1048608 | tf_op jit(solution)/shard_map/ppermute | solution.py:216
  98.0 35.1 %shard_map.135 = (f32[2,1024,1024]{2,1,0:T(8,128)}, f32[2,1024,1024]{2,1,0:T(8,128)}, f32[2,2,1,1024]{3,2,1,0:T(1,128)}, f32[2,3,512,512]{3,2,1,0:T(8,128)}, f32[2,3,512,512]{3,2,1,0:T(8,128)}) custom-call(s32[2,2]{1,0:T(2,128)} %get-tuple-element.306.nt_ref, f32[2,2,1,1024]{3,2,1,0:T(1,128)} %get-tuple-element.276.pos_ref, ...), custom_call_target="tpu_custom_call" | custom-call | flops 100000000 | bytes 80000000 | tf_op jit(solution)/shard_map/pallas_call | solution.py:175
  141.9 4.2 all-to-all-start
  151.7 35.5 %shard_map.136 = (f32[2,1024,1024]{2,1,0:T(8,128)}, f32[2,1024,1024]{2,1,0:T(8,128)}, f32[2,2,1,1024]{3,2,1,0:T(1,128)}, f32[2,3,512,512]{3,2,1,0:T(8,128)}, f32[2,3,512,512]{3,2,1,0:T(8,128)}) custom-call(s32[2,2]{1,0:T(2,128)} %get-tuple-element.304.nt_ref, ...), custom_call_target="tpu_custom_call", output_to_operand_aliasing={{3}: (11, {}), {4}: (12, {})} | custom-call | flops 100000000 | bytes 80000000 | tf_op jit(solution)/shard_map/pallas_call | solution.py:175
  187.3 10.8 collective-permute-start.10
  198.0 39.9 %all-to-all-done = f32[8,4,2,2048]{3,2,1,0:T(2,128)} async-done(((f32[8,4,2,2048]{3,2,1,0:T(2,128)}), f32[8,4,2,2048]{3,2,1,0:T(2,128)}, u32[]{:S(2)}, u32[]{:S(2)}) %all-to-all-start) | async-done | bytes 524320 | tf_op jit(solution)/shard_map/all_to_all | solution.py:272
  251.4 103.7 %shard_map.137 = (f32[2,1024,1024]{2,1,0:T(8,128)}, f32[2,1024,1024]{2,1,0:T(8,128)}, f32[2,1024,1024]{2,1,0:T(8,128)}, f32[2,1024,1024]{2,1,0:T(8,128)}, f32[4,...) custom-call(s32[4,4]{1,0:T(4,128)} %pad_add_fusion.2.nt_ref, ...), custom_call_target="tpu_custom_call", output_to_operand_aliasing={{5}: (13, {}), {6}: (14, {})} | custom-call | flops 100000000 | bytes 80000000 | tf_op jit(solution)/shard_map/pallas_call | solution.py:175
  355.1 13.5 collective-permute-start.20
  368.7 23.3 %collective-permute-start.18 = (bf16[2,1024,1024]{2,1,0:T(8,128)(2,1)}, bf16[2,1024,1024]{2,1,0:T(8,128)(2,1)}, u32[]{:S(2)}, u32[]{:S(2)}) collective-permute-start(bf16[2,1024,1024]{2,1,0:T(8,128)(2,1)} %fusion.5.rest_0_.rest_2_), channel_id=1, source_target_pairs={{0,2},{1,3},{2,0},{3,1},{4,6},{5,7},{6,4},{7,5},{8,10},{9,11},{10,... | collective-permute-start | bytes 12582920 | tf_op jit(solution)/shard_map/ppermute | solution.py:212
  394.1 22.9 %collective-permute-start.42 = (f32[2,32]{1,0:T(2,128)S(1)}, f32[2,32]{1,0:T(2,128)S(1)}, u32[]{:S(2)}, u32[]{:S(2)}) collective-permute-start(f32[2,32]{1,0:T(2,128)S(1)} %add.318), channel_id=1, source_target_pairs={{0,2},{1,3},{2,0},{3,1},{4,6},{5,7},{6,4},{7,5},{8,10},{9,11},{10,... | collective-permute-start | bytes 776 | tf_op jit(solution)/shard_map/ppermute | solution.py:212
  417.1 66.0 %collective-permute-done.42 = f32[2,32]{1,0:T(2,128)S(1)} collective-permute-done((f32[2,32]{1,0:T(2,128)S(1)}, f32[2,32]{1,0:T(2,128)S(1)}, u32[]{:S(2)}, u32[]{:S(2)}) %collective-permute-start.42) | collective-permute-done | bytes 288 | tf_op jit(solution)/shard_map/ppermute | solution.py:212
  490.0 12.0 fusion.33
  502.1 12.2 fusion.31
  521.8 104.7 %shard_map.138 = (f32[2,1024,1024]{2,1,0:T(8,128)}, f32[2,1024,1024]{2,1,0:T(8,128)}, f32[2,1024,1024]{2,1,0:T(8,128)}, f32[2,1024,1024]{2,1,0:T(8,128)}, f32[4,...) custom-call(s32[4,4]{1,0:T(4,128)} %pad_add_fusion.3.nt_ref, ...), custom_call_target="tpu_custom_call", output_to_operand_aliasing={{5}: (13, {}), {6}: (14, {}), {7}: (15, {}), {8}: (16, {})} | custom-call | flops 100000000 | bytes 80000000 | tf_op jit(solution)/shard_map/pallas_call | solution.py:175
  626.5 26.6 %collective-permute-start.28 = (f32[1024,1024]{1,0:T(8,128)}, f32[1024,1024]{1,0:T(8,128)}, u32[]{:S(2)}, u32[]{:S(2)}) collective-permute-start(f32[1024,1024]{1,0:T(8,128)} %get-tuple-element.151), channel_id=1, source_target_pairs={{0,4},{1,5},{2,6},{3,7},{4,0},{5,1},{6,2},{7,3},{8,12},{9,13},{10,... | collective-permute-start | bytes 12582920 | tf_op jit(solution)/shard_map/ppermute | solution.py:212
  654.3 14.0 collective-permute-start.29
  669.5 59.0 %shard_map.139 = (f32[2,1024,1024]{2,1,0:T(8,128)}, f32[2,1024,1024]{2,1,0:T(8,128)}, f32[2,1024,1024]{2,1,0:T(8,128)}, f32[2,1024,1024]{2,1,0:T(8,128)}, f32[4,...) custom-call(s32[4,2]{1,0:T(4,128)} %pad_add_fusion.1.nt_ref, ...), custom_call_target="tpu_custom_call", output_to_operand_aliasing={{5}: (13, {}), {6}: (14, {})} | custom-call | flops 100000000 | bytes 80000000 | tf_op jit(solution)/shard_map/pallas_call | solution.py:175
  728.5 58.8 %shard_map.140 = (f32[2,1024,1024]{2,1,0:T(8,128)}, f32[2,1024,1024]{2,1,0:T(8,128)}, f32[2,1024,1024]{2,1,0:T(8,128)}, f32[2,1024,1024]{2,1,0:T(8,128)}, f32[4,...) custom-call(s32[4,2]{1,0:T(4,128)} %pad_add_fusion.nt_ref, ...), custom_call_target="tpu_custom_call", output_to_operand_aliasing={{5}: (13, {}), {6}: (14, {})} | custom-call | flops 100000000 | bytes 80000000 | tf_op jit(solution)/shard_map/pallas_call | solution.py:175
  791.8 27.5 %collective-permute-start.49 = (f32[4,2048]{1,0:T(4,128)S(1)}, f32[4,2048]{1,0:T(4,128)S(1)}, u32[]{:S(2)}, u32[]{:S(2)}) collective-permute-start(f32[4,2048]{1,0:T(4,128)S(1)} %bitcast.266), channel_id=1, source_target_pairs={{0,1},{1,0},{2,3},{3,2},{4,5},{5,4},{6,7},{7,6},{8,9},{9,8},{10,11... | collective-permute-start | bytes 98312 | tf_op jit(solution)/shard_map/ppermute | solution.py:212
  820.5 27.7 %collective-permute-start.30 = (f32[1024,1024]{1,0:T(8,128)}, f32[1024,1024]{1,0:T(8,128)}, u32[]{:S(2)}, u32[]{:S(2)}) collective-permute-start(f32[1024,1024]{1,0:T(8,128)} %get-tuple-element.153), channel_id=1, source_target_pairs={{0,4},{1,5},{2,6},{3,7},{4,0},{5,1},{6,2},{7,3},{8,12},{9,13},{10,... | collective-permute-start | bytes 12582920 | tf_op jit(solution)/shard_map/ppermute | solution.py:212
  848.3 6.8 copy.53
  857.1 82.5 %collective-permute-done.30 = f32[1024,1024]{1,0:T(8,128)} collective-permute-done((f32[1024,1024]{1,0:T(8,128)}, f32[1024,1024]{1,0:T(8,128)}, u32[]{:S(2)}, u32[]{:S(2)}) %collective-permute-start.30) | collective-permute-done | bytes 4194336 | tf_op jit(solution)/shard_map/ppermute | solution.py:212
  942.0 12.3 fusion.17
  954.3 12.0 fusion.15
  966.4 58.9 %shard_map.141 = (f32[2,1024,1024]{2,1,0:T(8,128)}, f32[2,1024,1024]{2,1,0:T(8,128)}, f32[2,1024,1024]{2,1,0:T(8,128)}, f32[2,1024,1024]{2,1,0:T(8,128)}, f32[4,...) custom-call(s32[4,2]{1,0:T(4,128)} %pad_add_fusion.4.nt_ref, ...), custom_call_target="tpu_custom_call", output_to_operand_aliasing={{5}: (13, {}), {6}: (14, {})} | custom-call | flops 100000000 | bytes 80000000 | tf_op jit(solution)/shard_map/pallas_call | solution.py:175
  1032.1 5.7 fusion.3
  1038.9 17.9 %collective-permute-start.37 = (f32[1024,1024]{1,0:T(8,128)}, f32[1024,1024]{1,0:T(8,128)}, u32[]{:S(2)}, u32[]{:S(2)}) collective-permute-start(f32[1024,1024]{1,0:T(8,128)} %get-tuple-element.170), channel_id=1, source_target_pairs={{0,2},{1,3},{2,0},{3,1},{4,6},{5,7},{6,4},{7,5},{8,10},{9,11},{10,... | collective-permute-start | bytes 12582920 | tf_op jit(solution)/shard_map/ppermute | solution.py:212
  1057.7 6.0 all-to-all-start.1
  1063.7 19.8 %fusion.24 = (f32[1024,1024]{1,0:T(8,128)}, f32[1024,1024]{1,0:T(8,128)}) fusion(f32[1024,1024]{1,0:T(8,128)} %collective-permute-done.29, f32[2,1024,1024]{2,1,0:T(8,128)} %collective-permute-done.24, f32[2,1024,1024]{2,1,0:T(8,128)} %collective-permute-done.5, f32[2,1024,1024]{2,1,0:T(8,128)} %get-tuple-element.144, ...), kind=kLoop, calls=%fused_computation.57 | loop fusion | flops 8388608 | bytes 50331648 | tf_op jit(solution)/shard_map/add | solution.py:382
  1085.7 19.6 %fusion.21 = (f32[1024,1024]{1,0:T(8,128)}, f32[1024,1024]{1,0:T(8,128)}) fusion(f32[1024,1024]{1,0:T(8,128)} %collective-permute-done.30, f32[2,1024,1024]{2,1,0:T(8,128)} %collective-permute-done.27, f32[2,1024,1024]{2,1,0:T(8,128)} %collective-permute-done.26, f32[2,1024,1024]{2,1,0:T(8,128)} %get-tuple-element.149, ...), kind=kLoop, calls=%fused_computation.52 | loop fusion | flops 8388608 | bytes 50331648 | tf_op jit(solution)/shard_map/add | solution.py:382
  1106.7 48.8 %all-to-all-done.1 = f32[8,4,2048]{2,1,0:T(4,128)S(1)} async-done(((f32[8,4,2048]{2,1,0:T(4,128)}), f32[8,4,2048]{2,1,0:T(4,128)S(1)}, u32[]{:S(2)}, u32[]{:S(2)}) %all-to-all-start.1) | async-done | bytes 262176 | tf_op jit(solution)/shard_map/all_to_all | solution.py:369
  1155.8 10.6 collective-permute-start.50
  1166.7 10.7 fusion.14
  1178.9 7.4 fusion.11
  1189.6 51.7 %collective-permute-done.45 = f32[1024,1024]{1,0:T(8,128)} collective-permute-done((f32[1024,1024]{1,0:T(8,128)}, f32[1024,1024]{1,0:T(8,128)}, u32[]{:S(2)}, u32[]{:S(2)}) %collective-permute-start.45) | collective-permute-done | bytes 4194336 | tf_op jit(solution)/shard_map/ppermute | solution.py:212
  1241.3 8.8 bitcast_add_fusion.1
  1250.1 18.6 %collective-permute-done.46 = f32[1024,1024]{1,0:T(8,128)} collective-permute-done((f32[1024,1024]{1,0:T(8,128)}, f32[1024,1024]{1,0:T(8,128)}, u32[]{:S(2)}, u32[]{:S(2)}) %collective-permute-start.46) | collective-permute-done | bytes 4194336 | tf_op jit(solution)/shard_map/ppermute | solution.py:212
  1268.7 7.4 bitcast_add_fusion
  1287.8 13.4 collective-permute-done.50
  1301.2 5.8 add_convert_fusion
  1311.9 20.1 %collective-permute-done.40 = f32[1024,1024]{1,0:T(8,128)} collective-permute-done((f32[1024,1024]{1,0:T(8,128)}, f32[1024,1024]{1,0:T(8,128)}, u32[]{:S(2)}, u32[]{:S(2)}) %collective-permute-start.40) | collective-permute-done | bytes 4194336 | tf_op jit(solution)/shard_map/ppermute | solution.py:212
  1334.9 25.1 %collective-permute-done.39 = f32[1024,1024]{1,0:T(8,128)} collective-permute-done((f32[1024,1024]{1,0:T(8,128)}, f32[1024,1024]{1,0:T(8,128)}, u32[]{:S(2)}, u32[]{:S(2)}) %collective-permute-start.39) | collective-permute-done | bytes 4194336 | tf_op jit(solution)/shard_map/ppermute | solution.py:212
  1363.5 7.9 fusion.4
  1371.4 50.9 %collective-permute-done.48 = f32[1024,1024]{1,0:T(8,128)} collective-permute-done((f32[1024,1024]{1,0:T(8,128)}, f32[1024,1024]{1,0:T(8,128)}, u32[]{:S(2)}, u32[]{:S(2)}) %collective-permute-start.48) | collective-permute-done | bytes 4194336 | tf_op jit(solution)/shard_map/ppermute | solution.py:212
  1425.3 24.0 %collective-permute-done.47 = f32[1024,1024]{1,0:T(8,128)} collective-permute-done((f32[1024,1024]{1,0:T(8,128)}, f32[1024,1024]{1,0:T(8,128)}, u32[]{:S(2)}, u32[]{:S(2)}) %collective-permute-start.47) | collective-permute-done | bytes 4194336 | tf_op jit(solution)/shard_map/ppermute | solution.py:212
  1453.8 3.9 fusion.2
  (325 shorter events, 148.2 us)
Async XLA Ops:
  14.4 118.7 %collective-permute-start.13 = (bf16[2,1024,1024]{2,1,0:T(8,128)(2,1)}, bf16[2,1024,1024]{2,1,0:T(8,128)(2,1)}, u32[]{:S(2)}, u32[]{:S(2)}) collective-permute-start(bf16[2,1024,1024]{2,1,0:T(8,128)(2,1)} %fusion.6.rest_0_), channel_id=1, source_target_pairs={{0,2},{1,3},{2,0},{3,1},{4,6},{5,7},{6,4},{7,5},{8,10},{9,11},{10,... | collective-permute-start | bytes 12582920 | tf_op jit(solution)/shard_map/ppermute | solution.py:212
  17.6 80.4 %collective-permute-start.4 = (bf16[2,1024,1024]{2,1,0:T(8,128)(2,1)}, bf16[2,1024,1024]{2,1,0:T(8,128)(2,1)}, u32[]{:S(2)}, u32[]{:S(2)}) collective-permute-start(bf16[2,1024,1024]{2,1,0:T(8,128)(2,1)} %fusion.6.rest_0_), channel_id=1, source_target_pairs={{0,1},{1,0},{2,3},{3,2},{4,5},{5,4},{6,7},{7,6},{8,9},{9,8},{10,11... | collective-permute-start | bytes 12582920 | tf_op jit(solution)/shard_map/ppermute | solution.py:212
  24.0 109.1 %collective-permute-start.11 = (bf16[2,1024,1024]{2,1,0:T(8,128)(2,1)}, bf16[2,1024,1024]{2,1,0:T(8,128)(2,1)}, u32[]{:S(2)}, u32[]{:S(2)}) collective-permute-start(bf16[2,1024,1024]{2,1,0:T(8,128)(2,1)} %fusion.5.rest_0_.rest_2_), channel_id=1, source_target_pairs={{0,4},{1,5},{2,6},{3,7},{4,0},{5,1},{6,2},{7,3},{8,12},{9,13},{10,... | collective-permute-start | bytes 12582920 | tf_op jit(solution)/shard_map/ppermute | solution.py:212
  40.8 94.9 %collective-permute-start.9 = (bf16[2,1024,1024]{2,1,0:T(8,128)(2,1)}, bf16[2,1024,1024]{2,1,0:T(8,128)(2,1)}, u32[]{:S(2)}, u32[]{:S(2)}) collective-permute-start(bf16[2,1024,1024]{2,1,0:T(8,128)(2,1)} %fusion.5.rest_0_.rest_2_), channel_id=1, source_target_pairs={{0,1},{1,0},{2,3},{3,2},{4,5},{5,4},{6,7},{7,6},{8,9},{9,8},{10,11... | collective-permute-start | bytes 12582920 | tf_op jit(solution)/shard_map/ppermute | solution.py:212
  94.8 39.3 %collective-permute-start.6 = (bf16[2,512,512]{2,1,0:T(8,128)(2,1)}, bf16[2,512,512]{2,1,0:T(8,128)(2,1)}, u32[]{:S(2)}, u32[]{:S(2)}) collective-permute-start(bf16[2,512,512]{2,1,0:T(8,128)(2,1)} %get-tuple-element.248), channel_id=1, source_target_pairs={{0,8},{8,0},{1,9},{9,1},{2,10},{10,2},{3,11},{11,3},{4,12},{12,4},... | collective-permute-start | bytes 3145736 | tf_op jit(solution)/shard_map/ppermute | solution.py:216
  133.2 118.2 %collective-permute-start.15 = (bf16[2,1024,1024]{2,1,0:T(8,128)(2,1)}, bf16[2,1024,1024]{2,1,0:T(8,128)(2,1)}, u32[]{:S(2)}, u32[]{:S(2)}) collective-permute-start(bf16[2,1024,1024]{2,1,0:T(8,128)(2,1)} %collective-permute-done.13.rest_0_), channel_id=1, source_target_pairs={{0,1},{1,0},{2,3},{3,2},{4,5},{5,4},{6,7},{7,6},{8,9},{9,8},{10,11... | collective-permute-start | bytes 12582920 | tf_op jit(solution)/shard_map/ppermute | solution.py:212
  133.2 118.2 %collective-permute-start.16 = (bf16[2,1024,1024]{2,1,0:T(8,128)(2,1)}, bf16[2,1024,1024]{2,1,0:T(8,128)(2,1)}, u32[]{:S(2)}, u32[]{:S(2)}) collective-permute-start(bf16[2,1024,1024]{2,1,0:T(8,128)(2,1)} %collective-permute-done.11.rest_2_), channel_id=1, source_target_pairs={{0,1},{1,0},{2,3},{3,2},{4,5},{5,4},{6,7},{7,6},{8,9},{9,8},{10,11... | collective-permute-start | bytes 12582920 | tf_op jit(solution)/shard_map/ppermute | solution.py:212
  133.7 53.5 %collective-permute-start.7 = (bf16[2,512,512]{2,1,0:T(8,128)(2,1)}, bf16[2,512,512]{2,1,0:T(8,128)(2,1)}, u32[]{:S(2)}, u32[]{:S(2)}) collective-permute-start(bf16[2,512,512]{2,1,0:T(8,128)(2,1)} %get-tuple-element.246), channel_id=1, source_target_pairs={{0,8},{8,0},{1,9},{9,1},{2,10},{10,2},{3,11},{11,3},{4,12},{12,4},... | collective-permute-start | bytes 3145736 | tf_op jit(solution)/shard_map/ppermute | solution.py:216
  134.2 103.8 %collective-permute-start.8 = (bf16[2,512,512]{2,1,0:T(8,128)(2,1)}, bf16[2,512,512]{2,1,0:T(8,128)(2,1)}, u32[]{:S(2)}, u32[]{:S(2)}) collective-permute-start(bf16[2,512,512]{2,1,0:T(8,128)(2,1)} %get-tuple-element.244), channel_id=1, source_target_pairs={{0,8},{8,0},{1,9},{9,1},{2,10},{10,2},{3,11},{11,3},{4,12},{12,4},... | collective-permute-start | bytes 3145736 | tf_op jit(solution)/shard_map/ppermute | solution.py:216
  135.7 232.9 %collective-permute-start.12 = (bf16[2,1024,1024]{2,1,0:T(8,128)(2,1)}, bf16[2,1024,1024]{2,1,0:T(8,128)(2,1)}, u32[]{:S(2)}, u32[]{:S(2)}) collective-permute-start(bf16[2,1024,1024]{2,1,0:T(8,128)(2,1)} %collective-permute-done.11.rest_2_), channel_id=1, source_target_pairs={{0,2},{1,3},{2,0},{3,1},{4,6},{5,7},{6,4},{7,5},{8,10},{9,11},{10,... | collective-permute-start | bytes 12582920 | tf_op jit(solution)/shard_map/ppermute | solution.py:212
  141.9 96.0 %all-to-all-start = ((f32[8,4,2,2048]{3,2,1,0:T(2,128)}), f32[8,4,2,2048]{3,2,1,0:T(2,128)}, u32[]{:S(2)}, u32[]{:S(2)}) async-start(f32[8,4,2,2048]{3,2,1,0:T(2,128)} %pad_maximum_fusion.7), calls=%async_computation | async-start | bytes 1048576 | tf_op jit(solution)/shard_map/all_to_all | solution.py:272
  187.3 206.9 %collective-permute-start.10 = (bf16[2,1024,1024]{2,1,0:T(8,128)(2,1)}, bf16[2,1024,1024]{2,1,0:T(8,128)(2,1)}, u32[]{:S(2)}, u32[]{:S(2)}) collective-permute-start(bf16[2,1024,1024]{2,1,0:T(8,128)(2,1)} %fusion.6.rest_0_), channel_id=1, source_target_pairs={{0,4},{1,5},{2,6},{3,7},{4,0},{5,1},{6,2},{7,3},{8,12},{9,13},{10,... | collective-permute-start | bytes 12582920 | tf_op jit(solution)/shard_map/ppermute | solution.py:212
  238.0 154.6 %collective-permute-start.14 = (bf16[2,1024,1024]{2,1,0:T(8,128)(2,1)}, bf16[2,1024,1024]{2,1,0:T(8,128)(2,1)}, u32[]{:S(2)}, u32[]{:S(2)}) collective-permute-start(bf16[2,1024,1024]{2,1,0:T(8,128)(2,1)} %collective-permute-done.13.rest_0_), channel_id=1, source_target_pairs={{0,4},{1,5},{2,6},{3,7},{4,0},{5,1},{6,2},{7,3},{8,12},{9,13},{10,... | collective-permute-start | bytes 12582920 | tf_op jit(solution)/shard_map/ppermute | solution.py:212
  355.1 133.2 %collective-permute-start.20 = (f32[2,1024,1024]{2,1,0:T(8,128)}, f32[2,1024,1024]{2,1,0:T(8,128)}, u32[]{:S(2)}, u32[]{:S(2)}) collective-permute-start(f32[2,1024,1024]{2,1,0:T(8,128)} %get-tuple-element.130), channel_id=1, source_target_pairs={{0,1},{1,0},{2,3},{3,2},{4,5},{5,4},{6,7},{7,6},{8,9},{9,8},{10,11... | collective-permute-start | bytes 25165832 | tf_op jit(solution)/shard_map/ppermute | solution.py:212
  368.6 119.7 %collective-permute-start.21 = (f32[2,1024,1024]{2,1,0:T(8,128)}, f32[2,1024,1024]{2,1,0:T(8,128)}, u32[]{:S(2)}, u32[]{:S(2)}) collective-permute-start(f32[2,1024,1024]{2,1,0:T(8,128)} %get-tuple-element.132), channel_id=1, source_target_pairs={{0,1},{1,0},{2,3},{3,2},{4,5},{5,4},{6,7},{7,6},{8,9},{9,8},{10,11... | collective-permute-start | bytes 25165832 | tf_op jit(solution)/shard_map/ppermute | solution.py:212
  368.7 114.4 %collective-permute-start.18 = (bf16[2,1024,1024]{2,1,0:T(8,128)(2,1)}, bf16[2,1024,1024]{2,1,0:T(8,128)(2,1)}, u32[]{:S(2)}, u32[]{:S(2)}) collective-permute-start(bf16[2,1024,1024]{2,1,0:T(8,128)(2,1)} %fusion.5.rest_0_.rest_2_), channel_id=1, source_target_pairs={{0,2},{1,3},{2,0},{3,1},{4,6},{5,7},{6,4},{7,5},{8,10},{9,11},{10,... | collective-permute-start | bytes 12582920 | tf_op jit(solution)/shard_map/ppermute | solution.py:212
  393.8 94.0 %collective-permute-start.23 = (bf16[2,1024,1024]{2,1,0:T(8,128)(2,1)}, bf16[2,1024,1024]{2,1,0:T(8,128)(2,1)}, u32[]{:S(2)}, u32[]{:S(2)}) collective-permute-start(bf16[2,1024,1024]{2,1,0:T(8,128)(2,1)} %collective-permute-done.12.rest_2_), channel_id=1, source_target_pairs={{0,1},{1,0},{2,3},{3,2},{4,5},{5,4},{6,7},{7,6},{8,9},{9,8},{10,11... | collective-permute-start | bytes 12582920 | tf_op jit(solution)/shard_map/ppermute | solution.py:212
  394.1 88.9 %collective-permute-start.42 = (f32[2,32]{1,0:T(2,128)S(1)}, f32[2,32]{1,0:T(2,128)S(1)}, u32[]{:S(2)}, u32[]{:S(2)}) collective-permute-start(f32[2,32]{1,0:T(2,128)S(1)} %add.318), channel_id=1, source_target_pairs={{0,2},{1,3},{2,0},{3,1},{4,6},{5,7},{6,4},{7,5},{8,10},{9,11},{10,... | collective-permute-start | bytes 776 | tf_op jit(solution)/shard_map/ppermute | solution.py:212
  483.0 143.4 %collective-permute-start.5 = (f32[2,1024,1024]{2,1,0:T(8,128)}, f32[2,1024,1024]{2,1,0:T(8,128)}, u32[]{:S(2)}, u32[]{:S(2)}) collective-permute-start(f32[2,1024,1024]{2,1,0:T(8,128)} %get-tuple-element.110), channel_id=1, source_target_pairs={{0,1},{1,0},{2,3},{3,2},{4,5},{5,4},{6,7},{7,6},{8,9},{9,8},{10,11... | collective-permute-start | bytes 25165832 | tf_op jit(solution)/shard_map/ppermute | solution.py:212
  487.7 300.4 %collective-permute-start.26 = (f32[2,1024,1024]{2,1,0:T(8,128)}, f32[2,1024,1024]{2,1,0:T(8,128)}, u32[]{:S(2)}, u32[]{:S(2)}) collective-permute-start(f32[2,1024,1024]{2,1,0:T(8,128)} %get-tuple-element.148), channel_id=1, source_target_pairs={{0,1},{1,0},{2,3},{3,2},{4,5},{5,4},{6,7},{7,6},{8,9},{9,8},{10,11... | collective-permute-start | bytes 25165832 | tf_op jit(solution)/shard_map/ppermute | solution.py:212
  487.8 26.8 %collective-permute-start.22 = (bf16[2,1024,1024]{2,1,0:T(8,128)(2,1)}, bf16[2,1024,1024]{2,1,0:T(8,128)(2,1)}, u32[]{:S(2)}, u32[]{:S(2)}) collective-permute-start(bf16[2,1024,1024]{2,1,0:T(8,128)(2,1)} %collective-permute-done.14.rest_0_), channel_id=1, source_target_pairs={{0,1},{1,0},{2,3},{3,2},{4,5},{5,4},{6,7},{7,6},{8,9},{9,8},{10,11... | collective-permute-start | bytes 12582920 | tf_op jit(solution)/shard_map/ppermute | solution.py:212
  488.3 164.8 %collective-permute-start.19 = (bf16[2,1024,1024]{2,1,0:T(8,128)(2,1)}, bf16[2,1024,1024]{2,1,0:T(8,128)(2,1)}, u32[]{:S(2)}, u32[]{:S(2)}) collective-permute-start(bf16[2,1024,1024]{2,1,0:T(8,128)(2,1)} %collective-permute-done.18.rest_2_), channel_id=1, source_target_pairs={{0,1},{1,0},{2,3},{3,2},{4,5},{5,4},{6,7},{7,6},{8,9},{9,8},{10,11... | collective-permute-start | bytes 12582920 | tf_op jit(solution)/shard_map/ppermute | solution.py:212
  488.3 165.9 %collective-permute-start.17 = (bf16[2,1024,1024]{2,1,0:T(8,128)(2,1)}, bf16[2,1024,1024]{2,1,0:T(8,128)(2,1)}, u32[]{:S(2)}, u32[]{:S(2)}) collective-permute-start(bf16[2,1024,1024]{2,1,0:T(8,128)(2,1)} %collective-permute-done.10.rest_0_), channel_id=1, source_target_pairs={{0,1},{1,0},{2,3},{3,2},{4,5},{5,4},{6,7},{7,6},{8,9},{9,8},{10,11... | collective-permute-start | bytes 12582920 | tf_op jit(solution)/shard_map/ppermute | solution.py:212
  514.5 306.0 %collective-permute-start.25 = (f32[1024,1024]{1,0:T(8,128)}, f32[1024,1024]{1,0:T(8,128)}, u32[]{:S(2)}, u32[]{:S(2)}) collective-permute-start(f32[1024,1024]{1,0:T(8,128)} %get-tuple-element.146), channel_id=1, source_target_pairs={{0,2},{1,3},{2,0},{3,1},{4,6},{5,7},{6,4},{7,5},{8,10},{9,11},{10,... | collective-permute-start | bytes 12582920 | tf_op jit(solution)/shard_map/ppermute | solution.py:212
  626.5 228.6 %collective-permute-start.28 = (f32[1024,1024]{1,0:T(8,128)}, f32[1024,1024]{1,0:T(8,128)}, u32[]{:S(2)}, u32[]{:S(2)}) collective-permute-start(f32[1024,1024]{1,0:T(8,128)} %get-tuple-element.151), channel_id=1, source_target_pairs={{0,4},{1,5},{2,6},{3,7},{4,0},{5,1},{6,2},{7,3},{8,12},{9,13},{10,... | collective-permute-start | bytes 12582920 | tf_op jit(solution)/shard_map/ppermute | solution.py:212
  653.0 286.6 %collective-permute-start.31 = (f32[2,1024,1024]{2,1,0:T(8,128)}, f32[2,1024,1024]{2,1,0:T(8,128)}, u32[]{:S(2)}, u32[]{:S(2)}) collective-permute-start(f32[2,1024,1024]{2,1,0:T(8,128)} %get-tuple-element.156), channel_id=1, source_target_pairs={{0,1},{1,0},{2,3},{3,2},{4,5},{5,4},{6,7},{7,6},{8,9},{9,8},{10,11... | collective-permute-start | bytes 25165832 | tf_op jit(solution)/shard_map/ppermute | solution.py:212
  654.3 202.8 %collective-permute-start.29 = (f32[1024,1024]{1,0:T(8,128)}, f32[1024,1024]{1,0:T(8,128)}, u32[]{:S(2)}, u32[]{:S(2)}) collective-permute-start(f32[1024,1024]{1,0:T(8,128)} %get-tuple-element.152), channel_id=1, source_target_pairs={{0,2},{1,3},{2,0},{3,1},{4,6},{5,7},{6,4},{7,5},{8,10},{9,11},{10,... | collective-permute-start | bytes 12582920 | tf_op jit(solution)/shard_map/ppermute | solution.py:212
  791.8 28.3 %collective-permute-start.49 = (f32[4,2048]{1,0:T(4,128)S(1)}, f32[4,2048]{1,0:T(4,128)S(1)}, u32[]{:S(2)}, u32[]{:S(2)}) collective-permute-start(f32[4,2048]{1,0:T(4,128)S(1)} %bitcast.266), channel_id=1, source_target_pairs={{0,1},{1,0},{2,3},{3,2},{4,5},{5,4},{6,7},{7,6},{8,9},{9,8},{10,11... | collective-permute-start | bytes 98312 | tf_op jit(solution)/shard_map/ppermute | solution.py:212
  820.1 121.9 %collective-permute-start.32 = (f32[2,1024,1024]{2,1,0:T(8,128)}, f32[2,1024,1024]{2,1,0:T(8,128)}, u32[]{:S(2)}, u32[]{:S(2)}) collective-permute-start(f32[2,1024,1024]{2,1,0:T(8,128)} %get-tuple-element.158), channel_id=1, source_target_pairs={{0,1},{1,0},{2,3},{3,2},{4,5},{5,4},{6,7},{7,6},{8,9},{9,8},{10,11... | collective-permute-start | bytes 25165832 | tf_op jit(solution)/shard_map/ppermute | solution.py:212
  820.5 119.1 %collective-permute-start.30 = (f32[1024,1024]{1,0:T(8,128)}, f32[1024,1024]{1,0:T(8,128)}, u32[]{:S(2)}, u32[]{:S(2)}) collective-permute-start(f32[1024,1024]{1,0:T(8,128)} %get-tuple-element.153), channel_id=1, source_target_pairs={{0,4},{1,5},{2,6},{3,7},{4,0},{5,1},{6,2},{7,3},{8,12},{9,13},{10,... | collective-permute-start | bytes 12582920 | tf_op jit(solution)/shard_map/ppermute | solution.py:212
  855.0 170.3 %collective-permute-start.51 = (f32[2,3,512,512]{3,2,0,1:T(8,128)}, f32[2,3,512,512]{3,2,0,1:T(8,128)}, u32[]{:S(2)}, u32[]{:S(2)}) collective-permute-start(f32[2,3,512,512]{3,2,0,1:T(8,128)} %copy.53), channel_id=1, source_target_pairs={{0,8},{8,0},{1,9},{9,1},{2,10},{10,2},{3,11},{11,3},{4,12},{12,4},... | collective-permute-start | bytes 18874376 | tf_op jit(solution)/shard_map/ppermute | solution.py:216
  857.1 181.6 %collective-permute-start.34 = (f32[2,1024,1024]{2,1,0:T(8,128)}, f32[2,1024,1024]{2,1,0:T(8,128)}, u32[]{:S(2)}, u32[]{:S(2)}) collective-permute-start(f32[2,1024,1024]{2,1,0:T(8,128)} %get-tuple-element.165), channel_id=1, source_target_pairs={{0,1},{1,0},{2,3},{3,2},{4,5},{5,4},{6,7},{7,6},{8,9},{9,8},{10,11... | collective-permute-start | bytes 25165832 | tf_op jit(solution)/shard_map/ppermute | solution.py:212
  939.6 99.3 %collective-permute-start.24 = (f32[2,1024,1024]{2,1,0:T(8,128)}, f32[2,1024,1024]{2,1,0:T(8,128)}, u32[]{:S(2)}, u32[]{:S(2)}) collective-permute-start(f32[2,1024,1024]{2,1,0:T(8,128)} %get-tuple-element.145), channel_id=1, source_target_pairs={{0,1},{1,0},{2,3},{3,2},{4,5},{5,4},{6,7},{7,6},{8,9},{9,8},{10,11... | collective-permute-start | bytes 25165832 | tf_op jit(solution)/shard_map/ppermute | solution.py:212
  939.6 143.9 %collective-permute-start.27 = (f32[2,1024,1024]{2,1,0:T(8,128)}, f32[2,1024,1024]{2,1,0:T(8,128)}, u32[]{:S(2)}, u32[]{:S(2)}) collective-permute-start(f32[2,1024,1024]{2,1,0:T(8,128)} %get-tuple-element.150), channel_id=1, source_target_pairs={{0,1},{1,0},{2,3},{3,2},{4,5},{5,4},{6,7},{7,6},{8,9},{9,8},{10,11... | collective-permute-start | bytes 25165832 | tf_op jit(solution)/shard_map/ppermute | solution.py:212
  942.0 163.3 %collective-permute-start.36 = (f32[2,1024,1024]{2,1,0:T(8,128)}, f32[2,1024,1024]{2,1,0:T(8,128)}, u32[]{:S(2)}, u32[]{:S(2)}) collective-permute-start(f32[2,1024,1024]{2,1,0:T(8,128)} %get-tuple-element.169), channel_id=1, source_target_pairs={{0,1},{1,0},{2,3},{3,2},{4,5},{5,4},{6,7},{7,6},{8,9},{9,8},{10,11... | collective-permute-start | bytes 25165832 | tf_op jit(solution)/shard_map/ppermute | solution.py:212
  1025.3 130.5 %collective-permute-start.33 = (f32[2,1024,1024]{2,1,0:T(8,128)}, f32[2,1024,1024]{2,1,0:T(8,128)}, u32[]{:S(2)}, u32[]{:S(2)}) collective-permute-start(f32[2,1024,1024]{2,1,0:T(8,128)} %get-tuple-element.164), channel_id=1, source_target_pairs={{0,1},{1,0},{2,3},{3,2},{4,5},{5,4},{6,7},{7,6},{8,9},{9,8},{10,11... | collective-permute-start | bytes 25165832 | tf_op jit(solution)/shard_map/ppermute | solution.py:212
  1038.7 140.1 %collective-permute-start.35 = (f32[2,1024,1024]{2,1,0:T(8,128)}, f32[2,1024,1024]{2,1,0:T(8,128)}, u32[]{:S(2)}, u32[]{:S(2)}) collective-permute-start(f32[2,1024,1024]{2,1,0:T(8,128)} %get-tuple-element.168), channel_id=1, source_target_pairs={{0,1},{1,0},{2,3},{3,2},{4,5},{5,4},{6,7},{7,6},{8,9},{9,8},{10,11... | collective-permute-start | bytes 25165832 | tf_op jit(solution)/shard_map/ppermute | solution.py:212
  1038.9 116.6 %collective-permute-start.37 = (f32[1024,1024]{1,0:T(8,128)}, f32[1024,1024]{1,0:T(8,128)}, u32[]{:S(2)}, u32[]{:S(2)}) collective-permute-start(f32[1024,1024]{1,0:T(8,128)} %get-tuple-element.170), channel_id=1, source_target_pairs={{0,2},{1,3},{2,0},{3,1},{4,6},{5,7},{6,4},{7,5},{8,10},{9,11},{10,... | collective-permute-start | bytes 12582920 | tf_op jit(solution)/shard_map/ppermute | solution.py:212
  1057.7 97.8 %all-to-all-start.1 = ((f32[8,4,2048]{2,1,0:T(4,128)}), f32[8,4,2048]{2,1,0:T(4,128)S(1)}, u32[]{:S(2)}, u32[]{:S(2)}) async-start(f32[8,4,2048]{2,1,0:T(4,128)} %bitcast.253), calls=%async_computation.1 | async-start | bytes 524288 | tf_op jit(solution)/shard_map/all_to_all | solution.py:369
  1063.7 394.0 %all-reduce.2.cloned.1.call-start = ((), (), s32[]{:S(2)}) async-start(), calls=%async_computation.2 | async-start | bytes 262144 | tf_op jit(solution)/shard_map/psum | solution.py:380
  1083.5 95.3 %collective-permute-start.38 = (f32[1024,1024]{1,0:T(8,128)}, f32[1024,1024]{1,0:T(8,128)}, u32[]{:S(2)}, u32[]{:S(2)}) collective-permute-start(f32[1024,1024]{1,0:T(8,128)} %get-tuple-element.171), channel_id=1, source_target_pairs={{0,4},{1,5},{2,6},{3,7},{4,0},{5,1},{6,2},{7,3},{8,12},{9,13},{10,... | collective-permute-start | bytes 12582920 | tf_op jit(solution)/shard_map/ppermute | solution.py:212
  1105.3 136.0 %collective-permute-start.45 = (f32[1024,1024]{1,0:T(8,128)}, f32[1024,1024]{1,0:T(8,128)}, u32[]{:S(2)}, u32[]{:S(2)}) collective-permute-start(f32[1024,1024]{1,0:T(8,128)} %get-tuple-element.195), channel_id=1, source_target_pairs={{0,2},{1,3},{2,0},{3,1},{4,6},{5,7},{6,4},{7,5},{8,10},{9,11},{10,... | collective-permute-start | bytes 12582920 | tf_op jit(solution)/shard_map/ppermute | solution.py:212
  1155.6 113.1 %collective-permute-start.46 = (f32[1024,1024]{1,0:T(8,128)}, f32[1024,1024]{1,0:T(8,128)}, u32[]{:S(2)}, u32[]{:S(2)}) collective-permute-start(f32[1024,1024]{1,0:T(8,128)} %get-tuple-element.196), channel_id=1, source_target_pairs={{0,4},{1,5},{2,6},{3,7},{4,0},{5,1},{6,2},{7,3},{8,12},{9,13},{10,... | collective-permute-start | bytes 12582920 | tf_op jit(solution)/shard_map/ppermute | solution.py:212
  1155.8 145.4 %collective-permute-start.50 = (f32[2,3,512,512]{3,2,1,0:T(8,128)}, f32[2,3,512,512]{3,2,1,0:T(8,128)}, u32[]{:S(2)}, u32[]{:S(2)}) collective-permute-start(f32[2,3,512,512]{3,2,1,0:T(8,128)} %get-tuple-element.208), channel_id=1, source_target_pairs={{0,8},{8,0},{1,9},{9,1},{2,10},{10,2},{3,11},{11,3},{4,12},{12,4},... | collective-permute-start | bytes 18874376 | tf_op jit(solution)/shard_map/ppermute | solution.py:216
  1186.2 173.7 %collective-permute-start.39 = (f32[1024,1024]{1,0:T(8,128)}, f32[1024,1024]{1,0:T(8,128)}, u32[]{:S(2)}, u32[]{:S(2)}) collective-permute-start(f32[1024,1024]{1,0:T(8,128)} %fusion.14), channel_id=1, source_target_pairs={{0,4},{1,5},{2,6},{3,7},{4,0},{5,1},{6,2},{7,3},{8,12},{9,13},{10,... | collective-permute-start | bytes 12582920 | tf_op jit(solution)/shard_map/ppermute | solution.py:212
  1188.3 143.7 %collective-permute-start.40 = (f32[1024,1024]{1,0:T(8,128)}, f32[1024,1024]{1,0:T(8,128)}, u32[]{:S(2)}, u32[]{:S(2)}) collective-permute-start(f32[1024,1024]{1,0:T(8,128)} %fusion.11), channel_id=1, source_target_pairs={{0,2},{1,3},{2,0},{3,1},{4,6},{5,7},{6,4},{7,5},{8,10},{9,11},{10,... | collective-permute-start | bytes 12582920 | tf_op jit(solution)/shard_map/ppermute | solution.py:212
  1276.1 173.3 %collective-permute-start.47 = (f32[1024,1024]{1,0:T(8,128)}, f32[1024,1024]{1,0:T(8,128)}, u32[]{:S(2)}, u32[]{:S(2)}) collective-permute-start(f32[1024,1024]{1,0:T(8,128)} %bitcast_add_fusion.1), channel_id=1, source_target_pairs={{0,4},{1,5},{2,6},{3,7},{4,0},{5,1},{6,2},{7,3},{8,12},{9,13},{10,... | collective-permute-start | bytes 12582920 | tf_op jit(solution)/shard_map/ppermute | solution.py:212
  1278.2 144.1 %collective-permute-start.48 = (f32[1024,1024]{1,0:T(8,128)}, f32[1024,1024]{1,0:T(8,128)}, u32[]{:S(2)}, u32[]{:S(2)}) collective-permute-start(f32[1024,1024]{1,0:T(8,128)} %bitcast_add_fusion), channel_id=1, source_target_pairs={{0,2},{1,3},{2,0},{3,1},{4,6},{5,7},{6,4},{7,5},{8,10},{9,11},{10,... | collective-permute-start | bytes 12582920 | tf_op jit(solution)/shard_map/ppermute | solution.py:212
  (68 other events, 2077.4 us)
Sparse Core Ops, SparseCore 0:
  1288.0 71.2 all-reduce.1

commit v3 on v2

--- a/solution.py
+++ b/solution.py
@@ -11,6 +11,7 @@
 AUX_COEF = 0.01
 BLK = 1024
 TILE = 256
+NARROW = 256
 X, Y = 2, 4
 F32 = jnp.float32
 BF16 = jnp.bfloat16
@@ -20,7 +21,7 @@
     return lax.dot_general(a, b, (((ca,), (cb,)), ((), ())), preferred_element_type=F32)
 
 
-def expert_kernel(n_blk, n_exp, fresh, nt_ref, pos_ref, gate_ref, wg0_ref, wg1_ref, wu0_ref, wu1_ref, wd0_ref, wd1_ref, *rest):
+def expert_kernel(n_blk, n_exp, fresh, nt_ref, win_ref, pos_ref, gate_ref, wg0_ref, wg1_ref, wu0_ref, wu1_ref, wd0_ref, wd1_ref, *rest):
     n_pair = n_exp // 2
     rest = list(rest)
     take = lambda n: [rest.pop(0) for _ in range(n)]
@@ -87,16 +88,15 @@
     wg, wu, wd = (wg0_ref, wg1_ref), (wu0_ref, wu1_ref), (wd0_ref, wd1_ref)
     cols = (slice(0, half), slice(half, 2 * half))
 
-    gate_row = gate_ref[0, 0]
-
-    def tile(base, size, first):
-        pos = pos_ref[0, 0]
-        rows = (lax.broadcasted_iota(jnp.int32, (size, BLK), 0) + base).astype(F32)
+    def tile(base, size, first, tok, n_tok):
+        pos = pos_ref[0, 0, :, tok]
+        gate_row = gate_ref[0, 0, :, tok]
+        rows = (lax.broadcasted_iota(jnp.int32, (size, n_tok), 0) + base).astype(F32)
         hit = rows == pos
         pick = jnp.where(hit, 1.0, 0.0).astype(BF16)
         gate_c = jnp.sum(jnp.where(hit, gate_row, 0.0), axis=1, keepdims=True)
-        xc = [dot(pick, xd_ref[slot, 0, :, c], 1, 0).astype(BF16) for c in cols]
-        dyc = [dot(pick, xd_ref[slot, 1, :, c], 1, 0) for c in cols]
+        xc = [dot(pick, xd_ref[slot, 0, tok, c], 1, 0).astype(BF16) for c in cols]
+        dyc = [dot(pick, xd_ref[slot, 1, tok, c], 1, 0) for c in cols]
         hg = dot(xc[0], wg[0][0], 1, 0) + dot(xc[1], wg[1][0], 1, 0)
         hu = dot(xc[0], wu[0][0], 1, 0) + dot(xc[1], wu[1][0], 1, 0)
         sig = jax.nn.sigmoid(hg)
@@ -107,30 +107,43 @@
         dhu = (da * hg * sig).astype(BF16)
         o = [dot(act, w[0], 1, 0).astype(BF16) for w in wd]
         dgate_c = sum(jnp.sum(dyc[s] * o[s].astype(F32), axis=1, keepdims=True) for s in range(2))
-        dgate_ref[0, 0] += jnp.sum(jnp.where(hit, dgate_c, 0.0), axis=0, keepdims=True)
+        dgate_ref[0, 0, :, tok] += jnp.sum(jnp.where(hit, dgate_c, 0.0), axis=0, keepdims=True)
         db = [(dot(dhg, wg[s][0], 1, 1) + dot(dhu, wu[s][0], 1, 1)).astype(BF16) for s in range(2)]
         pl.when(first)(acc_ready)
         for s in range(2):
             acc_ref[e, s, 0] += dot(xc[s], dhg, 0, 0)
             acc_ref[e, s, 1] += dot(xc[s], dhu, 0, 0)
             acc_ref[e, s, 2] += dot(act, do[s], 0, 0)
-        gate_t = jnp.transpose(jnp.broadcast_to(gate_row, (8, BLK)))[:, :1]
+        gate_t = jnp.transpose(jnp.broadcast_to(gate_row, (8, n_tok)))[:, :1]
         width = 256
         for s in range(2):
             for c in range(half // width):
                 part = slice(c * width, (c + 1) * width)
                 out = slice(s * half + c * width, s * half + (c + 1) * width)
-                yd_ref[slot, 0, :, out] += gate_t * dot(pick, o[s][:, part], 0, 0)
-                yd_ref[slot, 1, :, out] += dot(pick, db[s][:, part], 0, 0)
+                yd_ref[slot, 0, tok, out] += gate_t * dot(pick, o[s][:, part], 0, 0)
+                yd_ref[slot, 1, tok, out] += dot(pick, db[s][:, part], 0, 0)
+
+    every = pl.ds(0, BLK)
 
     def full_tile(i, carry):
-        tile(i * TILE, TILE, i == 0)
+        tile(i * TILE, TILE, i == 0, every, BLK)
         return carry
 
     tiles = nt_ref[b, e]
+    start = win_ref[b, e]
     full = jnp.right_shift(tiles, 1)
     lax.fori_loop(0, full, full_tile, 0)
-    pl.when((tiles & 1) == 1)(lambda: tile(full * TILE, TILE // 2, full == 0))
+    rest_rows = (tiles & 1) == 1
+
+    @pl.when(rest_rows & (start >= 0))
+    def _():
+        tok = pl.ds(pl.multiple_of(jnp.maximum(start, 0), 128), NARROW)
+        tile(full * TILE, TILE // 2, full == 0, tok, NARROW)
+
+    @pl.when(rest_rows & (start < 0))
+    def _():
+        tile(full * TILE, TILE // 2, full == 0, every, BLK)
+
     pl.when(tiles == 0)(acc_ready)
 
     for k in range(n_blk):
@@ -153,18 +166,18 @@
                 c.wait()
 
 
-def experts(nt, pos, gate, toks, weights, e0, acc):
+def experts(nt, win, pos, gate, toks, weights, e0, acc):
     n_blk, n_exp = nt.shape
     d_model = toks[0].shape[2]
     half, d_ff = weights[0].shape[1:]
-    row = pl.BlockSpec((1, 1, 1, BLK), lambda b, e, nt: (b, e, 0, 0))
-    up = pl.BlockSpec((1, half, d_ff), lambda b, e, nt: (e + e0, 0, 0))
-    down = pl.BlockSpec((1, d_ff, half), lambda b, e, nt: (e + e0, 0, 0))
+    row = pl.BlockSpec((1, 1, 1, BLK), lambda b, e, nt, win: (b, e, 0, 0))
+    up = pl.BlockSpec((1, half, d_ff), lambda b, e, nt, win: (e + e0, 0, 0))
+    down = pl.BlockSpec((1, d_ff, half), lambda b, e, nt, win: (e + e0, 0, 0))
     hbm = pl.BlockSpec(memory_space=pl.ANY)
     fresh = tuple(a is None for a in acc)
     acc_args = [r for a in acc if a is not None for r in a]
     acc_shape = jax.ShapeDtypeStruct((2, 3, half, d_ff), F32)
-    first_in = 1 + 8 + n_blk
+    first_in = 2 + 8 + n_blk
     first_out = n_blk + 1
     aliases = {}
     for p, a in enumerate(acc):
@@ -175,7 +188,7 @@
     res = pl.pallas_call(
         functools.partial(expert_kernel, n_blk, n_exp, fresh),
         grid_spec=pltpu.PrefetchScalarGridSpec(
-            num_scalar_prefetch=1,
+            num_scalar_prefetch=2,
             grid=(n_blk, n_exp),
             in_specs=[row, row, up, up, up, up, down, down] + [hbm] * (n_blk + len(acc_args)),
             out_specs=[hbm] * n_blk + [row] + [hbm] * (2 * len(acc)),
@@ -195,7 +208,7 @@
         compiler_params=pltpu.CompilerParams(
             dimension_semantics=("arbitrary", "arbitrary"), vmem_limit_bytes=67_000_000),
         cost_estimate=pl.CostEstimate(flops=100_000_000, bytes_accessed=80_000_000, transcendentals=1_000_000),
-    )(nt, pos, gate, *weights, *toks, *acc_args)
+    )(nt, win, pos, gate, *weights, *toks, *acc_args)
     toks_out, dgate, acc = res[:n_blk], res[n_blk], res[n_blk + 1:]
     return toks_out, dgate, [acc[2 * p:2 * p + 2] for p in range(len(acc) // 2)]
 
@@ -273,14 +286,20 @@
 
         def blocked(m):
             m = m.reshape(-1, local_exp, 2, halves, BLK).transpose(3, 0, 1, 2, 4)
-            nt = ((jnp.max(m[..., 0, :], axis=-1) + TILE // 2) / (TILE // 2)).astype(jnp.int32)
-            return nt, m[..., 0:1, :], m[..., 1:2, :]
+            place = m[..., 0, :]
+            nt = jnp.floor((jnp.max(place, axis=-1) + TILE // 2) / (TILE // 2))
+            at = jnp.arange(BLK, dtype=jnp.int32)
+            inside = place >= jnp.floor(nt / 2)[..., None] * TILE
+            lo = jnp.min(jnp.where(inside, at, BLK), axis=-1)
+            hi = jnp.max(jnp.where(inside, at, -1), axis=-1)
+            start = jnp.minimum(lo // 128 * 128, BLK - NARROW)
+            return nt.astype(jnp.int32), jnp.where(hi - start < NARROW, start, -1), m[..., 0:1, :], m[..., 1:2, :]
 
         metas = [blocked(jnp.stack([own_meta, peer_meta])), None]
 
         def meta_of(sets, e_lo, e_hi):
             out = []
-            for j in range(3):
+            for j in range(4):
                 rows = [metas[k != 0][j][h, k:k + 2, e_lo:e_hi] for k, h in sets]
                 out.append(jnp.concatenate(rows, axis=0))
             return out
@@ -308,7 +327,7 @@
 
         stat_bits = [1, X, Y]
         for n, (sets, e_lo, e_hi) in enumerate(calls):
-            nt, pos_k, gate_k = meta_of(sets, e_lo, e_hi)
+            nt, win, pos_k, gate_k = meta_of(sets, e_lo, e_hi)
             if n in (3, 4):
                 ready = calls[n - 1][0]
                 nt, done = lax.optimization_barrier((nt, [part[n - 1, k, h] for k, h in ready]))
@@ -317,7 +336,7 @@
             toks = [xd[k + c, h] for k, h in sets for c in range(2)]
             pairs = slice(e_lo // 2, e_hi // 2)
             outs, dgate[n], acc[pairs] = experts(
-                nt, pos_k, gate_k, toks, first_weights if n < 2 else weights, e_lo, acc[pairs])
+                nt, win, pos_k, gate_k, toks, first_weights if n < 2 else weights, e_lo, acc[pairs])
             for j, (k, h) in enumerate(sets):
                 raw[n, k, h] = outs[2 * j:2 * j + 2]
             if n not in (4, 5):

time: 1480 us -> 1410 us (0.953)
  starting transfers between devices: 241 us -> 177 us
    ppermute x43, starting transfers between devices: 209 us -> 144 us  [hop(): return lax.ppermute(a, 'ep', [(i, i ^ bit) for i in range(8)])]
    all_to_all x1, waiting for transfers between devices: 39.9 us -> 0.01 us  [local_step(): far_meta = lax.all_to_all(meta, 'ep', 0, 0, tiled=True)]
    ppermute x43, waiting for transfers between devices: 347 us -> 373 us  [hop(): return lax.ppermute(a, 'ep', [(i, i ^ bit) for i in range(8)])]
  transfers between devices with their start and end apart: 55 -> 55, of which waited for: 21 -> 21; matrix products, arithmetic and copies ran while one was open for 17% -> 17% of each run, Pallas kernels for 31% -> 33%
where the time goes in v3:
time: 1410 us; the launch traced here: 1400 us
  waiting for transfers between devices  495 us (35%)
  Pallas kernels  457 us (32%)
  other arithmetic  193 us (14%)
  starting transfers between devices  177 us (13%)
  local copies, waits for them, and re-layouts  48.6 us (3%)
  between operations  17.2 us (1%)
    pallas_call x7, Pallas kernels, experts(): pl.pallas_call(functools.partial(expert_kernel, n_blk, n_exp, fresh), gri...  457 us
    ppermute x43, waiting for transfers between devices, hop(): return lax.ppermute(a, 'ep', [(i, i ^ bit) for i in range(8)])  373 us
    ppermute x43, starting transfers between devices, hop(): return lax.ppermute(a, 'ep', [(i, i ^ bit) for i in range(8)])  144 us
    ppermute x9, waiting for transfers between devices, hop_z(): return lax.ppermute(a, 'fsdp', [(0, 1), (1, 0)])  73 us
    all_to_all x1, waiting for transfers between devices, local_step(): far = lax.all_to_all(far, 'ep', 0, 0, tiled=True)  48.6 us
    add x4, other arithmetic, reduce_core(): part[n, k, h] = [mine[i] + other[i] for i in range(2)]  48.4 us
    add x2, other arithmetic, local_step(): part[h, 0, h][i] + part[6, 0, h][i] + direct[i][h]  39.6 us
    add x4, other arithmetic, local_step(): m0[i] + o0[i] + (m1[i] + o1[i]) + d  34.3 us
  transfers between devices with their start and end apart: 55, of which 21 were waited for; matrix products, arithmetic and copies ran while one was open for 17% of the time, Pallas kernels for 33%

profile of v3, /device:TPU:0, one launch (start us, length us, event | category | flops | bytes accessed | tf_op | source)
XLA Modules:
  0.0 1399.9 jit_solution(9913528430492348249)
XLA Ops:
  34.6 22.5 %collective-permute-done.1.wg1_ref = bf16[2,512,512]{2,1,0:T(8,128)(2,1)S(1)} collective-permute-done((bf16[2,512,512]{2,1,0:T(8,128)(2,1)S(1)}, bf16[2,512,512]{2,1,0:T(8,128)(2,1)S(1)}, u32[]{:S(2)}, u32[]{:S(2)}) %collective-permute-start.1) | collective-permute-done | bytes 1048608 | tf_op jit(solution)/shard_map/ppermute | solution.py:229
  59.9 21.8 %collective-permute-done.2.wu1_ref = bf16[2,512,512]{2,1,0:T(8,128)(2,1)S(1)} collective-permute-done((bf16[2,512,512]{2,1,0:T(8,128)(2,1)S(1)}, bf16[2,512,512]{2,1,0:T(8,128)(2,1)S(1)}, u32[]{:S(2)}, u32[]{:S(2)}) %collective-permute-start.2) | collective-permute-done | bytes 1048608 | tf_op jit(solution)/shard_map/ppermute | solution.py:229
  85.5 4.1 all-to-all-start
  90.4 16.1 %collective-permute-done.3.wd1_ref = bf16[2,512,512]{2,1,0:T(8,128)(2,1)} collective-permute-done((bf16[2,512,512]{2,1,0:T(8,128)(2,1)S(1)}, bf16[2,512,512]{2,1,0:T(8,128)(2,1)}, u32[]{:S(2)}, u32[]{:S(2)}) %collective-permute-start.3) | collective-permute-done | bytes 1048608 | tf_op jit(solution)/shard_map/ppermute | solution.py:229
  113.5 35.1 %shard_map.135 = (f32[2,1024,1024]{2,1,0:T(8,128)}, f32[2,1024,1024]{2,1,0:T(8,128)}, f32[2,2,1,1024]{3,2,1,0:T(1,128)}, f32[2,3,512,512]{3,2,1,0:T(8,128)}, f32[2,3,512,512]{3,2,1,0:T(8,128)}) custom-call(s32[2,2]{1,0:T(2,128)} %get-tuple-element.328.nt_ref, s32[2,2]{1,0:T(2,128)} %get-tuple-element.324.win_ref, ...), custom_call_target="tpu_custom_call" | custom-call | flops 100000000 | bytes 80000000 | tf_op jit(solution)/shard_map/pallas_call | solution.py:188
  156.0 35.6 %shard_map.136 = (f32[2,1024,1024]{2,1,0:T(8,128)}, f32[2,1024,1024]{2,1,0:T(8,128)}, f32[2,2,1,1024]{3,2,1,0:T(1,128)}, f32[2,3,512,512]{3,2,1,0:T(8,128)}, f32[2,3,512,512]{3,2,1,0:T(8,128)}) custom-call(s32[2,2]{1,0:T(2,128)} %get-tuple-element.326.nt_ref, s32[2,2]{1,0:T(2,128)} %get-tuple-element.322.win_ref, ...), custom_call_target="tpu_custom_call", output_to_operand_aliasing={{3}: (12, {}), {4}: (13, {})} | custom-call | flops 100000000 | bytes 80000000 | tf_op jit(solution)/shard_map/pallas_call | solution.py:188
  191.6 8.4 collective-permute-start.10
  215.5 104.2 %shard_map.137 = (f32[2,1024,1024]{2,1,0:T(8,128)}, f32[2,1024,1024]{2,1,0:T(8,128)}, f32[2,1024,1024]{2,1,0:T(8,128)}, f32[2,1024,1024]{2,1,0:T(8,128)}, f32[4,...) custom-call(s32[4,4]{1,0:T(4,128)} %pad_add_fusion.4.nt_ref, ...), custom_call_target="tpu_custom_call", output_to_operand_aliasing={{5}: (14, {}), {6}: (15, {})} | custom-call | flops 100000000 | bytes 80000000 | tf_op jit(solution)/shard_map/pallas_call | solution.py:188
  319.7 8.7 collective-permute-start.20
  328.4 20.3 %collective-permute-start.18 = (bf16[2,1024,1024]{2,1,0:T(8,128)(2,1)}, bf16[2,1024,1024]{2,1,0:T(8,128)(2,1)}, u32[]{:S(2)}, u32[]{:S(2)}) collective-permute-start(bf16[2,1024,1024]{2,1,0:T(8,128)(2,1)} %fusion.5.rest_0_.rest_2_), channel_id=1, source_target_pairs={{0,2},{1,3},{2,0},{3,1},{4,6},{5,7},{6,4},{7,5},{8,10},{9,11},{10,... | collective-permute-start | bytes 12582920 | tf_op jit(solution)/shard_map/ppermute | solution.py:225
  349.4 25.2 %collective-permute-done.14.rest_0_ = bf16[2,1024,1024]{2,1,0:T(8,128)(2,1)} collective-permute-done((bf16[2,1024,1024]{2,1,0:T(8,128)(2,1)}, bf16[2,1024,1024]{2,1,0:T(8,128)(2,1)}, u32[]{:S(2)}, u32[]{:S(2)}) %collective-permute-start.14) | collective-permute-done | bytes 4194336 | tf_op jit(solution)/shard_map/ppermute | solution.py:225
  377.7 62.2 %collective-permute-done.42 = f32[2,32]{1,0:T(2,128)S(1)} collective-permute-done((f32[2,32]{1,0:T(2,128)S(1)}, f32[2,32]{1,0:T(2,128)S(1)}, u32[]{:S(2)}, u32[]{:S(2)}) %collective-permute-start.42) | collective-permute-done | bytes 288 | tf_op jit(solution)/shard_map/ppermute | solution.py:225
  446.9 12.0 fusion.33
  459.1 12.2 fusion.31
  481.0 105.1 %shard_map.138 = (f32[2,1024,1024]{2,1,0:T(8,128)}, f32[2,1024,1024]{2,1,0:T(8,128)}, f32[2,1024,1024]{2,1,0:T(8,128)}, f32[2,1024,1024]{2,1,0:T(8,128)}, f32[4,...) custom-call(s32[4,4]{1,0:T(4,128)} %pad_add_fusion.6.nt_ref, ...), custom_call_target="tpu_custom_call", output_to_operand_aliasing={{5}: (14, {}), {6}: (15, {}), {7}: (16, {}), {8}: (17, {})} | custom-call | flops 100000000 | bytes 80000000 | tf_op jit(solution)/shard_map/pallas_call | solution.py:188
  586.1 19.9 %collective-permute-start.28 = (f32[1024,1024]{1,0:T(8,128)}, f32[1024,1024]{1,0:T(8,128)}, u32[]{:S(2)}, u32[]{:S(2)}) collective-permute-start(f32[1024,1024]{1,0:T(8,128)} %get-tuple-element.151), channel_id=1, source_target_pairs={{0,4},{1,5},{2,6},{3,7},{4,0},{5,1},{6,2},{7,3},{8,12},{9,13},{10,... | collective-permute-start | bytes 12582920 | tf_op jit(solution)/shard_map/ppermute | solution.py:225
  607.2 10.1 collective-permute-start.29
  617.9 58.9 %shard_map.139 = (f32[2,1024,1024]{2,1,0:T(8,128)}, f32[2,1024,1024]{2,1,0:T(8,128)}, f32[2,1024,1024]{2,1,0:T(8,128)}, f32[2,1024,1024]{2,1,0:T(8,128)}, f32[4,...) custom-call(s32[4,2]{1,0:T(4,128)} %pad_add_fusion.2.nt_ref, ...), custom_call_target="tpu_custom_call", output_to_operand_aliasing={{5}: (14, {}), {6}: (15, {})} | custom-call | flops 100000000 | bytes 80000000 | tf_op jit(solution)/shard_map/pallas_call | solution.py:188
  676.8 59.2 %shard_map.140 = (f32[2,1024,1024]{2,1,0:T(8,128)}, f32[2,1024,1024]{2,1,0:T(8,128)}, f32[2,1024,1024]{2,1,0:T(8,128)}, f32[2,1024,1024]{2,1,0:T(8,128)}, f32[4,...) custom-call(s32[4,2]{1,0:T(4,128)} %pad_add_fusion.nt_ref, ...), custom_call_target="tpu_custom_call", output_to_operand_aliasing={{5}: (14, {}), {6}: (15, {})} | custom-call | flops 100000000 | bytes 80000000 | tf_op jit(solution)/shard_map/pallas_call | solution.py:188
  737.0 4.9 collective-permute-start.44
  743.4 23.4 %collective-permute-start.49 = (f32[4,2048]{1,0:T(4,128)S(1)}, f32[4,2048]{1,0:T(4,128)S(1)}, u32[]{:S(2)}, u32[]{:S(2)}) collective-permute-start(f32[4,2048]{1,0:T(4,128)S(1)} %bitcast.294), channel_id=1, source_target_pairs={{0,1},{1,0},{2,3},{3,2},{4,5},{5,4},{6,7},{7,6},{8,9},{9,8},{10,11... | collective-permute-start | bytes 98312 | tf_op jit(solution)/shard_map/ppermute | solution.py:225
  768.0 18.3 %collective-permute-start.30 = (f32[1024,1024]{1,0:T(8,128)}, f32[1024,1024]{1,0:T(8,128)}, u32[]{:S(2)}, u32[]{:S(2)}) collective-permute-start(f32[1024,1024]{1,0:T(8,128)} %get-tuple-element.153), channel_id=1, source_target_pairs={{0,4},{1,5},{2,6},{3,7},{4,0},{5,1},{6,2},{7,3},{8,12},{9,13},{10,... | collective-permute-start | bytes 12582920 | tf_op jit(solution)/shard_map/ppermute | solution.py:225
  786.4 6.8 copy.53
  795.2 82.5 %collective-permute-done.30 = f32[1024,1024]{1,0:T(8,128)} collective-permute-done((f32[1024,1024]{1,0:T(8,128)}, f32[1024,1024]{1,0:T(8,128)}, u32[]{:S(2)}, u32[]{:S(2)}) %collective-permute-start.30) | collective-permute-done | bytes 4194336 | tf_op jit(solution)/shard_map/ppermute | solution.py:225
  880.7 12.1 fusion.17
  892.9 12.1 fusion.15
  905.0 58.9 %shard_map.141 = (f32[2,1024,1024]{2,1,0:T(8,128)}, f32[2,1024,1024]{2,1,0:T(8,128)}, f32[2,1024,1024]{2,1,0:T(8,128)}, f32[2,1024,1024]{2,1,0:T(8,128)}, f32[4,...) custom-call(s32[4,2]{1,0:T(4,128)} %pad_add_fusion.8.nt_ref, ...), custom_call_target="tpu_custom_call", output_to_operand_aliasing={{5}: (14, {}), {6}: (15, {})} | custom-call | flops 100000000 | bytes 80000000 | tf_op jit(solution)/shard_map/pallas_call | solution.py:188
  970.7 5.7 fusion.3
  977.5 12.8 collective-permute-start.37
  991.1 4.8 all-to-all-start.1
  996.0 20.0 %fusion.24 = (f32[1024,1024]{1,0:T(8,128)}, f32[1024,1024]{1,0:T(8,128)}) fusion(f32[1024,1024]{1,0:T(8,128)} %collective-permute-done.29, f32[2,1024,1024]{2,1,0:T(8,128)} %collective-permute-done.24, f32[2,1024,1024]{2,1,0:T(8,128)} %collective-permute-done.5, f32[2,1024,1024]{2,1,0:T(8,128)} %get-tuple-element.144, ...), kind=kLoop, calls=%fused_computation.57 | loop fusion | flops 8388608 | bytes 50331648 | tf_op jit(solution)/shard_map/add | solution.py:401
  1018.1 19.6 %fusion.21 = (f32[1024,1024]{1,0:T(8,128)}, f32[1024,1024]{1,0:T(8,128)}) fusion(f32[1024,1024]{1,0:T(8,128)} %collective-permute-done.30, f32[2,1024,1024]{2,1,0:T(8,128)} %collective-permute-done.27, f32[2,1024,1024]{2,1,0:T(8,128)} %collective-permute-done.26, f32[2,1024,1024]{2,1,0:T(8,128)} %get-tuple-element.149, ...), kind=kLoop, calls=%fused_computation.52 | loop fusion | flops 8388608 | bytes 50331648 | tf_op jit(solution)/shard_map/add | solution.py:401
  1039.1 48.6 %all-to-all-done.1 = f32[8,4,2048]{2,1,0:T(4,128)S(1)} async-done(((f32[8,4,2048]{2,1,0:T(4,128)}), f32[8,4,2048]{2,1,0:T(4,128)S(1)}, u32[]{:S(2)}, u32[]{:S(2)}) %all-to-all-start.1) | async-done | bytes 262176 | tf_op jit(solution)/shard_map/all_to_all | solution.py:388
  1088.0 8.5 collective-permute-start.50
  1096.8 10.7 fusion.14
  1111.3 7.4 fusion.11
  1122.0 52.7 %collective-permute-done.45 = f32[1024,1024]{1,0:T(8,128)} collective-permute-done((f32[1024,1024]{1,0:T(8,128)}, f32[1024,1024]{1,0:T(8,128)}, u32[]{:S(2)}, u32[]{:S(2)}) %collective-permute-start.45) | collective-permute-done | bytes 4194336 | tf_op jit(solution)/shard_map/ppermute | solution.py:225
  1174.7 8.8 bitcast_add_fusion.1
  1183.5 17.6 %collective-permute-done.46 = f32[1024,1024]{1,0:T(8,128)} collective-permute-done((f32[1024,1024]{1,0:T(8,128)}, f32[1024,1024]{1,0:T(8,128)}, u32[]{:S(2)}, u32[]{:S(2)}) %collective-permute-start.46) | collective-permute-done | bytes 4194336 | tf_op jit(solution)/shard_map/ppermute | solution.py:225
  1201.1 7.4 bitcast_add_fusion
  1220.2 11.1 collective-permute-done.50
  1231.3 5.7 add_convert_fusion
  1242.0 23.4 %collective-permute-done.40 = f32[1024,1024]{1,0:T(8,128)} collective-permute-done((f32[1024,1024]{1,0:T(8,128)}, f32[1024,1024]{1,0:T(8,128)}, u32[]{:S(2)}, u32[]{:S(2)}) %collective-permute-start.40) | collective-permute-done | bytes 4194336 | tf_op jit(solution)/shard_map/ppermute | solution.py:225
  1268.3 24.1 %collective-permute-done.39 = f32[1024,1024]{1,0:T(8,128)} collective-permute-done((f32[1024,1024]{1,0:T(8,128)}, f32[1024,1024]{1,0:T(8,128)}, u32[]{:S(2)}, u32[]{:S(2)}) %collective-permute-start.39) | collective-permute-done | bytes 4194336 | tf_op jit(solution)/shard_map/ppermute | solution.py:225
  1295.9 7.9 fusion.4
  1303.8 51.9 %collective-permute-done.48 = f32[1024,1024]{1,0:T(8,128)} collective-permute-done((f32[1024,1024]{1,0:T(8,128)}, f32[1024,1024]{1,0:T(8,128)}, u32[]{:S(2)}, u32[]{:S(2)}) %collective-permute-start.48) | collective-permute-done | bytes 4194336 | tf_op jit(solution)/shard_map/ppermute | solution.py:225
  1358.8 23.0 %collective-permute-done.47 = f32[1024,1024]{1,0:T(8,128)} collective-permute-done((f32[1024,1024]{1,0:T(8,128)}, f32[1024,1024]{1,0:T(8,128)}, u32[]{:S(2)}, u32[]{:S(2)}) %collective-permute-start.47) | collective-permute-done | bytes 4194336 | tf_op jit(solution)/shard_map/ppermute | solution.py:225
  1386.2 3.9 fusion.2
  (345 shorter events, 146.5 us)
Async XLA Ops:
  14.4 95.0 %collective-permute-start.11 = (bf16[2,1024,1024]{2,1,0:T(8,128)(2,1)}, bf16[2,1024,1024]{2,1,0:T(8,128)(2,1)}, u32[]{:S(2)}, u32[]{:S(2)}) collective-permute-start(bf16[2,1024,1024]{2,1,0:T(8,128)(2,1)} %fusion.5.rest_0_.rest_2_), channel_id=1, source_target_pairs={{0,4},{1,5},{2,6},{3,7},{4,0},{5,1},{6,2},{7,3},{8,12},{9,13},{10,... | collective-permute-start | bytes 12582920 | tf_op jit(solution)/shard_map/ppermute | solution.py:225
  17.6 131.1 %collective-permute-start.9 = (bf16[2,1024,1024]{2,1,0:T(8,128)(2,1)}, bf16[2,1024,1024]{2,1,0:T(8,128)(2,1)}, u32[]{:S(2)}, u32[]{:S(2)}) collective-permute-start(bf16[2,1024,1024]{2,1,0:T(8,128)(2,1)} %fusion.5.rest_0_.rest_2_), channel_id=1, source_target_pairs={{0,1},{1,0},{2,3},{3,2},{4,5},{5,4},{6,7},{7,6},{8,9},{9,8},{10,11... | collective-permute-start | bytes 12582920 | tf_op jit(solution)/shard_map/ppermute | solution.py:225
  21.0 127.6 %collective-permute-start.13 = (bf16[2,1024,1024]{2,1,0:T(8,128)(2,1)}, bf16[2,1024,1024]{2,1,0:T(8,128)(2,1)}, u32[]{:S(2)}, u32[]{:S(2)}) collective-permute-start(bf16[2,1024,1024]{2,1,0:T(8,128)(2,1)} %fusion.6.rest_0_), channel_id=1, source_target_pairs={{0,2},{1,3},{2,0},{3,1},{4,6},{5,7},{6,4},{7,5},{8,10},{9,11},{10,... | collective-permute-start | bytes 12582920 | tf_op jit(solution)/shard_map/ppermute | solution.py:225
  22.5 89.0 %collective-permute-start.4 = (bf16[2,1024,1024]{2,1,0:T(8,128)(2,1)}, bf16[2,1024,1024]{2,1,0:T(8,128)(2,1)}, u32[]{:S(2)}, u32[]{:S(2)}) collective-permute-start(bf16[2,1024,1024]{2,1,0:T(8,128)(2,1)} %fusion.6.rest_0_), channel_id=1, source_target_pairs={{0,1},{1,0},{2,3},{3,2},{4,5},{5,4},{6,7},{7,6},{8,9},{9,8},{10,11... | collective-permute-start | bytes 12582920 | tf_op jit(solution)/shard_map/ppermute | solution.py:225
  31.8 25.3 %collective-permute-start.1 = (bf16[2,512,512]{2,1,0:T(8,128)(2,1)S(1)}, bf16[2,512,512]{2,1,0:T(8,128)(2,1)S(1)}, u32[]{:S(2)}, u32[]{:S(2)}) collective-permute-start(bf16[2,512,512]{2,1,0:T(8,128)(2,1)S(1)} %get-tuple-element.251), channel_id=1, source_target_pairs={{0,8},{8,0},{1,9},{9,1},{2,10},{10,2},{3,11},{11,3},{4,12},{12,4},... | collective-permute-start | bytes 3145736 | tf_op jit(solution)/shard_map/ppermute | solution.py:229
  85.5 114.5 %all-to-all-start = ((f32[8,4,2,2048]{3,2,1,0:T(2,128)}), f32[8,4,2,2048]{3,2,1,0:T(2,128)}, u32[]{:S(2)}, u32[]{:S(2)}) async-start(f32[8,4,2,2048]{3,2,1,0:T(2,128)} %pad_maximum_fusion.7), calls=%async_computation | async-start | bytes 1048576 | tf_op jit(solution)/shard_map/all_to_all | solution.py:285
  106.5 85.1 %collective-permute-start.6 = (bf16[2,512,512]{2,1,0:T(8,128)(2,1)}, bf16[2,512,512]{2,1,0:T(8,128)(2,1)}, u32[]{:S(2)}, u32[]{:S(2)}) collective-permute-start(bf16[2,512,512]{2,1,0:T(8,128)(2,1)} %get-tuple-element.252), channel_id=1, source_target_pairs={{0,8},{8,0},{1,9},{9,1},{2,10},{10,2},{3,11},{11,3},{4,12},{12,4},... | collective-permute-start | bytes 3145736 | tf_op jit(solution)/shard_map/ppermute | solution.py:229
  109.4 90.7 %collective-permute-start.7 = (bf16[2,512,512]{2,1,0:T(8,128)(2,1)}, bf16[2,512,512]{2,1,0:T(8,128)(2,1)}, u32[]{:S(2)}, u32[]{:S(2)}) collective-permute-start(bf16[2,512,512]{2,1,0:T(8,128)(2,1)} %get-tuple-element.250), channel_id=1, source_target_pairs={{0,8},{8,0},{1,9},{9,1},{2,10},{10,2},{3,11},{11,3},{4,12},{12,4},... | collective-permute-start | bytes 3145736 | tf_op jit(solution)/shard_map/ppermute | solution.py:229
  111.4 88.6 %collective-permute-start.8 = (bf16[2,512,512]{2,1,0:T(8,128)(2,1)}, bf16[2,512,512]{2,1,0:T(8,128)(2,1)}, u32[]{:S(2)}, u32[]{:S(2)}) collective-permute-start(bf16[2,512,512]{2,1,0:T(8,128)(2,1)} %get-tuple-element.248), channel_id=1, source_target_pairs={{0,8},{8,0},{1,9},{9,1},{2,10},{10,2},{3,11},{11,3},{4,12},{12,4},... | collective-permute-start | bytes 3145736 | tf_op jit(solution)/shard_map/ppermute | solution.py:229
  148.6 66.9 %collective-permute-start.15 = (bf16[2,1024,1024]{2,1,0:T(8,128)(2,1)}, bf16[2,1024,1024]{2,1,0:T(8,128)(2,1)}, u32[]{:S(2)}, u32[]{:S(2)}) collective-permute-start(bf16[2,1024,1024]{2,1,0:T(8,128)(2,1)} %collective-permute-done.13.rest_0_), channel_id=1, source_target_pairs={{0,1},{1,0},{2,3},{3,2},{4,5},{5,4},{6,7},{7,6},{8,9},{9,8},{10,11... | collective-permute-start | bytes 12582920 | tf_op jit(solution)/shard_map/ppermute | solution.py:225
  148.7 66.8 %collective-permute-start.16 = (bf16[2,1024,1024]{2,1,0:T(8,128)(2,1)}, bf16[2,1024,1024]{2,1,0:T(8,128)(2,1)}, u32[]{:S(2)}, u32[]{:S(2)}) collective-permute-start(bf16[2,1024,1024]{2,1,0:T(8,128)(2,1)} %collective-permute-done.11.rest_2_), channel_id=1, source_target_pairs={{0,1},{1,0},{2,3},{3,2},{4,5},{5,4},{6,7},{7,6},{8,9},{9,8},{10,11... | collective-permute-start | bytes 12582920 | tf_op jit(solution)/shard_map/ppermute | solution.py:225
  191.6 184.3 %collective-permute-start.10 = (bf16[2,1024,1024]{2,1,0:T(8,128)(2,1)}, bf16[2,1024,1024]{2,1,0:T(8,128)(2,1)}, u32[]{:S(2)}, u32[]{:S(2)}) collective-permute-start(bf16[2,1024,1024]{2,1,0:T(8,128)(2,1)} %fusion.6.rest_0_), channel_id=1, source_target_pairs={{0,4},{1,5},{2,6},{3,7},{4,0},{5,1},{6,2},{7,3},{8,12},{9,13},{10,... | collective-permute-start | bytes 12582920 | tf_op jit(solution)/shard_map/ppermute | solution.py:225
  200.0 128.4 %collective-permute-start.12 = (bf16[2,1024,1024]{2,1,0:T(8,128)(2,1)}, bf16[2,1024,1024]{2,1,0:T(8,128)(2,1)}, u32[]{:S(2)}, u32[]{:S(2)}) collective-permute-start(bf16[2,1024,1024]{2,1,0:T(8,128)(2,1)} %collective-permute-done.11.rest_2_), channel_id=1, source_target_pairs={{0,2},{1,3},{2,0},{3,1},{4,6},{5,7},{6,4},{7,5},{8,10},{9,11},{10,... | collective-permute-start | bytes 12582920 | tf_op jit(solution)/shard_map/ppermute | solution.py:225
  200.1 174.5 %collective-permute-start.14 = (bf16[2,1024,1024]{2,1,0:T(8,128)(2,1)}, bf16[2,1024,1024]{2,1,0:T(8,128)(2,1)}, u32[]{:S(2)}, u32[]{:S(2)}) collective-permute-start(bf16[2,1024,1024]{2,1,0:T(8,128)(2,1)} %collective-permute-done.13.rest_0_), channel_id=1, source_target_pairs={{0,4},{1,5},{2,6},{3,7},{4,0},{5,1},{6,2},{7,3},{8,12},{9,13},{10,... | collective-permute-start | bytes 12582920 | tf_op jit(solution)/shard_map/ppermute | solution.py:225
  319.7 125.4 %collective-permute-start.20 = (f32[2,1024,1024]{2,1,0:T(8,128)}, f32[2,1024,1024]{2,1,0:T(8,128)}, u32[]{:S(2)}, u32[]{:S(2)}) collective-permute-start(f32[2,1024,1024]{2,1,0:T(8,128)} %get-tuple-element.130), channel_id=1, source_target_pairs={{0,1},{1,0},{2,3},{3,2},{4,5},{5,4},{6,7},{7,6},{8,9},{9,8},{10,11... | collective-permute-start | bytes 25165832 | tf_op jit(solution)/shard_map/ppermute | solution.py:225
  328.4 116.8 %collective-permute-start.21 = (f32[2,1024,1024]{2,1,0:T(8,128)}, f32[2,1024,1024]{2,1,0:T(8,128)}, u32[]{:S(2)}, u32[]{:S(2)}) collective-permute-start(f32[2,1024,1024]{2,1,0:T(8,128)} %get-tuple-element.132), channel_id=1, source_target_pairs={{0,1},{1,0},{2,3},{3,2},{4,5},{5,4},{6,7},{7,6},{8,9},{9,8},{10,11... | collective-permute-start | bytes 25165832 | tf_op jit(solution)/shard_map/ppermute | solution.py:225
  328.4 111.4 %collective-permute-start.18 = (bf16[2,1024,1024]{2,1,0:T(8,128)(2,1)}, bf16[2,1024,1024]{2,1,0:T(8,128)(2,1)}, u32[]{:S(2)}, u32[]{:S(2)}) collective-permute-start(bf16[2,1024,1024]{2,1,0:T(8,128)(2,1)} %fusion.5.rest_0_.rest_2_), channel_id=1, source_target_pairs={{0,2},{1,3},{2,0},{3,1},{4,6},{5,7},{6,4},{7,5},{8,10},{9,11},{10,... | collective-permute-start | bytes 12582920 | tf_op jit(solution)/shard_map/ppermute | solution.py:225
  375.8 68.8 %collective-permute-start.23 = (bf16[2,1024,1024]{2,1,0:T(8,128)(2,1)}, bf16[2,1024,1024]{2,1,0:T(8,128)(2,1)}, u32[]{:S(2)}, u32[]{:S(2)}) collective-permute-start(bf16[2,1024,1024]{2,1,0:T(8,128)(2,1)} %collective-permute-done.12.rest_2_), channel_id=1, source_target_pairs={{0,1},{1,0},{2,3},{3,2},{4,5},{5,4},{6,7},{7,6},{8,9},{9,8},{10,11... | collective-permute-start | bytes 12582920 | tf_op jit(solution)/shard_map/ppermute | solution.py:225
  376.0 63.9 %collective-permute-start.42 = (f32[2,32]{1,0:T(2,128)S(1)}, f32[2,32]{1,0:T(2,128)S(1)}, u32[]{:S(2)}, u32[]{:S(2)}) collective-permute-start(f32[2,32]{1,0:T(2,128)S(1)} %add.328), channel_id=1, source_target_pairs={{0,2},{1,3},{2,0},{3,1},{4,6},{5,7},{6,4},{7,5},{8,10},{9,11},{10,... | collective-permute-start | bytes 776 | tf_op jit(solution)/shard_map/ppermute | solution.py:225
  439.8 146.3 %collective-permute-start.5 = (f32[2,1024,1024]{2,1,0:T(8,128)}, f32[2,1024,1024]{2,1,0:T(8,128)}, u32[]{:S(2)}, u32[]{:S(2)}) collective-permute-start(f32[2,1024,1024]{2,1,0:T(8,128)} %get-tuple-element.110), channel_id=1, source_target_pairs={{0,1},{1,0},{2,3},{3,2},{4,5},{5,4},{6,7},{7,6},{8,9},{9,8},{10,11... | collective-permute-start | bytes 25165832 | tf_op jit(solution)/shard_map/ppermute | solution.py:225
  444.6 292.4 %collective-permute-start.26 = (f32[2,1024,1024]{2,1,0:T(8,128)}, f32[2,1024,1024]{2,1,0:T(8,128)}, u32[]{:S(2)}, u32[]{:S(2)}) collective-permute-start(f32[2,1024,1024]{2,1,0:T(8,128)} %get-tuple-element.148), channel_id=1, source_target_pairs={{0,1},{1,0},{2,3},{3,2},{4,5},{5,4},{6,7},{7,6},{8,9},{9,8},{10,11... | collective-permute-start | bytes 25165832 | tf_op jit(solution)/shard_map/ppermute | solution.py:225
  444.6 26.7 %collective-permute-start.22 = (bf16[2,1024,1024]{2,1,0:T(8,128)(2,1)}, bf16[2,1024,1024]{2,1,0:T(8,128)(2,1)}, u32[]{:S(2)}, u32[]{:S(2)}) collective-permute-start(bf16[2,1024,1024]{2,1,0:T(8,128)(2,1)} %collective-permute-done.14.rest_0_), channel_id=1, source_target_pairs={{0,1},{1,0},{2,3},{3,2},{4,5},{5,4},{6,7},{7,6},{8,9},{9,8},{10,11... | collective-permute-start | bytes 12582920 | tf_op jit(solution)/shard_map/ppermute | solution.py:225
  445.1 160.9 %collective-permute-start.19 = (bf16[2,1024,1024]{2,1,0:T(8,128)(2,1)}, bf16[2,1024,1024]{2,1,0:T(8,128)(2,1)}, u32[]{:S(2)}, u32[]{:S(2)}) collective-permute-start(bf16[2,1024,1024]{2,1,0:T(8,128)(2,1)} %collective-permute-done.18.rest_2_), channel_id=1, source_target_pairs={{0,1},{1,0},{2,3},{3,2},{4,5},{5,4},{6,7},{7,6},{8,9},{9,8},{10,11... | collective-permute-start | bytes 12582920 | tf_op jit(solution)/shard_map/ppermute | solution.py:225
  445.1 162.0 %collective-permute-start.17 = (bf16[2,1024,1024]{2,1,0:T(8,128)(2,1)}, bf16[2,1024,1024]{2,1,0:T(8,128)(2,1)}, u32[]{:S(2)}, u32[]{:S(2)}) collective-permute-start(bf16[2,1024,1024]{2,1,0:T(8,128)(2,1)} %collective-permute-done.10.rest_0_), channel_id=1, source_target_pairs={{0,1},{1,0},{2,3},{3,2},{4,5},{5,4},{6,7},{7,6},{8,9},{9,8},{10,11... | collective-permute-start | bytes 12582920 | tf_op jit(solution)/shard_map/ppermute | solution.py:225
  471.3 296.7 %collective-permute-start.25 = (f32[1024,1024]{1,0:T(8,128)}, f32[1024,1024]{1,0:T(8,128)}, u32[]{:S(2)}, u32[]{:S(2)}) collective-permute-start(f32[1024,1024]{1,0:T(8,128)} %get-tuple-element.146), channel_id=1, source_target_pairs={{0,2},{1,3},{2,0},{3,1},{4,6},{5,7},{6,4},{7,5},{8,10},{9,11},{10,... | collective-permute-start | bytes 12582920 | tf_op jit(solution)/shard_map/ppermute | solution.py:225
  586.1 207.1 %collective-permute-start.28 = (f32[1024,1024]{1,0:T(8,128)}, f32[1024,1024]{1,0:T(8,128)}, u32[]{:S(2)}, u32[]{:S(2)}) collective-permute-start(f32[1024,1024]{1,0:T(8,128)} %get-tuple-element.151), channel_id=1, source_target_pairs={{0,4},{1,5},{2,6},{3,7},{4,0},{5,1},{6,2},{7,3},{8,12},{9,13},{10,... | collective-permute-start | bytes 12582920 | tf_op jit(solution)/shard_map/ppermute | solution.py:225
  606.0 271.7 %collective-permute-start.31 = (f32[2,1024,1024]{2,1,0:T(8,128)}, f32[2,1024,1024]{2,1,0:T(8,128)}, u32[]{:S(2)}, u32[]{:S(2)}) collective-permute-start(f32[2,1024,1024]{2,1,0:T(8,128)} %get-tuple-element.156), channel_id=1, source_target_pairs={{0,1},{1,0},{2,3},{3,2},{4,5},{5,4},{6,7},{7,6},{8,9},{9,8},{10,11... | collective-permute-start | bytes 25165832 | tf_op jit(solution)/shard_map/ppermute | solution.py:225
  607.2 188.0 %collective-permute-start.29 = (f32[1024,1024]{1,0:T(8,128)}, f32[1024,1024]{1,0:T(8,128)}, u32[]{:S(2)}, u32[]{:S(2)}) collective-permute-start(f32[1024,1024]{1,0:T(8,128)} %get-tuple-element.152), channel_id=1, source_target_pairs={{0,2},{1,3},{2,0},{3,1},{4,6},{5,7},{6,4},{7,5},{8,10},{9,11},{10,... | collective-permute-start | bytes 12582920 | tf_op jit(solution)/shard_map/ppermute | solution.py:225
  767.7 113.1 %collective-permute-start.32 = (f32[2,1024,1024]{2,1,0:T(8,128)}, f32[2,1024,1024]{2,1,0:T(8,128)}, u32[]{:S(2)}, u32[]{:S(2)}) collective-permute-start(f32[2,1024,1024]{2,1,0:T(8,128)} %get-tuple-element.158), channel_id=1, source_target_pairs={{0,1},{1,0},{2,3},{3,2},{4,5},{5,4},{6,7},{7,6},{8,9},{9,8},{10,11... | collective-permute-start | bytes 25165832 | tf_op jit(solution)/shard_map/ppermute | solution.py:225
  768.0 109.7 %collective-permute-start.30 = (f32[1024,1024]{1,0:T(8,128)}, f32[1024,1024]{1,0:T(8,128)}, u32[]{:S(2)}, u32[]{:S(2)}) collective-permute-start(f32[1024,1024]{1,0:T(8,128)} %get-tuple-element.153), channel_id=1, source_target_pairs={{0,4},{1,5},{2,6},{3,7},{4,0},{5,1},{6,2},{7,3},{8,12},{9,13},{10,... | collective-permute-start | bytes 12582920 | tf_op jit(solution)/shard_map/ppermute | solution.py:225
  793.2 170.7 %collective-permute-start.51 = (f32[2,3,512,512]{3,2,0,1:T(8,128)}, f32[2,3,512,512]{3,2,0,1:T(8,128)}, u32[]{:S(2)}, u32[]{:S(2)}) collective-permute-start(f32[2,3,512,512]{3,2,0,1:T(8,128)} %copy.53), channel_id=1, source_target_pairs={{0,8},{8,0},{1,9},{9,1},{2,10},{10,2},{3,11},{11,3},{4,12},{12,4},... | collective-permute-start | bytes 18874376 | tf_op jit(solution)/shard_map/ppermute | solution.py:229
  795.2 182.0 %collective-permute-start.34 = (f32[2,1024,1024]{2,1,0:T(8,128)}, f32[2,1024,1024]{2,1,0:T(8,128)}, u32[]{:S(2)}, u32[]{:S(2)}) collective-permute-start(f32[2,1024,1024]{2,1,0:T(8,128)} %get-tuple-element.165), channel_id=1, source_target_pairs={{0,1},{1,0},{2,3},{3,2},{4,5},{5,4},{6,7},{7,6},{8,9},{9,8},{10,11... | collective-permute-start | bytes 25165832 | tf_op jit(solution)/shard_map/ppermute | solution.py:225
  877.7 99.8 %collective-permute-start.24 = (f32[2,1024,1024]{2,1,0:T(8,128)}, f32[2,1024,1024]{2,1,0:T(8,128)}, u32[]{:S(2)}, u32[]{:S(2)}) collective-permute-start(f32[2,1024,1024]{2,1,0:T(8,128)} %get-tuple-element.145), channel_id=1, source_target_pairs={{0,1},{1,0},{2,3},{3,2},{4,5},{5,4},{6,7},{7,6},{8,9},{9,8},{10,11... | collective-permute-start | bytes 25165832 | tf_op jit(solution)/shard_map/ppermute | solution.py:225
  877.7 138.2 %collective-permute-start.27 = (f32[2,1024,1024]{2,1,0:T(8,128)}, f32[2,1024,1024]{2,1,0:T(8,128)}, u32[]{:S(2)}, u32[]{:S(2)}) collective-permute-start(f32[2,1024,1024]{2,1,0:T(8,128)} %get-tuple-element.150), channel_id=1, source_target_pairs={{0,1},{1,0},{2,3},{3,2},{4,5},{5,4},{6,7},{7,6},{8,9},{9,8},{10,11... | collective-permute-start | bytes 25165832 | tf_op jit(solution)/shard_map/ppermute | solution.py:225
  880.7 157.0 %collective-permute-start.36 = (f32[2,1024,1024]{2,1,0:T(8,128)}, f32[2,1024,1024]{2,1,0:T(8,128)}, u32[]{:S(2)}, u32[]{:S(2)}) collective-permute-start(f32[2,1024,1024]{2,1,0:T(8,128)} %get-tuple-element.169), channel_id=1, source_target_pairs={{0,1},{1,0},{2,3},{3,2},{4,5},{5,4},{6,7},{7,6},{8,9},{9,8},{10,11... | collective-permute-start | bytes 25165832 | tf_op jit(solution)/shard_map/ppermute | solution.py:225
  963.9 124.1 %collective-permute-start.33 = (f32[2,1024,1024]{2,1,0:T(8,128)}, f32[2,1024,1024]{2,1,0:T(8,128)}, u32[]{:S(2)}, u32[]{:S(2)}) collective-permute-start(f32[2,1024,1024]{2,1,0:T(8,128)} %get-tuple-element.164), channel_id=1, source_target_pairs={{0,1},{1,0},{2,3},{3,2},{4,5},{5,4},{6,7},{7,6},{8,9},{9,8},{10,11... | collective-permute-start | bytes 25165832 | tf_op jit(solution)/shard_map/ppermute | solution.py:225
  977.3 134.0 %collective-permute-start.35 = (f32[2,1024,1024]{2,1,0:T(8,128)}, f32[2,1024,1024]{2,1,0:T(8,128)}, u32[]{:S(2)}, u32[]{:S(2)}) collective-permute-start(f32[2,1024,1024]{2,1,0:T(8,128)} %get-tuple-element.168), channel_id=1, source_target_pairs={{0,1},{1,0},{2,3},{3,2},{4,5},{5,4},{6,7},{7,6},{8,9},{9,8},{10,11... | collective-permute-start | bytes 25165832 | tf_op jit(solution)/shard_map/ppermute | solution.py:225
  977.5 110.3 %collective-permute-start.37 = (f32[1024,1024]{1,0:T(8,128)}, f32[1024,1024]{1,0:T(8,128)}, u32[]{:S(2)}, u32[]{:S(2)}) collective-permute-start(f32[1024,1024]{1,0:T(8,128)} %get-tuple-element.170), channel_id=1, source_target_pairs={{0,2},{1,3},{2,0},{3,1},{4,6},{5,7},{6,4},{7,5},{8,10},{9,11},{10,... | collective-permute-start | bytes 12582920 | tf_op jit(solution)/shard_map/ppermute | solution.py:225
  991.1 96.5 %all-to-all-start.1 = ((f32[8,4,2048]{2,1,0:T(4,128)}), f32[8,4,2048]{2,1,0:T(4,128)S(1)}, u32[]{:S(2)}, u32[]{:S(2)}) async-start(f32[8,4,2048]{2,1,0:T(4,128)} %bitcast.281), calls=%async_computation.1 | async-start | bytes 524288 | tf_op jit(solution)/shard_map/all_to_all | solution.py:388
  995.9 394.2 %all-reduce.2.cloned.1.call-start = ((), (), s32[]{:S(2)}) async-start(), calls=%async_computation.2 | async-start | bytes 262144 | tf_op jit(solution)/shard_map/psum | solution.py:399
  1016.0 95.3 %collective-permute-start.38 = (f32[1024,1024]{1,0:T(8,128)}, f32[1024,1024]{1,0:T(8,128)}, u32[]{:S(2)}, u32[]{:S(2)}) collective-permute-start(f32[1024,1024]{1,0:T(8,128)} %get-tuple-element.171), channel_id=1, source_target_pairs={{0,4},{1,5},{2,6},{3,7},{4,0},{5,1},{6,2},{7,3},{8,12},{9,13},{10,... | collective-permute-start | bytes 12582920 | tf_op jit(solution)/shard_map/ppermute | solution.py:225
  1037.7 137.0 %collective-permute-start.45 = (f32[1024,1024]{1,0:T(8,128)}, f32[1024,1024]{1,0:T(8,128)}, u32[]{:S(2)}, u32[]{:S(2)}) collective-permute-start(f32[1024,1024]{1,0:T(8,128)} %get-tuple-element.195), channel_id=1, source_target_pairs={{0,2},{1,3},{2,0},{3,1},{4,6},{5,7},{6,4},{7,5},{8,10},{9,11},{10,... | collective-permute-start | bytes 12582920 | tf_op jit(solution)/shard_map/ppermute | solution.py:225
  1087.8 113.3 %collective-permute-start.46 = (f32[1024,1024]{1,0:T(8,128)}, f32[1024,1024]{1,0:T(8,128)}, u32[]{:S(2)}, u32[]{:S(2)}) collective-permute-start(f32[1024,1024]{1,0:T(8,128)} %get-tuple-element.196), channel_id=1, source_target_pairs={{0,4},{1,5},{2,6},{3,7},{4,0},{5,1},{6,2},{7,3},{8,12},{9,13},{10,... | collective-permute-start | bytes 12582920 | tf_op jit(solution)/shard_map/ppermute | solution.py:225
  1088.0 143.3 %collective-permute-start.50 = (f32[2,3,512,512]{3,2,1,0:T(8,128)}, f32[2,3,512,512]{3,2,1,0:T(8,128)}, u32[]{:S(2)}, u32[]{:S(2)}) collective-permute-start(f32[2,3,512,512]{3,2,1,0:T(8,128)} %get-tuple-element.208), channel_id=1, source_target_pairs={{0,8},{8,0},{1,9},{9,1},{2,10},{10,2},{3,11},{11,3},{4,12},{12,4},... | collective-permute-start | bytes 18874376 | tf_op jit(solution)/shard_map/ppermute | solution.py:229
  1118.7 173.7 %collective-permute-start.39 = (f32[1024,1024]{1,0:T(8,128)}, f32[1024,1024]{1,0:T(8,128)}, u32[]{:S(2)}, u32[]{:S(2)}) collective-permute-start(f32[1024,1024]{1,0:T(8,128)} %fusion.14), channel_id=1, source_target_pairs={{0,4},{1,5},{2,6},{3,7},{4,0},{5,1},{6,2},{7,3},{8,12},{9,13},{10,... | collective-permute-start | bytes 12582920 | tf_op jit(solution)/shard_map/ppermute | solution.py:225
  1120.7 144.7 %collective-permute-start.40 = (f32[1024,1024]{1,0:T(8,128)}, f32[1024,1024]{1,0:T(8,128)}, u32[]{:S(2)}, u32[]{:S(2)}) collective-permute-start(f32[1024,1024]{1,0:T(8,128)} %fusion.11), channel_id=1, source_target_pairs={{0,2},{1,3},{2,0},{3,1},{4,6},{5,7},{6,4},{7,5},{8,10},{9,11},{10,... | collective-permute-start | bytes 12582920 | tf_op jit(solution)/shard_map/ppermute | solution.py:225
  1208.5 173.3 %collective-permute-start.47 = (f32[1024,1024]{1,0:T(8,128)}, f32[1024,1024]{1,0:T(8,128)}, u32[]{:S(2)}, u32[]{:S(2)}) collective-permute-start(f32[1024,1024]{1,0:T(8,128)} %bitcast_add_fusion.1), channel_id=1, source_target_pairs={{0,4},{1,5},{2,6},{3,7},{4,0},{5,1},{6,2},{7,3},{8,12},{9,13},{10,... | collective-permute-start | bytes 12582920 | tf_op jit(solution)/shard_map/ppermute | solution.py:225
  1210.6 145.1 %collective-permute-start.48 = (f32[1024,1024]{1,0:T(8,128)}, f32[1024,1024]{1,0:T(8,128)}, u32[]{:S(2)}, u32[]{:S(2)}) collective-permute-start(f32[1024,1024]{1,0:T(8,128)} %bitcast_add_fusion), channel_id=1, source_target_pairs={{0,2},{1,3},{2,0},{3,1},{4,6},{5,7},{6,4},{7,5},{8,10},{9,11},{10,... | collective-permute-start | bytes 12582920 | tf_op jit(solution)/shard_map/ppermute | solution.py:225
  (72 other events, 2336.4 us)
Sparse Core Ops, SparseCore 0:
  1220.4 69.1 all-reduce.1
